TPU v7x, 32 devices: a whole 2x2x4 slice. The times are simulated.
32 devices in a mesh: dp: 2 (over x), sp: 16 (over z, y, core).
Axes of the slice: x: 2, y: 2, z: 4, core: 2. Of those that a mesh axis runs over, the one named last changes fastest.
Arguments:
- x: bfloat16 [4, 16384, 2048], P('dp', 'sp'), parts along dimension 0
- w_q: bfloat16 [2048, 8, 256], replicated
- w_k: bfloat16 [2048, 8, 256], replicated
- w_v: bfloat16 [2048, 8, 256], replicated
- w_o: bfloat16 [8, 256, 2048], replicated
Outputs:
- output: bfloat16 [4, 16384, 2048], P('dp', 'sp'), parts along dimension 0
There are 2 independent parts. A program takes and returns all parts, laid end to end along the dimension named above; an argument that names none is the same for every part.
All inputs are finite; a program needn't handle non-finite values.
Results may differ from a plain program's by a relative error of at most 0.00355872.
Values are sent between devices in bfloat16 or wider.
A program may use at most 1 GiB of HBM per device.

v0:
```python
import jax
import jax.numpy as jnp
from jax import lax
from jax.sharding import PartitionSpec as P, NamedSharding

SEGMENT = 2048
BRANCHES = 4
QUERY_BLOCK = 128


def pick_rows(values, dilation):
    if dilation == 1:
        return values
    n_seqs, n_rows, n_heads, head_dim = values.shape
    split_view = values.reshape(n_seqs, n_rows // dilation, dilation, n_heads // dilation, dilation, head_dim)
    picked = jnp.stack([split_view[:, :, phase_idx, :, phase_idx, :] for phase_idx in range(dilation)], axis=3)
    return picked.reshape(n_seqs, n_rows // dilation, n_heads, head_dim)


def spread_rows(o_sp, lse_sp, dilation):
    if dilation == 1:
        return o_sp, lse_sp
    n_seqs, n_rows, n_heads, head_dim = o_sp.shape
    keep_mask = jnp.eye(dilation, dtype=jnp.float32).reshape(1, 1, dilation, 1, dilation)
    o_full = o_sp.reshape(n_seqs, n_rows, 1, n_heads // dilation, dilation, head_dim) * keep_mask[..., None]
    lse_full = jnp.where(keep_mask > 0, lse_sp.reshape(n_seqs, n_rows, 1, n_heads // dilation, dilation), -jnp.inf)
    return o_full.reshape(n_seqs, n_rows * dilation, n_heads, head_dim), lse_full.reshape(n_seqs, n_rows * dilation, n_heads)


def attend(q_sp, k_sp, v_sp):
    n_groups, n_query, n_heads, head_dim = q_sp.shape
    blk_len = min(QUERY_BLOCK, n_query)
    n_blocks = n_query // blk_len
    q_blocks = q_sp.reshape(n_groups * n_blocks, blk_len, n_heads, head_dim)
    owners = jnp.arange(n_groups * n_blocks, dtype=jnp.int32) // n_blocks
    logit_scale = head_dim ** -0.5

    def one_block(block_item):
        q_tile, owner_idx = block_item
        k_seg = lax.dynamic_index_in_dim(k_sp, owner_idx, 0, keepdims=False)
        v_seg = lax.dynamic_index_in_dim(v_sp, owner_idx, 0, keepdims=False)
        scores = jnp.einsum('qhd,khd->hqk', q_tile, k_seg, preferred_element_type=jnp.float32) * logit_scale
        log_sum = jax.nn.logsumexp(scores, axis=-1)
        p_tile = jnp.exp(scores - log_sum[:, :, None]).astype(jnp.bfloat16)
        o_tile = jnp.einsum('hqk,khd->qhd', p_tile, v_seg, preferred_element_type=jnp.float32)
        return o_tile, log_sum.T

    o_all, lse_all = lax.map(one_block, (q_blocks, owners))
    return o_all.reshape(n_groups, n_query, n_heads, head_dim), lse_all.reshape(n_groups, n_query, n_heads)


def gather_group(k_part, v_part, group_size, n_dev):
    step_bit = 1
    while step_bit < group_size:
        perm_pairs = [(source, source ^ step_bit) for source in range(n_dev)]
        k_peer, v_peer = lax.ppermute((k_part, v_part), 'sp', perm_pairs)
        k_part = jnp.concatenate([k_part, k_peer], axis=1)
        v_part = jnp.concatenate([v_part, v_peer], axis=1)
        step_bit = step_bit * 2
    return k_part, v_part


def solution(mesh):
    n_dev = mesh.shape['sp']

    def local_step(x_loc, w_q, w_k, w_v, w_o):
        n_seqs, n_tok, model_dim = x_loc.shape
        n_heads, head_dim = w_q.shape[1], w_q.shape[2]
        x_flat = x_loc.reshape(n_seqs * n_tok, model_dim)

        def project(weight):
            product = jnp.dot(x_flat, weight.reshape(model_dim, n_heads * head_dim), preferred_element_type=jnp.float32)
            return product.astype(jnp.bfloat16).reshape(n_seqs, n_tok, n_heads, head_dim)

        q_all = project(w_q)
        k_all = project(w_k)
        v_all = project(w_v)
        for branch in range(BRANCHES):
            dilation = 2 ** branch
            seg_len = SEGMENT * dilation
            q_sp = pick_rows(q_all, dilation)
            k_sp = pick_rows(k_all, dilation)
            v_sp = pick_rows(v_all, dilation)
            if seg_len <= n_tok:
                seg_shape = (n_seqs * (n_tok // seg_len), SEGMENT, n_heads, head_dim)
                o_sp, lse_sp = attend(q_sp.reshape(seg_shape), k_sp.reshape(seg_shape), v_sp.reshape(seg_shape))
            else:
                k_grp, v_grp = gather_group(k_sp, v_sp, seg_len // n_tok, n_dev)
                o_sp, lse_sp = attend(q_sp, k_grp, v_grp)
            o_full, lse_full = spread_rows(o_sp.reshape(n_seqs, n_tok // dilation, n_heads, head_dim), lse_sp.reshape(n_seqs, n_tok // dilation, n_heads), dilation)
            if branch == 0:
                lse_max = lse_full
                numerator = o_full
                denominator = jnp.ones_like(lse_full)
            else:
                new_max = jnp.maximum(lse_max, lse_full)
                old_scale = jnp.exp(lse_max - new_max)
                new_scale = jnp.exp(lse_full - new_max)
                numerator = numerator * old_scale[..., None] + o_full * new_scale[..., None]
                denominator = denominator * old_scale + new_scale
                lse_max = new_max
        o_mix = (numerator / denominator[..., None]).astype(jnp.bfloat16)
        y_flat = jnp.dot(o_mix.reshape(n_seqs * n_tok, n_heads * head_dim), w_o.reshape(n_heads * head_dim, model_dim), preferred_element_type=jnp.float32)
        return y_flat.astype(jnp.bfloat16).reshape(n_seqs, n_tok, model_dim)

    return jax.shard_map(local_step, mesh=mesh, in_specs=(P('dp', 'sp', None), P(), P(), P(), P()), out_specs=P('dp', 'sp', None), check_vma=False)
```

profile of v0, /device:TPU:0, one launch (start us, length us, event | category | flops | bytes accessed | tf_op | source)
XLA Modules:
  0.0 1678.9 jit_solution(16222800071609351294)
XLA Ops:
  0.0 10.5 copy.270
  10.5 24.0 %convolution_convert_fusion.1 = bf16[2048,2048]{1,0:T(8,128)(2,1)} fusion(bf16[2048,2048]{1,0:T(8,128)(2,1)} %bitcast.453, bf16[2048,2048]{1,0:T(8,128)(2,1)} %bitcast.433), kind=kOutput, calls=%fused_computation.117 | convolution fusion | flops 17184063488 | bytes 25165824 | tf_op jit(solution)/shard_map/dot_general | solution.py:72
  34.5 14.5 reshape_reshape.48
  57.8 10.5 copy.266
  68.2 23.8 %convolution_convert_fusion.3 = bf16[2048,2048]{1,0:T(8,128)(2,1)} fusion(bf16[2048,2048]{1,0:T(8,128)(2,1)} %bitcast.454, bf16[2048,2048]{1,0:T(8,128)(2,1)} %bitcast.434), kind=kOutput, calls=%fused_computation.119 | convolution fusion | flops 17184063488 | bytes 25165824 | tf_op jit(solution)/shard_map/dot_general | solution.py:72
  92.0 14.5 reshape_reshape.45
  149.2 14.4 reshape_reshape.41
  163.6 9.1 fusion.105
  182.7 14.4 reshape_reshape.44
  197.2 10.6 copy.268
  207.8 23.7 %convolution_convert_fusion.2 = bf16[2048,2048]{1,0:T(8,128)(2,1)} fusion(bf16[2048,2048]{1,0:T(8,128)(2,1)} %bitcast.455, bf16[2048,2048]{1,0:T(8,128)(2,1)} %bitcast.435), kind=kOutput, calls=%fused_computation.118 | convolution fusion | flops 17184063488 | bytes 25165824 | tf_op jit(solution)/shard_map/dot_general | solution.py:72
  231.5 8.9 fusion.103
  240.4 14.4 reshape_reshape.42
  254.8 9.9 fusion.104
  264.7 14.5 reshape_reshape.46
  310.5 10.5 copy.267
  321.0 12.3 copy.132
  349.8 10.5 copy.271
  360.3 8.5 copy.134
  370.8 108.9 %collective-permute-done.13 = bf16[2,256,8,256]{1,3,2,0:T(8,128)(2,1)S(1)} collective-permute-done((bf16[2,256,8,256]{1,3,2,0:T(8,128)(2,1)}, bf16[2,256,8,256]{1,3,2,0:T(8,128)(2,1)S(1)}, u32[]{:S(2)}, u32[]{:S(2)}) %collective-permute-start.13) | collective-permute-done | bytes 2097184 | tf_op jit(solution)/shard_map/ppermute | solution.py:56
  504.8 10.4 copy.269
  545.3 8.0 pad_maximum_fusion.6
  553.3 7.5 pad_maximum_fusion.7
  560.7 7.0 pad_maximum_fusion.9
  567.7 11.0 collective-permute-done.7
  580.4 6.8 pad_maximum_fusion.8
  592.0 81.6 %collective-permute-done.14 = bf16[2,512,8,256]{1,3,2,0:T(8,128)(2,1)} collective-permute-done((bf16[2,512,8,256]{1,3,2,0:T(8,128)(2,1)}, bf16[2,512,8,256]{1,3,2,0:T(8,128)(2,1)}, u32[]{:S(2)}, u32[]{:S(2)}) %collective-permute-start.14) | collective-permute-done | bytes 4194336 | tf_op jit(solution)/shard_map/ppermute | solution.py:56
  679.9 7.5 pad_maximum_fusion.11
  687.4 7.0 pad_maximum_fusion.10
  694.9 14.1 pad_maximum_fusion
  711.5 10.3 pad_maximum_fusion.1
  721.8 296.0 %while.48 = (s32[]{:T(128)}, f32[16,128,8,256]{3,2,1,0:T(8,128)}, f32[16,128,8]{1,2,0:T(8,128)}, s32[16]{0:T(128)S(1)}, bf16[2,2048,8,256]{1,3,2,0:T(8,128)(2,1)...) while((s32[]{:T(128)}, f32[16,128,8,256]{3,2,1,0:T(8,128)}, ...), condition=%wide.region_3.4_spmd, body=%wide.region_0.3_spmd.sunk | while | flops 2164269056 | bytes 48809120 | solution.py:48
  1018.2 13.8 pad_maximum_fusion.2
  1032.0 13.5 pad_maximum_fusion.3
  1045.5 137.6 %while.49 = (s32[]{:T(128)}, f32[8,128,8,256]{3,1,0,2:T(8,128)}, f32[8,128,8]{1,0,2:T(8,128)S(1)}, s32[8]{0:T(128)S(1)}, bf16[2,2048,8,256]{1,3,2,0:T(8,128)(2,1...) while((s32[]{:T(128)}, f32[8,128,8,256]{3,1,0,2:T(8,128)}, ...), condition=%wide.region_7.8_spmd, body=%wide.region_4.7_spmd.sunk | while | flops 2164269056 | bytes 47768732 | solution.py:48
  1048.1 6.5 multiply_reduce_fusion.9
  1065.2 6.5 multiply_reduce_fusion.9
  1082.4 6.5 multiply_reduce_fusion.9
  1099.6 6.5 multiply_reduce_fusion.9
  1134.0 6.5 multiply_reduce_fusion.9
  1151.2 6.5 multiply_reduce_fusion.9
  1190.5 14.4 copy.152
  1205.0 6.7 mul.215
  1211.7 20.5 %mul.216 = f32[2,1024,8,256]{3,2,1,0:T(8,128)} reshape(f32[2,512,2,4,2,256]{5,4,3,2,1,0:T(2,128)} %mul.215) | data formatting | bytes 33554432 | tf_op jit(solution)/shard_map/mul | solution.py:25
  1232.2 13.7 pad_maximum_fusion.5
  1245.9 13.1 pad_maximum_fusion.4
  1259.0 94.1 %while.50 = (s32[]{:T(128)}, f32[4,128,8,256]{3,1,0,2:T(8,128)}, f32[4,128,8]{1,0,2:T(4,128)S(1)}, s32[4]{0:T(128)S(1)}, bf16[2,2048,8,256]{1,3,2,0:T(8,128)(2,1...) while((s32[]{:T(128)}, f32[4,128,8,256]{3,1,0,2:T(8,128)}, ...), condition=%wide.region_11.12_spmd, body=%wide.region_8.11_spmd.sunk | while | flops 2164269056 | bytes 81323192 | solution.py:48
  1261.2 6.5 multiply_reduce_fusion.10
  1272.7 8.2 fusion.146
  1284.6 6.5 multiply_reduce_fusion.10
  1296.2 8.2 fusion.146
  1308.0 6.5 multiply_reduce_fusion.10
  1319.6 8.2 fusion.146
  1331.5 6.5 multiply_reduce_fusion.10
  1343.0 8.2 fusion.146
  1366.4 19.4 %mul.227 = f32[2,1024,8,256]{3,2,1,0:T(8,128)} reshape(f32[2,256,4,2,4,256]{5,4,3,2,1,0:T(4,128)} %mul.226) | data formatting | bytes 33554432 | tf_op jit(solution)/shard_map/mul | solution.py:25
  1385.8 7.4 constant_dynamic-update-slice_fusion.9
  1393.1 166.2 %collective-permute-done.15 = bf16[2,1024,8,256]{1,3,2,0:T(8,128)(2,1)} collective-permute-done((bf16[2,1024,8,256]{1,3,2,0:T(8,128)(2,1)}, bf16[2,1024,8,256]{1,3,2,0:T(8,128)(2,1)}, u32[]{:S(2)}, u32[]{:S(2)}) %collective-permute-start.15) | collective-permute-done | bytes 8388640 | tf_op jit(solution)/shard_map/ppermute | solution.py:56
  1559.3 8.1 constant_dynamic-update-slice_fusion.4
  1567.4 34.7 %while.51 = (s32[]{:T(128)}, f32[2,128,8,256]{3,2,1,0:T(8,128)}, f32[2,128,8]{1,2,0:T(8,128)S(1)}, s32[2]{0:T(128)S(1)}, bf16[2,2048,8,256]{1,3,2,0:T(8,128)(2,1...) while((s32[]{:T(128)}, f32[2,128,8,256]{3,2,1,0:T(8,128)}, ...), condition=%wide.region_15.16_spmd, body=%wide.region_12.15_spmd.sunk | while | flops 2164269056 | bytes 47760540 | solution.py:48
  1609.5 8.8 mul.236
  1618.4 26.5 %fusion.80 = bf16[2,1024,8,256]{3,2,1,0:T(8,128)(2,1)} fusion(f32[2,1024,8,256]{3,2,1,0:T(8,128)} %bitcast.412, f32[2,1024,8,256]{3,2,1,0:T(8,128)} %mul.227, f32[2,1024,8,256]{3,2,1,0:T(8,128)} %mul.216, f32[2,1024,8]{2,1,0:T(8,128)S(1)} %copy-done.16, f32[2,1024,8]{2,1,0:T(8,128)S(1)} %copy-done.15, f32[1024,8]{1,0:T(8,128)S(1)} %copy-done.19, ...), kind=kLoop, calls=%fused_computation.109 | loop fusion | flops 58720256 | bytes 76054528 | tf_op jit(solution)/shard_map/convert_element_type | solution.py:102
  1644.9 10.4 copy.272
  1655.3 23.5 %convolution_convert_fusion = bf16[2048,2048]{1,0:T(8,128)(2,1)} fusion(bf16[2048,2048]{1,0:T(8,128)(2,1)} %bitcast.432, bf16[2048,2048]{1,0:T(8,128)(2,1)} %bitcast.456), kind=kOutput, calls=%fused_computation.116 | convolution fusion | flops 17184063488 | bytes 25165824 | tf_op jit(solution)/shard_map/dot_general | solution.py:103
  (525 shorter events, 619.9 us)
Async XLA Ops:
  57.3 238.8 %collective-permute-start.9 = (bf16[2,256,8,256]{3,1,2,0:T(8,128)(2,1)}, bf16[2,256,8,256]{3,1,2,0:T(8,128)(2,1)}, u32[]{:S(2)}, u32[]{:S(2)}) collective-permute-start(bf16[2,256,8,256]{3,1,2,0:T(8,128)(2,1)} %bitcast.63), channel_id=1, source_target_pairs={{0,1},{1,0},{2,3},{3,2},{4,5},{5,4},{6,7},{7,6},{8,9},{9,8},{10,11... | collective-permute-start | bytes 6291464 | tf_op jit(solution)/shard_map/ppermute | solution.py:56
  117.7 462.7 %copy-start.1 = (bf16[2,256,8,256]{1,3,2,0:T(8,128)(2,1)}, bf16[2,256,8,256]{1,3,2,0:T(8,128)(2,1)S(1)}, u32[]{:S(2)}) copy-start(bf16[2,256,8,256]{1,3,2,0:T(8,128)(2,1)S(1)} %copy.162) | copy-start | bytes 6291460
  117.7 222.0 %collective-permute-start.6 = (bf16[2,256,8,256]{1,3,2,0:T(8,128)(2,1)S(1)}, bf16[2,256,8,256]{1,3,2,0:T(8,128)(2,1)}, u32[]{:S(2)}, u32[]{:S(2)}) collective-permute-start(bf16[2,256,8,256]{1,3,2,0:T(8,128)(2,1)S(1)} %copy.162), channel_id=1, source_target_pairs={{0,1},{1,0},{2,3},{3,2},{4,5},{5,4},{6,7},{7,6},{8,9},{9,8},{10,11... | collective-permute-start | bytes 6291464 | tf_op jit(solution)/shard_map/ppermute | solution.py:56
  128.4 164.1 %collective-permute-start.16 = (bf16[2,128,8,256]{3,1,2,0:T(8,128)(2,1)}, bf16[2,128,8,256]{3,1,2,0:T(8,128)(2,1)}, u32[]{:S(2)}, u32[]{:S(2)}) collective-permute-start(bf16[2,128,8,256]{3,1,2,0:T(8,128)(2,1)} %bitcast.94), channel_id=1, source_target_pairs={{0,1},{1,0},{2,3},{3,2},{4,5},{5,4},{6,7},{7,6},{8,9},{9,8},{10,11... | collective-permute-start | bytes 3145736 | tf_op jit(solution)/shard_map/ppermute | solution.py:56
  148.7 154.5 %collective-permute-start.12 = (bf16[2,128,8,256]{1,3,2,0:T(8,128)(2,1)}, bf16[2,128,8,256]{1,3,2,0:T(8,128)(2,1)}, u32[]{:S(2)}, u32[]{:S(2)}) collective-permute-start(bf16[2,128,8,256]{1,3,2,0:T(8,128)(2,1)} %bitcast.420), channel_id=1, source_target_pairs={{0,1},{1,0},{2,3},{3,2},{4,5},{5,4},{6,7},{7,6},{8,9},{9,8},{10,11... | collective-permute-start | bytes 3145736 | tf_op jit(solution)/shard_map/ppermute | solution.py:56
  182.7 303.1 %collective-permute-start.2 = (bf16[2,512,8,256]{1,3,2,0:T(8,128)(2,1)}, bf16[2,512,8,256]{1,3,2,0:T(8,128)(2,1)}, u32[]{:S(2)}, u32[]{:S(2)}) collective-permute-start(bf16[2,512,8,256]{1,3,2,0:T(8,128)(2,1)} %copy.141), channel_id=1, source_target_pairs={{0,1},{1,0},{2,3},{3,2},{4,5},{5,4},{6,7},{7,6},{8,9},{9,8},{10,11... | collective-permute-start | bytes 12582920 | tf_op jit(solution)/shard_map/ppermute | solution.py:56
  197.2 34.4 %slice-start = ((s8[8388608]{0:T(1024)(128)(4,1)}), s8[4194304]{0:T(1024)(128)(4,1)S(1)}, s32[]{:S(2)}) async-start(s8[8388608]{0:T(1024)(128)(4,1)} %bitcast.414), calls=%async_computation | async-start | bytes 8388608
  207.8 23.7 %slice-start.1 = ((s8[8388608]{0:T(1024)(128)(4,1)}), s8[4194304]{0:T(1024)(128)(4,1)S(1)}, s32[]{:S(2)}) async-start(s8[8388608]{0:T(1024)(128)(4,1)} %bitcast.414), calls=%async_computation.1 | async-start | bytes 8388608
  279.2 6.5 copy-start.3
  292.5 198.8 %collective-permute-start.4 = (bf16[2,512,8,256]{3,1,2,0:T(8,128)(2,1)}, bf16[2,512,8,256]{3,1,2,0:T(8,128)(2,1)}, u32[]{:S(2)}, u32[]{:S(2)}) collective-permute-start(bf16[2,512,8,256]{3,1,2,0:T(8,128)(2,1)} %bitcast.47), channel_id=1, source_target_pairs={{0,1},{1,0},{2,3},{3,2},{4,5},{5,4},{6,7},{7,6},{8,9},{9,8},{10,11... | collective-permute-start | bytes 12582920 | tf_op jit(solution)/shard_map/ppermute | solution.py:56
  296.1 10.2 copy-start.10
  296.1 53.2 %collective-permute-start.17 = (bf16[2,256,8,256]{3,1,2,0:T(8,128)(2,1)}, bf16[2,256,8,256]{3,1,2,0:T(8,128)(2,1)}, u32[]{:S(2)}, u32[]{:S(2)}) collective-permute-start(bf16[2,256,8,256]{3,1,2,0:T(8,128)(2,1)} %pad_maximum_fusion.23), channel_id=1, source_target_pairs={{0,2},{1,3},{2,0},{3,1},{4,6},{5,7},{6,4},{7,5},{8,10},{9,11},{10,... | collective-permute-start | bytes 6291464 | tf_op jit(solution)/shard_map/ppermute | solution.py:56
  303.2 5.1 copy-start.9
  303.2 193.3 %collective-permute-start.10 = (bf16[2,512,8,256]{3,1,2,0:T(8,128)(2,1)}, bf16[2,512,8,256]{3,1,2,0:T(8,128)(2,1)}, u32[]{:S(2)}, u32[]{:S(2)}) collective-permute-start(bf16[2,512,8,256]{3,1,2,0:T(8,128)(2,1)} %pad_maximum_fusion.16), channel_id=1, source_target_pairs={{0,2},{1,3},{2,0},{3,1},{4,6},{5,7},{6,4},{7,5},{8,10},{9,11},{10,... | collective-permute-start | bytes 12582920 | tf_op jit(solution)/shard_map/ppermute | solution.py:56
  333.2 8.3 copy-start.11
  333.2 8.3 copy-start.12
  339.7 140.1 %collective-permute-start.13 = (bf16[2,256,8,256]{1,3,2,0:T(8,128)(2,1)}, bf16[2,256,8,256]{1,3,2,0:T(8,128)(2,1)S(1)}, u32[]{:S(2)}, u32[]{:S(2)}) collective-permute-start(bf16[2,256,8,256]{1,3,2,0:T(8,128)(2,1)} %pad_maximum_fusion.22), channel_id=1, source_target_pairs={{0,2},{1,3},{2,0},{3,1},{4,6},{5,7},{6,4},{7,5},{8,10},{9,11},{10,... | collective-permute-start | bytes 6291464 | tf_op jit(solution)/shard_map/ppermute | solution.py:56
  349.3 345.0 %collective-permute-start = (bf16[2,1024,8,256]{1,3,2,0:T(8,128)(2,1)}, bf16[2,1024,8,256]{1,3,2,0:T(8,128)(2,1)}, u32[]{:S(2)}, u32[]{:S(2)}) collective-permute-start(bf16[2,1024,8,256]{1,3,2,0:T(8,128)(2,1)} %copy.132), channel_id=1, source_target_pairs={{0,1},{1,0},{2,3},{3,2},{4,5},{5,4},{6,7},{7,6},{8,9},{9,8},{10,11... | collective-permute-start | bytes 25165832 | tf_op jit(solution)/shard_map/ppermute | solution.py:56
  479.7 13.1 copy-start.4
  479.7 229.2 %collective-permute-start.1 = (bf16[2,1024,8,256]{3,1,2,0:T(8,128)(2,1)}, bf16[2,1024,8,256]{3,1,2,0:T(8,128)(2,1)}, u32[]{:S(2)}, u32[]{:S(2)}) collective-permute-start(bf16[2,1024,8,256]{3,1,2,0:T(8,128)(2,1)} %copy.134), channel_id=1, source_target_pairs={{0,1},{1,0},{2,3},{3,2},{4,5},{5,4},{6,7},{7,6},{8,9},{9,8},{10,11... | collective-permute-start | bytes 25165832 | tf_op jit(solution)/shard_map/ppermute | solution.py:56
  481.8 11.1 copy-start.7
  485.9 92.8 %collective-permute-start.7 = (bf16[2,512,8,256]{1,3,2,0:T(8,128)(2,1)}, bf16[2,512,8,256]{1,3,2,0:T(8,128)(2,1)}, u32[]{:S(2)}, u32[]{:S(2)}) collective-permute-start(bf16[2,512,8,256]{1,3,2,0:T(8,128)(2,1)} %pad_maximum_fusion.15), channel_id=1, source_target_pairs={{0,2},{1,3},{2,0},{3,1},{4,6},{5,7},{6,4},{7,5},{8,10},{9,11},{10,... | collective-permute-start | bytes 12582920 | tf_op jit(solution)/shard_map/ppermute | solution.py:56
  491.3 95.9 %collective-permute-start.18 = (bf16[2,512,8,256]{3,1,2,0:T(8,128)(2,1)}, bf16[2,512,8,256]{3,1,2,0:T(8,128)(2,1)}, u32[]{:S(2)}, u32[]{:S(2)}) collective-permute-start(bf16[2,512,8,256]{3,1,2,0:T(8,128)(2,1)} %pad_maximum_fusion.18), channel_id=1, source_target_pairs={{0,4},{1,5},{2,6},{3,7},{4,0},{5,1},{6,2},{7,3},{8,12},{9,13},{10,... | collective-permute-start | bytes 12582920 | tf_op jit(solution)/shard_map/ppermute | solution.py:56
  496.5 177.1 %collective-permute-start.14 = (bf16[2,512,8,256]{1,3,2,0:T(8,128)(2,1)}, bf16[2,512,8,256]{1,3,2,0:T(8,128)(2,1)}, u32[]{:S(2)}, u32[]{:S(2)}) collective-permute-start(bf16[2,512,8,256]{1,3,2,0:T(8,128)(2,1)} %pad_maximum_fusion.17), channel_id=1, source_target_pairs={{0,4},{1,5},{2,6},{3,7},{4,0},{5,1},{6,2},{7,3},{8,12},{9,13},{10,... | collective-permute-start | bytes 12582920 | tf_op jit(solution)/shard_map/ppermute | solution.py:56
  529.2 14.6 copy-start.5
  578.7 439.2 %collective-permute-start.3 = (bf16[2,1024,8,256]{1,3,2,0:T(8,128)(2,1)}, bf16[2,1024,8,256]{1,3,2,0:T(8,128)(2,1)}, u32[]{:S(2)}, u32[]{:S(2)}) collective-permute-start(bf16[2,1024,8,256]{1,3,2,0:T(8,128)(2,1)} %pad_maximum_fusion.6), channel_id=1, source_target_pairs={{0,2},{1,3},{2,0},{3,1},{4,6},{5,7},{6,4},{7,5},{8,10},{9,11},{10,... | collective-permute-start | bytes 25165832 | tf_op jit(solution)/shard_map/ppermute | solution.py:56
  587.2 444.8 %collective-permute-start.5 = (bf16[2,1024,8,256]{3,1,2,0:T(8,128)(2,1)}, bf16[2,1024,8,256]{3,1,2,0:T(8,128)(2,1)}, u32[]{:S(2)}, u32[]{:S(2)}) collective-permute-start(bf16[2,1024,8,256]{3,1,2,0:T(8,128)(2,1)} %pad_maximum_fusion.7), channel_id=1, source_target_pairs={{0,2},{1,3},{2,0},{3,1},{4,6},{5,7},{6,4},{7,5},{8,10},{9,11},{10,... | collective-permute-start | bytes 25165832 | tf_op jit(solution)/shard_map/ppermute | solution.py:56
  673.7 558.5 %collective-permute-start.11 = (bf16[2,1024,8,256]{3,1,2,0:T(8,128)(2,1)}, bf16[2,1024,8,256]{3,1,2,0:T(8,128)(2,1)}, u32[]{:S(2)}, u32[]{:S(2)}) collective-permute-start(bf16[2,1024,8,256]{3,1,2,0:T(8,128)(2,1)} %pad_maximum_fusion.9), channel_id=1, source_target_pairs={{0,4},{1,5},{2,6},{3,7},{4,0},{5,1},{6,2},{7,3},{8,12},{9,13},{10,... | collective-permute-start | bytes 25165832 | tf_op jit(solution)/shard_map/ppermute | solution.py:56
  679.9 7.5 copy-start.6
  679.9 7.5 copy-start.8
  687.3 24.2 %slice-start.2 = ((s8[8388608]{0:T(1024)(128)(4,1)}), s8[4194304]{0:T(1024)(128)(4,1)S(1)}, s32[]{:S(2)}) async-start(s8[8388608]{0:T(1024)(128)(4,1)} %bitcast.418), calls=%async_computation.2 | async-start | bytes 8388608
  694.3 17.2 %slice-start.3 = ((s8[8388608]{0:T(1024)(128)(4,1)}), s8[4194304]{0:T(1024)(128)(4,1)S(1)}, s32[]{:S(2)}) async-start(s8[8388608]{0:T(1024)(128)(4,1)} %bitcast.418), calls=%async_computation.3 | async-start | bytes 8388608
  694.4 551.5 %collective-permute-start.8 = (bf16[2,1024,8,256]{1,3,2,0:T(8,128)(2,1)}, bf16[2,1024,8,256]{1,3,2,0:T(8,128)(2,1)}, u32[]{:S(2)}, u32[]{:S(2)}) collective-permute-start(bf16[2,1024,8,256]{1,3,2,0:T(8,128)(2,1)} %pad_maximum_fusion.8), channel_id=1, source_target_pairs={{0,4},{1,5},{2,6},{3,7},{4,0},{5,1},{6,2},{7,3},{8,12},{9,13},{10,... | collective-permute-start | bytes 25165832 | tf_op jit(solution)/shard_map/ppermute | solution.py:56
  708.9 676.8 %collective-permute-start.19 = (bf16[2,1024,8,256]{3,1,2,0:T(8,128)(2,1)}, bf16[2,1024,8,256]{3,1,2,0:T(8,128)(2,1)}, u32[]{:S(2)}, u32[]{:S(2)}) collective-permute-start(bf16[2,1024,8,256]{3,1,2,0:T(8,128)(2,1)} %pad_maximum_fusion.11), channel_id=1, source_target_pairs={{0,8},{1,9},{2,10},{3,11},{4,12},{5,13},{6,14},{7,15},{8,0},{9,1},... | collective-permute-start | bytes 25165832 | tf_op jit(solution)/shard_map/ppermute | solution.py:56
  1017.9 541.5 %collective-permute-start.15 = (bf16[2,1024,8,256]{1,3,2,0:T(8,128)(2,1)}, bf16[2,1024,8,256]{1,3,2,0:T(8,128)(2,1)}, u32[]{:S(2)}, u32[]{:S(2)}) collective-permute-start(bf16[2,1024,8,256]{1,3,2,0:T(8,128)(2,1)} %pad_maximum_fusion.10), channel_id=1, source_target_pairs={{0,8},{1,9},{2,10},{3,11},{4,12},{5,13},{6,14},{7,15},{8,0},{9,1},... | collective-permute-start | bytes 25165832 | tf_op jit(solution)/shard_map/ppermute | solution.py:56
  1032.0 13.5 copy-start.25
  1032.0 13.5 copy-start.29
  1232.2 13.7 copy-start.2
  1245.9 13.1 copy-start.26
  1245.9 13.1 copy-start.28
  1267.7 3.3 copy-start
  1291.2 3.3 copy-start
  1314.6 3.3 copy-start
  1338.0 3.3 copy-start
  1393.1 174.2 %copy-start.27 = (f32[2,128,8]{1,2,0:T(8,128)S(1)}, f32[2,128,8]{1,2,0:T(8,128)}, u32[]{:S(2)}) copy-start(f32[2,128,8]{1,2,0:T(8,128)} %custom-call.12) | copy-start | bytes 24580
  1567.4 35.6 %copy-start.20 = (f32[2,1024,8]{1,2,0:T(8,128)S(1)}, f32[2,1024,8]{1,2,0:T(8,128)}, u32[]{:S(2)}) copy-start(f32[2,1024,8]{1,2,0:T(8,128)} %broadcast_in_dim.158) | copy-start | bytes 196612
  1567.4 35.6 %copy-start.21 = (f32[16,128,8]{1,2,0:T(8,128)S(1)}, f32[16,128,8]{1,2,0:T(8,128)}, u32[]{:S(2)}) copy-start(f32[16,128,8]{1,2,0:T(8,128)} %get-tuple-element.158) | copy-start | bytes 196612
  1567.4 35.6 %copy-start.22 = (pred[1024,8]{0,1:T(8,128)(4,1)S(1)}, pred[1024,8]{0,1:T(8,128)(4,1)}, u32[]{:S(2)}) copy-start(pred[1024,8]{0,1:T(8,128)(4,1)} %broadcast_in_dim.152) | copy-start | bytes 24580
  1567.4 35.6 %copy-start.23 = (pred[1024,8]{0,1:T(8,128)(4,1)S(1)}, pred[1024,8]{0,1:T(8,128)(4,1)}, u32[]{:S(2)}) copy-start(pred[1024,8]{0,1:T(8,128)(4,1)} %broadcast_in_dim.161) | copy-start | bytes 24580
  1567.4 35.6 %copy-start.24 = (pred[1024,8]{0,1:T(8,128)(4,1)S(1)}, pred[1024,8]{0,1:T(8,128)(4,1)}, u32[]{:S(2)}) copy-start(pred[1024,8]{0,1:T(8,128)(4,1)} %broadcast_in_dim.169) | copy-start | bytes 24580
  1609.4 8.9 copy-start.13
  1609.4 8.9 copy-start.14
  1609.4 8.9 copy-start.15
  1609.4 8.9 copy-start.16
  1609.5 8.9 copy-start.17
  1609.5 8.9 copy-start.18
  1609.5 8.9 copy-start.19
where the time goes:
time: 1690 us; the launch traced here: 1680 us
  local copies, waits for them, and re-layouts  543 us (32%)
  matrix products  450 us (27%)
  waiting for transfers between devices  368 us (22%)
  other arithmetic  245 us (14%)
  loops' own time  54.8 us (3%)
  starting transfers between devices  17 us (1%)
    ppermute x20, waiting for transfers between devices, gather_group(): k_peer, v_peer = lax.ppermute((k_part, v_part), 'sp', perm_pairs)  368 us
    dot_general x30, matrix products, one_block(): jnp.einsum('qhd,khd->hqk', q_tile, k_seg, preferred_element_type=jnp.floa...  193 us
    dot_general x30, matrix products, one_block(): jnp.einsum('hqk,khd->qhd', p_tile, v_seg, preferred_element_type=jnp.floa...  162 us
    unnamed x122, local copies, waits for them, and re-layouts  134 us
    mul x14, local copies, waits for them, and re-layouts, spread_rows(): o_sp.reshape(n_seqs, n_rows, 1, n_heads // dilation, dilation, head_dim)  90.9 us
    another operation x6, local copies, waits for them, and re-layouts, pick_rows(): values.reshape(n_seqs, n_rows // dilation, dilation, n_heads // dilation,...  86.6 us
    concatenate x9, other arithmetic, gather_group(): v_part = jnp.concatenate([v_part, v_peer], axis=1)  73.6 us
    dot_general x3, matrix products, project(): jnp.dot(x_flat, weight.reshape(model_dim, n_heads * head_dim), preferred_...  71.5 us
  transfers between devices with their start and end apart: 20, of which 4 were waited for; matrix products, arithmetic and copies ran while one was open for 63% of the time, Pallas kernels for 0%

commit v1 on v0

v1 whole, which is shorter than its diff:
```python
import functools

import jax
import jax.numpy as jnp
from jax import lax
from jax.experimental import pallas as pl
from jax.experimental.pallas import tpu as pltpu
from jax.sharding import PartitionSpec as P


REL = (0, 4, 2, 6, 1, 5, 3, 7)
LOG2E = 1.4426950408889634
F32 = jnp.float32
BF16 = jnp.bfloat16
TILE = 256


def cost(flops, bytes_accessed, transcendentals=0):
    return pl.CostEstimate(flops=int(flops), bytes_accessed=int(bytes_accessed), transcendentals=int(transcendentals))


def onehot(transposed=False):
    dims = (1, 0) if transposed else (0, 1)
    out_row = lax.broadcasted_iota(jnp.int32, (TILE, TILE), dims[0])
    in_row = lax.broadcasted_iota(jnp.int32, (TILE, TILE), dims[1])
    hit = in_row == (out_row % 32) * 8 + out_row // 32
    return jnp.where(hit, 1.0, 0.0).astype(BF16)


def split_kernel(n_sub, a_ref, o_ref):
    take = onehot()
    for sub in range(n_sub):
        rows = jnp.dot(take, a_ref[sub * TILE:(sub + 1) * TILE, :], preferred_element_type=F32).astype(BF16)
        for res in range(8):
            o_ref[res, sub * 32:(sub + 1) * 32, :] = rows[res * 32:(res + 1) * 32]


def split_rows(a, n_sub):
    n_rows, width = a.shape
    blk = n_sub * TILE
    return pl.pallas_call(
        functools.partial(split_kernel, n_sub),
        grid=(n_rows // blk,),
        in_specs=[pl.BlockSpec((blk, width), lambda i: (i, 0))],
        out_specs=pl.BlockSpec((8, blk // 8, width), lambda i: (0, i, 0)),
        out_shape=jax.ShapeDtypeStruct((8, n_rows // 8, width), a.dtype),
        cost_estimate=cost(2 * n_rows * TILE * width, 4 * n_rows * width),
        name="split_rows",
    )(a)


def project_kernel(rels, n_seqs, n_w, whole, x_ref, *refs):
    head = pl.program_id(0)
    w_refs, o_refs = refs[:n_w], refs[n_w:]
    nb = x_ref.shape[1] // n_seqs
    for pos, rel in enumerate(rels):
        rows = x_ref[lax.rem(head + rel, 8)]
        for wi in range(n_w):
            out = jnp.dot(rows, w_refs[wi][0], preferred_element_type=F32).astype(BF16)
            for seq in range(n_seqs):
                part = out[seq * nb:(seq + 1) * nb]
                o_ref, at = (o_refs[0], seq) if whole else (o_refs[seq], 0)
                o_ref[wi, at, 0, pos * nb:(pos + 1) * nb, :] = part
                if whole and len(o_refs) > 1 and pos == 0:
                    o_refs[1][0, seq, 0] = part


def project(xp, ws, rels, n_seqs, whole=True, first_too=False):
    n_w, (_, rows, model_dim), head_dim = len(ws), xp.shape, ws[0].shape[2]
    n_heads, nb, n_pos = ws[0].shape[0], rows // n_seqs, len(rels)
    dims = [(n_w, n_seqs, n_heads, n_pos * nb, head_dim)] if whole else [(n_w, 1, n_heads, n_pos * nb, head_dim)] * n_seqs
    if first_too:
        dims.append((n_w, n_seqs, n_heads, nb, head_dim))
    return pl.pallas_call(
        functools.partial(project_kernel, rels, n_seqs, n_w, whole),
        grid=(n_heads,),
        in_specs=[pl.BlockSpec(xp.shape, lambda h: (0, 0, 0))]
        + [pl.BlockSpec((1, model_dim, head_dim), lambda h: (h, 0, 0)) for _ in ws],
        out_specs=[pl.BlockSpec((d[0], d[1], 1, d[3], d[4]), lambda h: (0, 0, h, 0, 0)) for d in dims],
        out_shape=[jax.ShapeDtypeStruct(d, BF16) for d in dims],
        cost_estimate=cost(2 * n_w * n_heads * n_pos * rows * model_dim * head_dim, 2 * (xp.size + n_w * ws[0].size) + 4 * n_w * n_pos * rows * n_heads * head_dim),
        name="project",
    )(xp, *ws)


def mult_of(group, key_group, level):
    return min(group, key_group) - level + 1


def by_group(groups, values):
    if all(value == 1 for value in values):
        return None
    n_rows = sum(rows for _, rows in groups)
    row = lax.broadcasted_iota(jnp.int32, (n_rows, 1), 0)
    column, base = jnp.full((n_rows, 1), float(values[-1]), F32), n_rows
    for value, (_, rows) in list(zip(values, groups))[::-1]:
        column = jnp.where(row < base, float(value), column)
        base -= rows
    return column


def lane_sum(p):
    total = p[:, :128]
    for lane in range(128, p.shape[1], 128):
        total = total + p[:, lane:lane + 128]
    return total


def scores(q, keys):
    return lax.dot_general(q, keys, (((1,), (1,)), ((), ())), preferred_element_type=F32)


def row_sum(p):
    return jnp.sum(p, axis=1, keepdims=True)


def run_tile(q, k_scr, v_scr, chunks, groups, level, state):
    scale = LOG2E * q.shape[1] ** -0.5
    for start, segs in chunks:
        size = sum(length for length, _ in segs)
        s = scores(q, k_scr[start:start + size, :])
        shift = jnp.max(s, axis=1, keepdims=True) * scale
        if state is not None:
            shift = jnp.maximum(state[0], shift)
        parts, off = [], 0
        for length, key_group in segs:
            mult = by_group(groups, [mult_of(group, key_group, level) for group, _ in groups])
            local = shift if mult is None else shift - jnp.log2(mult)
            parts.append(jnp.exp2(s[:, off:off + length] * scale - local))
            off += length
        p = parts[0] if len(parts) == 1 else jnp.concatenate(parts, axis=1)
        total = row_sum(lane_sum(p))
        acc = jnp.dot(p.astype(BF16), v_scr[start:start + size, :], preferred_element_type=F32)
        if state is not None:
            alpha = jnp.exp2(state[0] - shift)
            total = state[1] * alpha + total
            acc = state[2] * alpha + acc
        state = (shift, total, acc)
    return state


def run_branch0(q, k_scr, v_scr, chunks, groups, s_scr, p_scr):
    scale = LOG2E * q.shape[1] ** -0.5
    peak = None
    for start, segs in chunks:
        size = sum(length for length, _ in segs)
        s = scores(q, k_scr[start:start + size, :])
        s_scr[:, start:start + size] = s
        top = s[:, :128]
        for lane in range(128, size, 128):
            top = jnp.maximum(top, s[:, lane:lane + 128])
        peak = top if peak is None else jnp.maximum(peak, top)
    shift = jnp.max(peak, axis=1, keepdims=True) * scale
    sums = {}
    for start, segs in chunks:
        for length, key_group in segs:
            p = jnp.exp2(s_scr[:, start:start + length] * scale - shift)
            s_scr[:, start:start + length] = p
            part = lane_sum(p)
            sums[key_group] = part if key_group not in sums else sums[key_group] + part
            start += length
    sums = {key_group: row_sum(part) for key_group, part in sums.items()}
    total = functools.reduce(jnp.add, sums.values())
    inverse = 1.0 / total
    factors = {}
    for key_group in sums:
        mult = by_group(groups, [mult_of(group, key_group, 0) for group, _ in groups])
        factors[key_group] = inverse if mult is None else inverse * mult
    for start, segs in chunks:
        for length, key_group in segs:
            p_scr[:, start:start + length] = (s_scr[:, start:start + length] * factors[key_group]).astype(BF16)
            start += length
    acc = jnp.dot(p_scr[...], v_scr[...], preferred_element_type=F32)
    weight = functools.reduce(jnp.add, [sums[key_group] * factors[key_group] for key_group in sums])
    return shift + jnp.log2(total), weight, acc


def merge(one, two):
    shift = jnp.maximum(one[0], two[0])
    w_one, w_two = jnp.exp2(one[0] - shift), jnp.exp2(two[0] - shift)
    return shift, one[1] * w_one + two[1] * w_two, one[2] * w_one + two[2] * w_two


def gather_keys(kv_refs, k_scr, v_scr):
    off = 0
    for ref in kv_refs:
        rows = ref.shape[3]
        k_scr[off:off + rows, :] = ref[0, 0, 0]
        v_scr[off:off + rows, :] = ref[1, 0, 0]
        off += rows


def put_state(acc_ref, stat_ref, state):
    shift, total, acc = state
    lane = lax.broadcasted_iota(jnp.int32, (shift.shape[0], 128), 1)
    acc_ref[0, 0] = acc
    stat_ref[0, 0] = jnp.where(lane < 64, shift, total)


def get_state(acc_ref, stat_ref):
    stat = stat_ref[0, 0]
    return stat[:, 0:1], stat[:, 64:65], acc_ref[0, 0]


def cut(state, lo, hi):
    return tuple(part[lo:hi] for part in state)


def finish(state):
    return (state[2] / state[1]).astype(BF16)


def level0_kernel(nb, q_ref, *refs):
    kv_refs, (o_ref, acc_ref, stat_ref, k_scr, v_scr, s_scr, p_scr) = refs[:8], refs[8:]
    gather_keys(kv_refs, k_scr, v_scr)
    chunks = ((0, ((2 * nb, 3), (2 * nb, 2))), (4 * nb, ((4 * nb, 1),)), (8 * nb, ((4 * nb, 0),)), (12 * nb, ((4 * nb, 0),)))
    low = run_branch0(q_ref[0, 0, 0, :4 * nb, :], k_scr, v_scr, chunks, ((3, nb), (2, nb), (1, 2 * nb)), s_scr, p_scr)
    put_state(acc_ref, stat_ref, low)
    high = run_branch0(q_ref[0, 0, 0, 4 * nb:, :], k_scr, v_scr, chunks, ((0, 4 * nb),), s_scr, p_scr)
    o_ref[0, 0] = finish(high)


def level1_kernel(nb, q_ref, *refs):
    kv_refs, (acc_in, stat_in, acc_two, stat_two, far_ref, o_ref, k_scr, v_scr) = refs[:6], refs[6:]
    gather_keys(kv_refs, k_scr, v_scr)
    chunks = ((0, ((2 * nb, 3), (2 * nb, 2))), (4 * nb, ((4 * nb, 1),)))
    state = run_tile(q_ref[0, 0, 0], k_scr, v_scr, chunks, ((3, nb), (2, nb), (1, 2 * nb)), 1, get_state(acc_in, stat_in))
    o_ref[0, 0, 2 * nb:, :] = finish(cut(state, 2 * nb, 4 * nb))
    two = get_state(acc_two, stat_two)
    o_ref[0, 0, nb:2 * nb, :] = finish(merge(cut(state, nb, 2 * nb), cut(two, nb, 2 * nb)))

    def column(lane):
        return jnp.transpose(jnp.broadcast_to(far_ref[0, 0, nb:nb + 1, lane:lane + nb], (128, nb)))[:, 0:1]

    far = (column(0), column(128), far_ref[0, 0, :nb, :])
    o_ref[0, 0, :nb, :] = finish(merge(merge(cut(state, 0, nb), cut(two, 0, nb)), far))


def level2_kernel(nb, q_ref, *refs):
    kv_refs, (acc_ref, stat_ref, k_scr, v_scr) = refs[:8], refs[8:]
    gather_keys(kv_refs, k_scr, v_scr)
    chunks = ((0, ((4 * nb, 3),)), (4 * nb, ((4 * nb, 2),)))
    put_state(acc_ref, stat_ref, run_tile(q_ref[0, 0, 0], k_scr, v_scr, chunks, ((3, nb), (2, nb)), 2, None))


def level3_kernel(nb, q_ref, *refs):
    kv_refs, (far_ref, k_scr, v_scr) = refs[:8], refs[8:]
    gather_keys(kv_refs, k_scr, v_scr)
    shift, total, acc = run_tile(q_ref[0, 0, 0], k_scr, v_scr, ((0, ((8 * nb, 3),)),), ((3, nb),), 3, None)
    far_ref[0, 0, :nb, :] = acc
    far_ref[0, 0, nb:, 0:nb] = jnp.transpose(jnp.broadcast_to(shift, (nb, 128)))[0:8, :]
    far_ref[0, 0, nb:, 128:128 + nb] = jnp.transpose(jnp.broadcast_to(total, (nb, 128)))[0:8, :]


def attend(body, nb, q, q_rows, kvs, states, outs, seqs, with_scores=False):
    n_heads, head_dim = q.shape[2], q.shape[4]
    n_keys = sum(kv.shape[3] for kv in kvs)
    first, n_seqs = seqs

    def spec(n_here, rows, width):
        base = first if n_here > n_seqs else 0
        return pl.BlockSpec((1, 1, rows, width), lambda s, h: (s + base, h, 0, 0))

    def lead_spec(lead, n_here, rows):
        base = first if n_here > n_seqs else 0
        return pl.BlockSpec((lead, 1, 1, rows, head_dim), lambda s, h: (0, s + base, h, 0, 0))

    pairs = n_seqs * n_heads * q_rows * n_keys
    scratch = [pltpu.VMEM((n_keys, head_dim), BF16)] * 2
    if with_scores:
        scratch += [pltpu.VMEM((q_rows // 2, n_keys), F32), pltpu.VMEM((q_rows // 2, n_keys), BF16)]
    return pl.pallas_call(
        functools.partial(body, nb),
        grid=(n_seqs, n_heads),
        in_specs=[lead_spec(1, q.shape[1], q_rows)]
        + [lead_spec(2, kv.shape[1], kv.shape[3]) for kv in kvs]
        + [spec(state.shape[0], *state.shape[2:]) for state in states],
        out_specs=[spec(n_seqs, rows, width) for rows, width, _ in outs],
        out_shape=[jax.ShapeDtypeStruct((n_seqs, n_heads, rows, width), dtype) for rows, width, dtype in outs],
        scratch_shapes=scratch,
        cost_estimate=cost(4 * pairs * head_dim, 2 * n_seqs * n_heads * head_dim * (q_rows + 2 * n_keys), pairs),
    )(q, *kvs, *states)


def out_kernel(nb, n_sub, o_low, o_high, w_ref, *refs):
    y_ref, mix, lhs = refs[-3:]
    blk = pl.program_id(0)
    back = onehot(transposed=True)
    for sub in range(n_sub):
        first = pl.multiple_of((blk * n_sub + sub) * 32, 32)
        for res in range(8):
            for head in range(8):
                pos = REL[(res - head) % 8]
                ref, base = (o_low, 0) if pos < 4 else (o_high, 4)
                piece = ref[0, head, pl.ds((pos - base) * nb + first, 32), :]
                mix[res * 32:(res + 1) * 32, head * piece.shape[1]:(head + 1) * piece.shape[1]] = piece
        lhs[sub * TILE:(sub + 1) * TILE, :] = jnp.dot(back, mix[...], preferred_element_type=F32).astype(BF16)
    y_ref[0] = jnp.dot(lhs[...], w_ref[...], preferred_element_type=F32).astype(BF16)


def out_project(o_low, o_high, w, nb, seq, n_seqs, y_prev):
    width, model_dim = w.shape
    n_tok = nb * 8
    n_sub = min(2, n_tok // TILE)
    blk = n_sub * TILE
    in_specs = [pl.BlockSpec(a.shape, lambda i: (0, 0, 0, 0)) for a in (o_low, o_high)] + [pl.BlockSpec(w.shape, lambda i: (0, 0))]
    more = () if y_prev is None else (y_prev,)
    return pl.pallas_call(
        functools.partial(out_kernel, nb, n_sub),
        grid=(n_tok // blk,),
        in_specs=in_specs + [pl.BlockSpec(memory_space=pl.ANY) for _ in more],
        out_specs=pl.BlockSpec((1, blk, model_dim), lambda i: (seq, i, 0)),
        out_shape=jax.ShapeDtypeStruct((n_seqs, n_tok, model_dim), BF16),
        scratch_shapes=[pltpu.VMEM((TILE, width), BF16), pltpu.VMEM((blk, width), BF16)],
        input_output_aliases={3: 0} if more else {},
        cost_estimate=cost(2 * n_tok * width * model_dim, 4 * n_tok * width + 2 * w.size),
        name="out_project",
    )(o_low, o_high, w, *more)


def solution(mesh):
    n_dev = mesh.shape['sp']

    def swap(a, bit):
        return lax.ppermute(a, 'sp', [(d, d ^ bit) for d in range(n_dev)])

    def local_step(x_loc, w_q, w_k, w_v, w_o):
        n_seqs, n_tok, model_dim = x_loc.shape
        n_heads, head_dim = w_q.shape[1], w_q.shape[2]
        nb = n_tok // 8
        n_rows = n_seqs * n_tok
        after = lax.optimization_barrier

        def per_head(w):
            rows = w.reshape(model_dim * n_heads, head_dim)
            return split_rows(rows, 8 if rows.shape[0] % (8 * TILE) == 0 else 1)

        xp = split_rows(x_loc.reshape(n_rows, model_dim), 2 if n_rows % 512 == 0 else 1)
        wk, wv = per_head(w_k), per_head(w_v)

        e, = project(xp, (wk, wv), REL[0:1], n_seqs)
        wk, wv, e = after((wk, wv, e))
        y_e, z_e, c_e = swap(e, 2), swap(e, 4), swap(e, 1)
        b, = project(xp, (wk, wv), REL[1:2], n_seqs)
        wk, wv, b = after((wk, wv, b))
        y_b, z_b, c_b = swap(b, 2), swap(b, 4), swap(b, 1)
        g = project(xp, (wk, wv), REL[2:4], n_seqs, whole=False)
        wk, wv, g = after((wk, wv, g))
        y_g = [swap(g[0], 2)]
        c_g = [swap(g[0], 1), swap(g[1], 1)]
        r, = project(xp, (wk, wv), REL[4:8], n_seqs)
        w_q, r = after((w_q, r))
        c_r = swap(r, 1)
        wq = per_head(w_q)
        q_all, q_first = project(xp, (wq,), REL, n_seqs, first_too=True)

        q_all, q_first, y_e, z_e = after((q_all, q_first, y_e, z_e))
        zy_e, yc_e, zc_e = swap(y_e, 4), swap(y_e, 1), swap(z_e, 1)
        q_far = swap(q_first, 8)

        def level0(seq, q):
            kvs = (e, c_e, b, c_b, g[seq], c_g[seq], r, c_r)
            return attend(level0_kernel, nb, q, 8 * nb, kvs, (),
                          ((4 * nb, head_dim, BF16), (4 * nb, head_dim, F32), (4 * nb, 128, F32)), (seq, 1), with_scores=True)

        near0 = level0(0, q_all)
        near0, q_all, y_b, z_b, g1 = after((near0, q_all, y_b, z_b, g[1]))
        zy_b, yc_b, zc_b = swap(z_b, 2), swap(y_b, 1), swap(z_b, 1)
        y_g.append(swap(g1, 2))
        near1 = level0(1, q_all)
        near1, q_all, q_far, zy_e, y_g[0] = after((near1, q_all, q_far, zy_e, y_g[0]))
        near = (near0, near1)
        zyc_e = swap(zy_e, 1)
        yc_g = [swap(y_g[0], 1)]
        far, = attend(level3_kernel, nb, q_far, nb, (e, c_e, y_e, yc_e, z_e, zc_e, zy_e, zyc_e), (),
                      ((nb + 8, head_dim, F32),), (0, n_seqs))
        far_in = swap(far, 8)
        far, q_all, zy_b = after((far, q_all, zy_b))
        zyc_b = swap(zy_b, 1)
        two = attend(level2_kernel, nb, q_all, 2 * nb, (z_e, zc_e, zy_e, zyc_e, z_b, zc_b, zy_b, zyc_b), (),
                     ((2 * nb, head_dim, F32), (2 * nb, 128, F32)), (0, n_seqs))
        y = None
        w_out = w_o.reshape(n_heads * head_dim, model_dim)
        for seq in range(n_seqs):
            o_high, acc, stat = near[seq]
            kvs = (y_e, yc_e, y_b, yc_b, y_g[seq], yc_g[seq])
            o_low, = attend(level1_kernel, nb, q_all, 4 * nb, kvs, (acc, stat, *two, far_in), ((4 * nb, head_dim, BF16),), (seq, 1))
            if seq == 0:
                o_low, y_g[1] = after((o_low, y_g[1]))
                yc_g.append(swap(y_g[1], 1))
            y = out_project(o_low, o_high, w_out, nb, seq, n_seqs, y)
        return y

    return jax.shard_map(local_step, mesh=mesh, in_specs=(P('dp', 'sp', None), P(), P(), P(), P()), out_specs=P('dp', 'sp', None), check_vma=False)
```

time: 1690 us -> 517 us (0.31)
  local copies, waits for them, and re-layouts: 543 us -> 2.71 us
  matrix products: 450 us -> 0 us
  Pallas kernels: 0 us -> 339 us
  other arithmetic: 245 us -> 0 us
  waiting for transfers between devices: 368 us -> 156 us
  loops' own time: 54.8 us -> 0 us
    dot_general x64 -> x0, matrix products: 450 us -> none  [the longest x30 193 us: one_block(): jnp.einsum('qhd,khd->hqk', q_tile, k_seg, preferred_element_type=jnp.floa...]
    pallas_call x0 -> x17, Pallas kernels: none -> 339 us  [the longest x6 175 us: attend(): pl.pallas_call(functools.partial(body, nb), grid=(n_seqs, n_heads), in_sp...]
    ppermute x20 -> x23, waiting for transfers between devices: 368 us -> 156 us  [swap(): return lax.ppermute(a, 'sp', [(d, d ^ bit) for d in range(n_dev)])]
    concatenate x18 -> x0, other arithmetic: 144 us -> none  [the longest x9 73.6 us: gather_group(): v_part = jnp.concatenate([v_part, v_peer], axis=1)]
    unnamed x122 -> x8, local copies, waits for them, and re-layouts: 134 us -> 2.71 us
    another operation x14 -> x0, local copies, waits for them, and re-layouts: 97.8 us -> none  [the longest x6 86.6 us: pick_rows(): values.reshape(n_seqs, n_rows // dilation, dilation, n_heads // dilation,...]
    mul x14 -> x0, local copies, waits for them, and re-layouts: 90.9 us -> none  [spread_rows(): o_sp.reshape(n_seqs, n_rows, 1, n_heads // dilation, dilation, head_dim)]
    slice x9 -> x0, local copies, waits for them, and re-layouts: 60.4 us -> none  [pick_rows(): split_view[:, :, phase_idx, :, phase_idx, :]]
  transfers between devices with their start and end apart: 20 -> 23, of which waited for: 4 -> 7; matrix products, arithmetic and copies ran while one was open for 63% -> 0% of each run, Pallas kernels for 0% -> 38%
where the time goes in v1:
time: 517 us; the launch traced here: 515 us
  Pallas kernels  339 us (66%)
  waiting for transfers between devices  156 us (30%)
  starting transfers between devices  17.8 us (3%)
    pallas_call x6, Pallas kernels, attend(): pl.pallas_call(functools.partial(body, nb), grid=(n_seqs, n_heads), in_sp...  175 us
    ppermute x23, waiting for transfers between devices, swap(): return lax.ppermute(a, 'sp', [(d, d ^ bit) for d in range(n_dev)])  156 us
    pallas_call x5, Pallas kernels, project(): pl.pallas_call(functools.partial(project_kernel, rels, n_seqs, n_w, whole...  91.7 us
    pallas_call x4, Pallas kernels, split_rows(): pl.pallas_call(functools.partial(split_kernel, n_sub), grid=(n_rows // bl...  40.1 us
    pallas_call x2, Pallas kernels, out_project(): pl.pallas_call(functools.partial(out_kernel, nb, n_sub), grid=(n_tok // b...  32.4 us
    ppermute x23, starting transfers between devices, swap(): return lax.ppermute(a, 'sp', [(d, d ^ bit) for d in range(n_dev)])  17.8 us
  transfers between devices with their start and end apart: 23, of which 7 were waited for; matrix products, arithmetic and copies ran while one was open for 0% of the time, Pallas kernels for 38%

profile of v1, /device:TPU:0, one launch (start us, length us, event | category | flops | bytes accessed | tf_op | source)
XLA Modules:
  0.0 515.3 jit_solution(3254894471959217459)
XLA Ops:
  0.0 8.2 %split_rows.4.x_ref = bf16[8,256,2048]{2,1,0:T(8,128)(2,1)} custom-call(bf16[2048,2048]{1,0:T(8,128)(2,1)} %bitcast.5), custom_call_target="tpu_custom_call" | custom-call | flops 2147483648 | bytes 16777216 | tf_op jit(solution)/shard_map/split_rows/pallas_call | solution.py:41
  8.2 10.4 %split_rows.5.refs_0_ = bf16[8,2048,256]{2,1,0:T(8,128)(2,1)} custom-call(bf16[16384,256]{1,0:T(8,128)(2,1)} %bitcast.6), custom_call_target="tpu_custom_call" | custom-call | flops 2147483648 | bytes 16777216 | tf_op jit(solution)/shard_map/split_rows/pallas_call | solution.py:41
  18.6 10.4 %split_rows.6.refs_1_ = bf16[8,2048,256]{2,1,0:T(8,128)(2,1)} custom-call(bf16[16384,256]{1,0:T(8,128)(2,1)} %bitcast.7), custom_call_target="tpu_custom_call" | custom-call | flops 2147483648 | bytes 16777216 | tf_op jit(solution)/shard_map/split_rows/pallas_call | solution.py:41
  29.0 13.7 %project.5.refs_0_ = bf16[2,2,8,128,256]{4,3,2,1,0:T(8,128)(2,1)} custom-call(bf16[8,256,2048]{2,1,0:T(8,128)(2,1)} %split_rows.4.x_ref, bf16[8,2048,256]{2,1,0:T(8,128)(2,1)} %split_rows.5.refs_0_, bf16[8,2048,256]{2,1,0:T(8,128)(2,1)} %split_rows.6.refs_1_), custom_call_target="tpu_custom_call" | custom-call | flops 4294967296 | bytes 29360128 | tf_op jit(solution)/shard_map/project/pallas_call | solution.py:74
  42.7 13.7 %project.6.refs_2_ = bf16[2,2,8,128,256]{4,3,2,1,0:T(8,128)(2,1)} custom-call(bf16[8,256,2048]{2,1,0:T(8,128)(2,1)} %split_rows.4.x_ref, bf16[8,2048,256]{2,1,0:T(8,128)(2,1)} %split_rows.5.refs_0_, bf16[8,2048,256]{2,1,0:T(8,128)(2,1)} %split_rows.6.refs_1_), custom_call_target="tpu_custom_call" | custom-call | flops 4294967296 | bytes 29360128 | tf_op jit(solution)/shard_map/project/pallas_call | solution.py:74
  56.5 16.6 %project.7 = (bf16[2,1,8,256,256]{4,3,2,1,0:T(8,128)(2,1)}, bf16[2,1,8,256,256]{4,3,2,1,0:T(8,128)(2,1)}) custom-call(bf16[8,256,2048]{2,1,0:T(8,128)(2,1)} %split_rows.4.x_ref, bf16[8,2048,256]{2,1,0:T(8,128)(2,1)} %split_rows.5.refs_0_, bf16[8,2048,256]{2,1,0:T(8,128)(2,1)} %split_rows.6.refs_1_), custom_call_target="tpu_custom_call" | custom-call | flops 8589934592 | bytes 33554432 | tf_op jit(solution)/shard_map/project/pallas_call | solution.py:74
  73.1 23.9 %project.8.refs_6_ = bf16[2,2,8,512,256]{4,3,2,1,0:T(8,128)(2,1)} custom-call(bf16[8,256,2048]{2,1,0:T(8,128)(2,1)} %split_rows.4.x_ref, bf16[8,2048,256]{2,1,0:T(8,128)(2,1)} %split_rows.5.refs_0_, bf16[8,2048,256]{2,1,0:T(8,128)(2,1)} %split_rows.6.refs_1_), custom_call_target="tpu_custom_call" | custom-call | flops 17179869184 | bytes 41943040 | tf_op jit(solution)/shard_map/project/pallas_call | solution.py:74
  97.0 0.5 collective-permute-start.5
  97.5 2.5 collective-permute-start
  100.0 1.6 collective-permute-start.1
  101.6 0.0 collective-permute-start.4
  101.6 0.5 collective-permute-start.3
  102.1 44.4 %collective-permute-done.refs_2_.refs_0_ = bf16[2,2,8,128,256]{4,3,2,1,0:T(8,128)(2,1)S(1)} collective-permute-done((bf16[2,2,8,128,256]{4,3,2,1,0:T(8,128)(2,1)}, bf16[2,2,8,128,256]{4,3,2,1,0:T(8,128)(2,1)S(1)}, u32[]{:S(2)}, u32[]{:S(2)}) %collective-permute-start) | collective-permute-done | bytes 2097184 | tf_op jit(solution)/shard_map/ppermute | solution.py:325
  146.5 0.0 collective-permute-start.2
  146.6 11.2 %split_rows.7.refs_0_ = bf16[8,2048,256]{2,1,0:T(8,128)(2,1)} custom-call(bf16[16384,256]{1,0:T(8,128)(2,1)} %bitcast.8), custom_call_target="tpu_custom_call" | custom-call | flops 2147483648 | bytes 16777216 | tf_op jit(solution)/shard_map/split_rows/pallas_call | solution.py:41
  157.7 0.0 collective-permute-done.1.refs_4_.refs_0_
  157.7 1.7 collective-permute-start.6
  159.5 0.0 collective-permute-done.4.refs_5_
  159.5 1.6 collective-permute-start.7
  161.1 0.0 collective-permute-done.3.refs_3_
  161.1 0.0 collective-permute-start.8
  161.1 23.6 %project.9 = (bf16[1,2,8,1024,256]{4,3,2,1,0:T(8,128)(2,1)}, bf16[1,2,8,128,256]{4,3,2,1,0:T(8,128)(2,1)}) custom-call(bf16[8,256,2048]{2,1,0:T(8,128)(2,1)} %split_rows.4.x_ref, bf16[8,2048,256]{2,1,0:T(8,128)(2,1)} %split_rows.7.refs_0_), custom_call_target="tpu_custom_call" | custom-call | flops 17179869184 | bytes 33554432 | tf_op jit(solution)/shard_map/project/pallas_call | solution.py:74
  184.7 0.0 collective-permute-done.2.refs_1_
  184.7 0.5 collective-permute-start.11
  185.2 0.0 collective-permute-done.5.refs_7_
  185.2 0.2 collective-permute-start.10
  185.4 40.8 %shard_map.55 = (bf16[1,8,512,256]{3,2,1,0:T(8,128)(2,1)}, f32[1,8,512,256]{3,2,1,0:T(8,128)}, f32[1,8,512,128]{3,2,1,0:T(8,128)}) custom-call(bf16[1,2,8,1024,256]{4,3,2,1,0:T(8,128)(2,1)} %get-tuple-element.82.q_ref, bf16[2,2,8,128,256]{4,3,2,1,0:T(8,128)(2,1)} %project.5.refs_0_, bf16[2,2,8,128,256]{4,3,2,1,0:T(8,128)(2,1)} %collective-permute-done.2.refs_1_, ...), custom_call_target="tpu_custom_call" | custom-call | flops 17179869184 | bytes 20971520 | tf_op jit(solution)/shard_map/pallas_call | solution.py:272
  226.2 0.0 collective-permute-done.6.refs_2_
  226.2 0.1 collective-permute-start.12
  226.4 0.0 collective-permute-done.7.refs_4_
  226.4 2.8 collective-permute-start.9
  229.1 0.0 collective-permute-done.8.refs_5_
  229.1 0.1 collective-permute-start.13
  229.3 40.7 %shard_map.56 = (bf16[1,8,512,256]{3,2,1,0:T(8,128)(2,1)}, f32[1,8,512,256]{3,2,1,0:T(8,128)}, f32[1,8,512,128]{3,2,1,0:T(8,128)}) custom-call(bf16[1,2,8,1024,256]{4,3,2,1,0:T(8,128)(2,1)} %get-tuple-element.82.q_ref, bf16[2,2,8,128,256]{4,3,2,1,0:T(8,128)(2,1)} %project.5.refs_0_, bf16[2,2,8,128,256]{4,3,2,1,0:T(8,128)(2,1)} %collective-permute-done.2.refs_1_, ...), custom_call_target="tpu_custom_call" | custom-call | flops 17179869184 | bytes 20971520 | tf_op jit(solution)/shard_map/pallas_call | solution.py:272
  269.9 0.0 collective-permute-done.11.refs_4_
  270.0 3.4 collective-permute-done.9.q_ref
  273.3 0.9 collective-permute-done.10.refs_6_.refs_2_
  274.2 0.0 collective-permute-start.14
  274.2 3.0 collective-permute-start.15
  277.2 0.2 collective-permute-start.18
  277.4 0.0 collective-permute-done.12.refs_3_.refs_1_
  277.4 0.0 collective-permute-done.13.refs_5_.refs_1_
  277.4 1.3 collective-permute-done.14.refs_7_.refs_3_
  278.7 18.0 %shard_map.57 = f32[2,8,136,256]{3,2,1,0:T(8,128)} custom-call(bf16[1,2,8,128,256]{4,3,2,1,0:T(8,128)(2,1)} %copy-done.3, bf16[2,2,8,128,256]{4,3,2,1,0:T(8,128)(2,1)} %project.5.refs_0_, bf16[2,2,8,128,256]{4,3,2,1,0:T(8,128)(2,1)} %collective-permute-done.2.refs_1_, bf16[2,2,8,128,256]{4,3,2,1,0:T(8,128)(2,1)} %copy-done, ...), custom_call_target="tpu_custom_call" | custom-call | flops 2147483648 | bytes 17825792 | tf_op jit(solution)/shard_map/pallas_call | solution.py:272
  296.7 27.1 %collective-permute-done.15.refs_6_ = bf16[2,2,8,128,256]{4,3,2,1,0:T(8,128)(2,1)} collective-permute-done((bf16[2,2,8,128,256]{4,3,2,1,0:T(8,128)(2,1)}, bf16[2,2,8,128,256]{4,3,2,1,0:T(8,128)(2,1)}, u32[]{:S(2)}, u32[]{:S(2)}) %collective-permute-start.15) | collective-permute-done | bytes 2097184 | tf_op jit(solution)/shard_map/ppermute | solution.py:325
  323.8 0.0 collective-permute-start.19
  323.8 1.3 collective-permute-start.20
  325.0 0.2 collective-permute-start.17
  325.3 0.3 collective-permute-start.16
  325.6 0.0 collective-permute-done.18.refs_5_
  325.6 0.5 collective-permute-start.21
  326.1 2.2 collective-permute-done.19.refs_7_
  328.3 19.0 %shard_map.58 = (f32[2,8,256,256]{3,2,1,0:T(8,128)}, f32[2,8,256,128]{3,2,1,0:T(8,128)}) custom-call(bf16[1,2,8,1024,256]{4,3,2,1,0:T(8,128)(2,1)} %get-tuple-element.82.q_ref, bf16[2,2,8,128,256]{4,3,2,1,0:T(8,128)(2,1)} %collective-permute-done.1.refs_4_.refs_0_, bf16[2,2,8,128,256]{4,3,2,1,0:T(8,128)(2,1)} %collective-permute-done.13.refs_5_.refs_1_, ...), custom_call_target="tpu_custom_call" | custom-call | flops 4294967296 | bytes 18874368 | tf_op jit(solution)/shard_map/pallas_call | solution.py:272
  347.3 0.0 collective-permute-done.17.refs_5_
  347.3 0.0 collective-permute-done.16.refs_3_
  347.3 76.2 %collective-permute-done.20.refs_10_ = f32[2,8,136,256]{3,2,1,0:T(8,128)S(1)} collective-permute-done((f32[2,8,136,256]{3,2,1,0:T(8,128)}, f32[2,8,136,256]{3,2,1,0:T(8,128)S(1)}, u32[]{:S(2)}, u32[]{:S(2)}) %collective-permute-start.20) | collective-permute-done | bytes 2228256 | tf_op jit(solution)/shard_map/ppermute | solution.py:325
  423.5 1.3 copy-done.1
  424.8 28.4 %shard_map.59.o_low = bf16[1,8,512,256]{3,2,1,0:T(8,128)(2,1)} custom-call(bf16[1,2,8,1024,256]{4,3,2,1,0:T(8,128)(2,1)} %get-tuple-element.82.q_ref, bf16[2,2,8,128,256]{4,3,2,1,0:T(8,128)(2,1)} %copy-done, bf16[2,2,8,128,256]{4,3,2,1,0:T(8,128)(2,1)} %collective-permute-done.12.refs_3_.refs_1_, ...), custom_call_target="tpu_custom_call" | custom-call | flops 4294967296 | bytes 10485760 | tf_op jit(solution)/shard_map/pallas_call | solution.py:272
  453.2 0.1 collective-permute-start.22
  453.3 16.1 %out_project.2.refs_0_ = bf16[2,1024,2048]{2,1,0:T(8,128)(2,1)} custom-call(bf16[1,8,512,256]{3,2,1,0:T(8,128)(2,1)} %shard_map.59.o_low, bf16[1,8,512,256]{3,2,1,0:T(8,128)(2,1)} %get-tuple-element.96.o_high, bf16[2048,2048]{1,0:T(8,128)(2,1)} %bitcast.9), custom_call_target="tpu_custom_call" | custom-call | flops 8589934592 | bytes 16777216 | tf_op jit(solution)/shard_map/out_project/pallas_call | solution.py:308
  469.4 0.0 collective-permute-done.22.refs_5_
  469.4 1.4 copy-done.2
  470.7 28.2 %shard_map.60.o_low = bf16[1,8,512,256]{3,2,1,0:T(8,128)(2,1)} custom-call(bf16[1,2,8,1024,256]{4,3,2,1,0:T(8,128)(2,1)} %get-tuple-element.82.q_ref, bf16[2,2,8,128,256]{4,3,2,1,0:T(8,128)(2,1)} %copy-done, bf16[2,2,8,128,256]{4,3,2,1,0:T(8,128)(2,1)} %collective-permute-done.12.refs_3_.refs_1_, ...), custom_call_target="tpu_custom_call" | custom-call | flops 4294967296 | bytes 10485760 | tf_op jit(solution)/shard_map/pallas_call | solution.py:272
  498.9 16.3 %out_project.3 = bf16[2,1024,2048]{2,1,0:T(8,128)(2,1)} custom-call(bf16[1,8,512,256]{3,2,1,0:T(8,128)(2,1)} %shard_map.60.o_low, bf16[1,8,512,256]{3,2,1,0:T(8,128)(2,1)} %get-tuple-element.94.o_high, bf16[2048,2048]{1,0:T(8,128)(2,1)} %bitcast.10, bf16[2,1024,2048]{2,1,0:T(8,128)(2,1)} %out_project.2.refs_0_), custom_call_target="tpu_custom_call", output_to_operand_aliasing={{}: (3, {})} | custom-call | flops 8589934592 | bytes 16777216 | tf_op jit(solution)/shard_map/out_project/pallas_call | solution.py:308
  (7 shorter events, 0.0 us)
Async XLA Ops:
  97.0 88.2 %collective-permute-start.5 = (bf16[2,2,8,512,256]{4,3,2,1,0:T(8,128)(2,1)}, bf16[2,2,8,512,256]{4,3,2,1,0:T(8,128)(2,1)}, u32[]{:S(2)}, u32[]{:S(2)}) collective-permute-start(bf16[2,2,8,512,256]{4,3,2,1,0:T(8,128)(2,1)} %project.8.refs_6_), channel_id=1, source_target_pairs={{0,1},{1,0},{2,3},{3,2},{4,5},{5,4},{6,7},{7,6},{8,9},{9,8},{10,11... | collective-permute-start | bytes 25165832 | tf_op jit(solution)/shard_map/ppermute | solution.py:325
  97.5 49.0 %collective-permute-start = (bf16[2,2,8,128,256]{4,3,2,1,0:T(8,128)(2,1)}, bf16[2,2,8,128,256]{4,3,2,1,0:T(8,128)(2,1)S(1)}, u32[]{:S(2)}, u32[]{:S(2)}) collective-permute-start(bf16[2,2,8,128,256]{4,3,2,1,0:T(8,128)(2,1)} %project.5.refs_0_), channel_id=1, source_target_pairs={{0,2},{1,3},{2,0},{3,1},{4,6},{5,7},{6,4},{7,5},{8,10},{9,11},{10,... | collective-permute-start | bytes 6291464 | tf_op jit(solution)/shard_map/ppermute | solution.py:325
  100.0 57.7 %collective-permute-start.1 = (bf16[2,2,8,128,256]{4,3,2,1,0:T(8,128)(2,1)}, bf16[2,2,8,128,256]{4,3,2,1,0:T(8,128)(2,1)}, u32[]{:S(2)}, u32[]{:S(2)}) collective-permute-start(bf16[2,2,8,128,256]{4,3,2,1,0:T(8,128)(2,1)} %project.5.refs_0_), channel_id=1, source_target_pairs={{0,4},{1,5},{2,6},{3,7},{4,0},{5,1},{6,2},{7,3},{8,12},{9,13},{10,... | collective-permute-start | bytes 6291464 | tf_op jit(solution)/shard_map/ppermute | solution.py:325
  101.6 57.9 %collective-permute-start.4 = (bf16[2,1,8,256,256]{4,3,2,1,0:T(8,128)(2,1)}, bf16[2,1,8,256,256]{4,3,2,1,0:T(8,128)(2,1)}, u32[]{:S(2)}, u32[]{:S(2)}) collective-permute-start(bf16[2,1,8,256,256]{4,3,2,1,0:T(8,128)(2,1)} %get-tuple-element.65.refs_4_), channel_id=1, source_target_pairs={{0,1},{1,0},{2,3},{3,2},{4,5},{5,4},{6,7},{7,6},{8,9},{9,8},{10,11... | collective-permute-start | bytes 6291464 | tf_op jit(solution)/shard_map/ppermute | solution.py:325
  101.6 59.5 %collective-permute-start.3 = (bf16[2,2,8,128,256]{4,3,2,1,0:T(8,128)(2,1)}, bf16[2,2,8,128,256]{4,3,2,1,0:T(8,128)(2,1)}, u32[]{:S(2)}, u32[]{:S(2)}) collective-permute-start(bf16[2,2,8,128,256]{4,3,2,1,0:T(8,128)(2,1)} %project.6.refs_2_), channel_id=1, source_target_pairs={{0,1},{1,0},{2,3},{3,2},{4,5},{5,4},{6,7},{7,6},{8,9},{9,8},{10,11... | collective-permute-start | bytes 6291464 | tf_op jit(solution)/shard_map/ppermute | solution.py:325
  146.5 79.7 %copy-start = (bf16[2,2,8,128,256]{4,3,2,1,0:T(8,128)(2,1)}, bf16[2,2,8,128,256]{4,3,2,1,0:T(8,128)(2,1)S(1)}, u32[]{:S(2)}) copy-start(bf16[2,2,8,128,256]{4,3,2,1,0:T(8,128)(2,1)S(1)} %collective-permute-done.refs_2_.refs_0_) | copy-start | bytes 6291460
  146.5 38.2 %collective-permute-start.2 = (bf16[2,2,8,128,256]{4,3,2,1,0:T(8,128)(2,1)}, bf16[2,2,8,128,256]{4,3,2,1,0:T(8,128)(2,1)}, u32[]{:S(2)}, u32[]{:S(2)}) collective-permute-start(bf16[2,2,8,128,256]{4,3,2,1,0:T(8,128)(2,1)} %project.5.refs_0_), channel_id=1, source_target_pairs={{0,1},{1,0},{2,3},{3,2},{4,5},{5,4},{6,7},{7,6},{8,9},{9,8},{10,11... | collective-permute-start | bytes 6291464 | tf_op jit(solution)/shard_map/ppermute | solution.py:325
  157.7 68.5 %collective-permute-start.6 = (bf16[2,2,8,128,256]{4,3,2,1,0:T(8,128)(2,1)}, bf16[2,2,8,128,256]{4,3,2,1,0:T(8,128)(2,1)}, u32[]{:S(2)}, u32[]{:S(2)}) collective-permute-start(bf16[2,2,8,128,256]{4,3,2,1,0:T(8,128)(2,1)} %project.6.refs_2_), channel_id=1, source_target_pairs={{0,2},{1,3},{2,0},{3,1},{4,6},{5,7},{6,4},{7,5},{8,10},{9,11},{10,... | collective-permute-start | bytes 6291464 | tf_op jit(solution)/shard_map/ppermute | solution.py:325
  159.5 66.9 %collective-permute-start.7 = (bf16[2,2,8,128,256]{4,3,2,1,0:T(8,128)(2,1)}, bf16[2,2,8,128,256]{4,3,2,1,0:T(8,128)(2,1)}, u32[]{:S(2)}, u32[]{:S(2)}) collective-permute-start(bf16[2,2,8,128,256]{4,3,2,1,0:T(8,128)(2,1)} %project.6.refs_2_), channel_id=1, source_target_pairs={{0,4},{1,5},{2,6},{3,7},{4,0},{5,1},{6,2},{7,3},{8,12},{9,13},{10,... | collective-permute-start | bytes 6291464 | tf_op jit(solution)/shard_map/ppermute | solution.py:325
  161.1 68.1 %collective-permute-start.8 = (bf16[2,1,8,256,256]{4,3,2,1,0:T(8,128)(2,1)}, bf16[2,1,8,256,256]{4,3,2,1,0:T(8,128)(2,1)}, u32[]{:S(2)}, u32[]{:S(2)}) collective-permute-start(bf16[2,1,8,256,256]{4,3,2,1,0:T(8,128)(2,1)} %get-tuple-element.90.refs_4_), channel_id=1, source_target_pairs={{0,1},{1,0},{2,3},{3,2},{4,5},{5,4},{6,7},{7,6},{8,9},{9,8},{10,11... | collective-permute-start | bytes 6291464 | tf_op jit(solution)/shard_map/ppermute | solution.py:325
  184.7 85.2 %collective-permute-start.11 = (bf16[2,1,8,256,256]{4,3,2,1,0:T(8,128)(2,1)}, bf16[2,1,8,256,256]{4,3,2,1,0:T(8,128)(2,1)}, u32[]{:S(2)}, u32[]{:S(2)}) collective-permute-start(bf16[2,1,8,256,256]{4,3,2,1,0:T(8,128)(2,1)} %get-tuple-element.65.refs_4_), channel_id=1, source_target_pairs={{0,2},{1,3},{2,0},{3,1},{4,6},{5,7},{6,4},{7,5},{8,10},{9,11},{10,... | collective-permute-start | bytes 6291464 | tf_op jit(solution)/shard_map/ppermute | solution.py:325
  185.2 89.0 %collective-permute-start.10 = (bf16[2,2,8,128,256]{4,3,2,1,0:T(8,128)(2,1)S(1)}, bf16[2,2,8,128,256]{4,3,2,1,0:T(8,128)(2,1)}, u32[]{:S(2)}, u32[]{:S(2)}) collective-permute-start(bf16[2,2,8,128,256]{4,3,2,1,0:T(8,128)(2,1)S(1)} %collective-permute-done.refs_2_.refs_0_), channel_id=1, source_target_pairs={{0,4},{1,5},{2,6},{3,7},{4,0},{5,1},{6,2},{7,3},{8,12},{9,13},{10,... | collective-permute-start | bytes 6291464 | tf_op jit(solution)/shard_map/ppermute | solution.py:325
  226.2 51.2 %collective-permute-start.12 = (bf16[2,2,8,128,256]{4,3,2,1,0:T(8,128)(2,1)S(1)}, bf16[2,2,8,128,256]{4,3,2,1,0:T(8,128)(2,1)}, u32[]{:S(2)}, u32[]{:S(2)}) collective-permute-start(bf16[2,2,8,128,256]{4,3,2,1,0:T(8,128)(2,1)S(1)} %collective-permute-done.refs_2_.refs_0_), channel_id=1, source_target_pairs={{0,1},{1,0},{2,3},{3,2},{4,5},{5,4},{6,7},{7,6},{8,9},{9,8},{10,11... | collective-permute-start | bytes 6291464 | tf_op jit(solution)/shard_map/ppermute | solution.py:325
  226.4 47.0 %collective-permute-start.9 = (bf16[1,2,8,128,256]{4,3,2,1,0:T(8,128)(2,1)}, bf16[1,2,8,128,256]{4,3,2,1,0:T(8,128)(2,1)S(1)}, u32[]{:S(2)}, u32[]{:S(2)}) collective-permute-start(bf16[1,2,8,128,256]{4,3,2,1,0:T(8,128)(2,1)} %get-tuple-element.75), channel_id=1, source_target_pairs={{0,8},{1,9},{2,10},{3,11},{4,12},{5,13},{6,14},{7,15},{8,0},{9,1},... | collective-permute-start | bytes 3145736 | tf_op jit(solution)/shard_map/ppermute | solution.py:325
  229.1 48.3 %collective-permute-start.13 = (bf16[2,2,8,128,256]{4,3,2,1,0:T(8,128)(2,1)}, bf16[2,2,8,128,256]{4,3,2,1,0:T(8,128)(2,1)}, u32[]{:S(2)}, u32[]{:S(2)}) collective-permute-start(bf16[2,2,8,128,256]{4,3,2,1,0:T(8,128)(2,1)} %collective-permute-done.1.refs_4_.refs_0_), channel_id=1, source_target_pairs={{0,1},{1,0},{2,3},{3,2},{4,5},{5,4},{6,7},{7,6},{8,9},{9,8},{10,11... | collective-permute-start | bytes 6291464 | tf_op jit(solution)/shard_map/ppermute | solution.py:325
  273.3 5.4 %copy-start.3 = (bf16[1,2,8,128,256]{4,3,2,1,0:T(8,128)(2,1)}, bf16[1,2,8,128,256]{4,3,2,1,0:T(8,128)(2,1)S(1)}, u32[]{:S(2)}) copy-start(bf16[1,2,8,128,256]{4,3,2,1,0:T(8,128)(2,1)S(1)} %collective-permute-done.9.q_ref) | copy-start | bytes 3145732
  274.2 4.5 collective-permute-start.14
  274.2 49.6 %collective-permute-start.15 = (bf16[2,2,8,128,256]{4,3,2,1,0:T(8,128)(2,1)}, bf16[2,2,8,128,256]{4,3,2,1,0:T(8,128)(2,1)}, u32[]{:S(2)}, u32[]{:S(2)}) collective-permute-start(bf16[2,2,8,128,256]{4,3,2,1,0:T(8,128)(2,1)} %collective-permute-done.7.refs_4_), channel_id=1, source_target_pairs={{0,2},{1,3},{2,0},{3,1},{4,6},{5,7},{6,4},{7,5},{8,10},{9,11},{10,... | collective-permute-start | bytes 6291464 | tf_op jit(solution)/shard_map/ppermute | solution.py:325
  277.2 48.3 %collective-permute-start.18 = (bf16[2,2,8,128,256]{4,3,2,1,0:T(8,128)(2,1)}, bf16[2,2,8,128,256]{4,3,2,1,0:T(8,128)(2,1)}, u32[]{:S(2)}, u32[]{:S(2)}) collective-permute-start(bf16[2,2,8,128,256]{4,3,2,1,0:T(8,128)(2,1)} %collective-permute-done.7.refs_4_), channel_id=1, source_target_pairs={{0,1},{1,0},{2,3},{3,2},{4,5},{5,4},{6,7},{7,6},{8,9},{9,8},{10,11... | collective-permute-start | bytes 6291464 | tf_op jit(solution)/shard_map/ppermute | solution.py:325
  323.8 4.5 collective-permute-start.19
  323.8 99.7 %collective-permute-start.20 = (f32[2,8,136,256]{3,2,1,0:T(8,128)}, f32[2,8,136,256]{3,2,1,0:T(8,128)S(1)}, u32[]{:S(2)}, u32[]{:S(2)}) collective-permute-start(f32[2,8,136,256]{3,2,1,0:T(8,128)} %shard_map.57), channel_id=1, source_target_pairs={{0,8},{1,9},{2,10},{3,11},{4,12},{5,13},{6,14},{7,15},{8,0},{9,1},... | collective-permute-start | bytes 6684680 | tf_op jit(solution)/shard_map/ppermute | solution.py:325
  325.0 22.2 %collective-permute-start.17 = (bf16[2,1,8,256,256]{4,3,2,1,0:T(8,128)(2,1)}, bf16[2,1,8,256,256]{4,3,2,1,0:T(8,128)(2,1)}, u32[]{:S(2)}, u32[]{:S(2)}) collective-permute-start(bf16[2,1,8,256,256]{4,3,2,1,0:T(8,128)(2,1)} %collective-permute-done.11.refs_4_), channel_id=1, source_target_pairs={{0,1},{1,0},{2,3},{3,2},{4,5},{5,4},{6,7},{7,6},{8,9},{9,8},{10,11... | collective-permute-start | bytes 6291464 | tf_op jit(solution)/shard_map/ppermute | solution.py:325
  325.3 22.0 %collective-permute-start.16 = (bf16[2,2,8,128,256]{4,3,2,1,0:T(8,128)(2,1)}, bf16[2,2,8,128,256]{4,3,2,1,0:T(8,128)(2,1)}, u32[]{:S(2)}, u32[]{:S(2)}) collective-permute-start(bf16[2,2,8,128,256]{4,3,2,1,0:T(8,128)(2,1)} %collective-permute-done.6.refs_2_), channel_id=1, source_target_pairs={{0,1},{1,0},{2,3},{3,2},{4,5},{5,4},{6,7},{7,6},{8,9},{9,8},{10,11... | collective-permute-start | bytes 6291464 | tf_op jit(solution)/shard_map/ppermute | solution.py:325
  325.6 127.7 %collective-permute-start.21 = (bf16[2,1,8,256,256]{4,3,2,1,0:T(8,128)(2,1)}, bf16[2,1,8,256,256]{4,3,2,1,0:T(8,128)(2,1)}, u32[]{:S(2)}, u32[]{:S(2)}) collective-permute-start(bf16[2,1,8,256,256]{4,3,2,1,0:T(8,128)(2,1)} %get-tuple-element.90.refs_4_), channel_id=1, source_target_pairs={{0,2},{1,3},{2,0},{3,1},{4,6},{5,7},{6,4},{7,5},{8,10},{9,11},{10,... | collective-permute-start | bytes 6291464 | tf_op jit(solution)/shard_map/ppermute | solution.py:325
  423.5 1.3 copy-start.1
  453.2 16.2 %collective-permute-start.22 = (bf16[2,1,8,256,256]{4,3,2,1,0:T(8,128)(2,1)}, bf16[2,1,8,256,256]{4,3,2,1,0:T(8,128)(2,1)S(1)}, u32[]{:S(2)}, u32[]{:S(2)}) collective-permute-start(bf16[2,1,8,256,256]{4,3,2,1,0:T(8,128)(2,1)} %collective-permute-done.21.refs_4_), channel_id=1, source_target_pairs={{0,1},{1,0},{2,3},{3,2},{4,5},{5,4},{6,7},{7,6},{8,9},{9,8},{10,11... | collective-permute-start | bytes 6291464 | tf_op jit(solution)/shard_map/ppermute | solution.py:325
  469.4 1.4 copy-start.2

commit v2 on v0

v2 whole, which is shorter than its diff:
```python
import functools

import jax
import jax.numpy as jnp
from jax import lax
from jax.experimental import pallas as pl
from jax.experimental.pallas import tpu as pltpu
from jax.sharding import PartitionSpec as P


SLOT = (0, 4, 2, 6, 1, 5, 3, 7)
LOG2E = 1.4426950408889634
F32 = jnp.float32
BF16 = jnp.bfloat16
TILE = 256


def cost(flops, bytes_accessed, transcendentals=0):
    return pl.CostEstimate(flops=int(flops), bytes_accessed=int(bytes_accessed), transcendentals=int(transcendentals))


def swap_bits(head):
    return (head % 2) * 4 + (head // 2 % 2) * 2 + head // 4


def position(slot, own):
    if slot == own:
        return 0
    if slot // 2 == own // 2:
        return 1
    return 2 + slot % 2 if slot // 4 == own // 4 else 4 + slot % 4


def onehot(transposed=False):
    dims = (1, 0) if transposed else (0, 1)
    out_row = lax.broadcasted_iota(jnp.int32, (TILE, TILE), dims[0])
    in_row = lax.broadcasted_iota(jnp.int32, (TILE, TILE), dims[1])
    hit = in_row == (out_row % 32) * 8 + out_row // 32
    return jnp.where(hit, 1.0, 0.0).astype(BF16)


def split_kernel(n_sub, slots, *refs):
    take = onehot()
    half = len(refs) // 2
    for sub in range(n_sub):
        for a_ref, o_ref in zip(refs[:half], refs[half:]):
            rows = jnp.dot(take, a_ref[sub * TILE:(sub + 1) * TILE, :], preferred_element_type=F32).astype(BF16)
            for res in range(8):
                o_ref[slots[res], sub * 32:(sub + 1) * 32, :] = rows[res * 32:(res + 1) * 32]


def split_rows(arrays, n_sub, slots=tuple(range(8))):
    n_rows, width = arrays[0].shape
    blk = n_sub * TILE
    return pl.pallas_call(
        functools.partial(split_kernel, n_sub, slots),
        grid=(n_rows // blk,),
        in_specs=[pl.BlockSpec((blk, width), lambda i: (i, 0)) for _ in arrays],
        out_specs=[pl.BlockSpec((8, blk // 8, width), lambda i: (0, i, 0)) for _ in arrays],
        out_shape=[jax.ShapeDtypeStruct((8, n_rows // 8, width), BF16) for _ in arrays],
        cost_estimate=cost(2 * len(arrays) * n_rows * TILE * width, 4 * len(arrays) * n_rows * width),
        name="split_rows",
    )(*arrays)


def near_kernel(n_seqs, x_ref, *refs):
    w_refs, (e_ref, b_ref) = refs[:2], refs[2:]
    nb = x_ref.shape[0] // (2 * n_seqs)
    own = pl.program_id(0)
    for wi, w_ref in enumerate(w_refs):
        out = jnp.dot(x_ref[...], w_ref[0], preferred_element_type=F32).astype(BF16)
        for parity in range(2):
            @pl.when(own % 2 == parity)
            def _():
                for slot, o_ref in ((parity, e_ref), (1 - parity, b_ref)):
                    for seq in range(n_seqs):
                        at = (slot * n_seqs + seq) * nb
                        o_ref[wi, seq, 0] = out[at:at + nb]


def rest_kernel(n_seqs, x_ref, *refs):
    w_refs, g_refs, r_ref = refs[:2], refs[2:2 + n_seqs], refs[2 + n_seqs]
    rows = x_ref.shape[0] // 8
    nb = rows // n_seqs
    own = pl.program_id(0)
    pair = pl.ds(pl.multiple_of((own // 2 + 1 - 2 * (own // 2 % 2)) * 2 * rows, 2 * rows), 2 * rows)
    half = pl.ds(pl.multiple_of((1 - own // 4) * 4 * rows, 4 * rows), 4 * rows)
    for wi, w_ref in enumerate(w_refs):
        out = jnp.dot(x_ref[pair, :], w_ref[0], preferred_element_type=F32).astype(BF16)
        for slot in range(2):
            for seq in range(n_seqs):
                at = (slot * n_seqs + seq) * nb
                g_refs[seq][wi, 0, 0, slot * nb:(slot + 1) * nb, :] = out[at:at + nb]
        out = jnp.dot(x_ref[half, :], w_ref[0], preferred_element_type=F32).astype(BF16)
        for slot in range(4):
            for seq in range(n_seqs):
                at = (slot * n_seqs + seq) * nb
                r_ref[wi, seq, 0, slot * nb:(slot + 1) * nb, :] = out[at:at + nb]


def query_kernel(n_seqs, x_ref, w_ref, q_ref, *first_refs):
    rows = x_ref.shape[0] // 8
    nb = rows // n_seqs
    own = pl.program_id(0)
    out = jnp.dot(x_ref[...], w_ref[0], preferred_element_type=F32).astype(BF16)
    for slot in range(8):
        same_half = 1 - jnp.abs(slot // 4 - own // 4)
        same_pair = jnp.where(slot // 2 == own // 2, 1, 0)
        same = jnp.where(slot == own, 1, 0)
        pos = jnp.where(same == 1, 0, jnp.where(same_pair == 1, 1, jnp.where(same_half == 1, 2 + slot % 2, 4 + slot % 4)))
        for seq in range(n_seqs):
            at = (slot * n_seqs + seq) * nb
            q_ref[0, seq, 0, pl.ds(pl.multiple_of(pos * nb, nb), nb), :] = out[at:at + nb]
    for seq in range(n_seqs):
        first_refs[seq][0, 0, 0] = q_ref[0, seq, 0, :nb, :]


def project(kernel, xp, ws, n_seqs, outs, x_pair=False):
    n_heads, model_dim, head_dim = ws[0].shape
    rows = xp.shape[0]
    x_rows = rows // 4 if x_pair else rows
    out_rows = sum(n_w * seqs * n for n_w, seqs, n in outs)
    return pl.pallas_call(
        functools.partial(kernel, n_seqs),
        grid=(n_heads,),
        in_specs=[pl.BlockSpec((x_rows, model_dim), (lambda g: (g // 2, 0)) if x_pair else (lambda g: (0, 0)))]
        + [pl.BlockSpec((1, model_dim, head_dim), lambda g: (swap_bits(g), 0, 0)) for _ in ws],
        out_specs=[pl.BlockSpec((n_w, seqs, 1, n, head_dim), lambda g: (0, 0, swap_bits(g), 0, 0)) for n_w, seqs, n in outs],
        out_shape=[jax.ShapeDtypeStruct((n_w, seqs, n_heads, n, head_dim), BF16) for n_w, seqs, n in outs],
        cost_estimate=cost(2 * n_heads * out_rows * model_dim * head_dim, 2 * (xp.size + len(ws) * ws[0].size) + 2 * n_heads * out_rows * head_dim),
        name="project",
    )(xp, *ws)


def mult_of(group, key_group, level):
    return min(group, key_group) - level + 1


LOG2 = {1: 0.0, 2: 1.0, 3: 1.584962500721156, 4: 2.0}


def by_group(groups, key_group, level, log=False):
    mults = [mult_of(group, key_group, level) for group, _ in groups]
    if all(mult == 1 for mult in mults):
        return None
    values = [LOG2[mult] if log else float(mult) for mult in mults]
    n_cols = sum(cols for _, cols in groups)
    col = lax.broadcasted_iota(jnp.int32, (1, n_cols), 1)
    row, base = jnp.full((1, n_cols), values[-1], F32), n_cols
    for value, (_, cols) in list(zip(values, groups))[::-1]:
        row = jnp.where(col < base, value, row)
        base -= cols
    return row


def scores(keys, q):
    return lax.dot_general(keys, q, (((1,), (1,)), ((), ())), preferred_element_type=F32)


def fold(op, p):
    return op(p.reshape(p.shape[0] // 8, 8, p.shape[1]), axis=0)


def gather_keys(kv_refs, k_scr, v_scr):
    off = 0
    for ref in kv_refs:
        rows = ref.shape[3]
        k_scr[off:off + rows, :] = ref[0, 0, 0]
        v_scr[:, off:off + rows] = jnp.transpose(ref[1, 0, 0])
        off += rows


def run_branch0(q, k_scr, v_scr, segs, step, groups, s_scr, p_scr):
    scale = LOG2E * q.shape[1] ** -0.5
    peak = None
    for start in range(0, k_scr.shape[0], step):
        s = scores(k_scr[start:start + step, :], q)
        s_scr[start:start + step, :] = s
        top = fold(jnp.max, s)
        peak = top if peak is None else jnp.maximum(peak, top)
    shift = jnp.max(peak, axis=0, keepdims=True) * scale
    sums, start = [], 0
    for length, _ in segs:
        p = jnp.exp2(s_scr[start:start + length, :] * scale - shift)
        s_scr[start:start + length, :] = p
        sums.append(jnp.sum(fold(jnp.sum, p), axis=0, keepdims=True))
        start += length
    total = functools.reduce(jnp.add, sums)
    inverse = 1.0 / total
    weight, start = None, 0
    for (length, key_group), part in zip(segs, sums):
        mult = by_group(groups, key_group, 0)
        factor = inverse if mult is None else inverse * mult
        p_scr[start:start + length, :] = (s_scr[start:start + length, :] * factor).astype(BF16)
        weight = part * factor if weight is None else weight + part * factor
        start += length
    acc = jnp.dot(v_scr[...], p_scr[...], preferred_element_type=F32)
    return shift + jnp.log2(total), weight, acc


def level0_kernel(nb, q_ref, *refs):
    kv_refs, (o_ref, acc_ref, stat_ref, k_scr, v_scr, s_scr, p_scr, s_scr2, p_scr2) = refs[:8], refs[8:]
    gather_keys(kv_refs, k_scr, v_scr)
    segs = ((2 * nb, 3), (2 * nb, 2), (4 * nb, 1), (8 * nb, 0))
    groups = ((3, nb), (2, nb), (1, 2 * nb))
    shift, weight, acc = run_branch0(q_ref[0, 0, 0, :4 * nb, :], k_scr, v_scr, segs, 4 * nb, groups, s_scr, p_scr)
    acc_ref[0, 0] = acc
    stat_ref[0, 0, 0:1, :] = shift
    stat_ref[0, 0, 1:2, :] = weight
    _, _, acc = run_branch0(q_ref[0, 0, 0, 4 * nb:, :], k_scr, v_scr, segs, 4 * nb, ((0, 4 * nb),), s_scr2, p_scr2)
    o_ref[0, 0] = jnp.transpose(acc).astype(BF16)


def weights(s, shift, scale, segs, groups, level, p_scr):
    start, total = 0, None
    for length, key_group in segs:
        mult = by_group(groups, key_group, level, log=True)
        local = shift if mult is None else shift - mult
        p = jnp.exp2(s[start:start + length, :] * scale - local)
        p_scr[start:start + length, :] = p.astype(BF16)
        part = fold(jnp.sum, p)
        total = part if total is None else total + part
        start += length
    return jnp.sum(total, axis=0, keepdims=True)


def peak_of(s, scale):
    return jnp.max(fold(jnp.max, s), axis=0, keepdims=True) * scale


def upper(op, low, row):
    n_cols = low.shape[1]
    return jnp.concatenate([op(row[:, :n_cols], low), row[:, n_cols:]], axis=1)


def final_kernel(nb, q_ref, *refs):
    one_refs, two_refs, refs = refs[:6], refs[6:14], refs[14:]
    acc_in, stat_in, far_ref, o_ref, k_one, v_one, k_two, v_two, p_one, p_two = refs
    gather_keys(one_refs, k_one, v_one)
    gather_keys(two_refs, k_two, v_two)
    head_dim = q_ref.shape[4]
    scale = LOG2E * head_dim ** -0.5
    s_one = scores(k_one[...], q_ref[0, 0, 0])
    s_two = scores(k_two[...], q_ref[0, 0, 0, :2 * nb, :])
    shift_near, sum_near = stat_in[0, 0, 0:1, :], stat_in[0, 0, 1:2, :]
    shift_far, sum_far = far_ref[0, 0, head_dim:head_dim + 1, :], far_ref[0, 0, head_dim + 1:head_dim + 2, :]
    shift = jnp.maximum(shift_near, peak_of(s_one, scale))
    shift = upper(jnp.maximum, peak_of(s_two, scale), shift)
    shift = upper(jnp.maximum, shift_far, shift)
    low, mid, high = (3, nb), (2, nb), (1, 2 * nb)
    sum_one = weights(s_one, shift, scale, ((2 * nb, 3), (2 * nb, 2), (4 * nb, 1)), (low, mid, high), 1, p_one)
    sum_two = weights(s_two, shift[:, :2 * nb], scale, ((4 * nb, 3), (4 * nb, 2)), (low, mid), 2, p_two)
    near_scale = jnp.exp2(shift_near - shift)
    far_scale = jnp.exp2(shift_far - shift[:, :nb])
    total = upper(jnp.add, sum_far * far_scale, upper(jnp.add, sum_two, sum_near * near_scale + sum_one))
    inverse = 1.0 / total
    acc = acc_in[0, 0] * near_scale + jnp.dot(v_one[...], p_one[...], preferred_element_type=F32)
    acc_two = jnp.dot(v_two[...], p_two[...], preferred_element_type=F32)
    acc_two = upper(jnp.add, far_ref[0, 0, :head_dim, :] * far_scale, acc_two)
    acc = upper(jnp.add, acc_two, acc)
    o_ref[0, 0] = jnp.transpose(acc * inverse).astype(BF16)


def far_kernel(nb, q_ref, *refs):
    kv_refs, (far_ref, k_scr, v_scr, p_scr) = refs[:8], refs[8:]
    gather_keys(kv_refs, k_scr, v_scr)
    head_dim = q_ref.shape[4]
    scale = LOG2E * head_dim ** -0.5
    s = scores(k_scr[...], q_ref[0, 0, 0])
    shift = peak_of(s, scale)
    total = weights(s, shift, scale, ((8 * nb, 3),), ((3, nb),), 3, p_scr)
    far_ref[0, 0, :head_dim, :] = jnp.dot(v_scr[...], p_scr[...], preferred_element_type=F32)
    far_ref[0, 0, head_dim:, :] = jnp.concatenate([shift, total] + [jnp.zeros_like(shift)] * 6, axis=0)


def attend(body, nb, q, q_rows, kvs, states, outs, seq, scratch, pairs):
    n_heads, head_dim = q.shape[2], q.shape[4]
    n_keys = sum(kv.shape[3] for kv in kvs)

    def spec(n_here, *dims):
        base = seq if n_here > 1 else 0
        return pl.BlockSpec((1, 1, *dims), lambda h: (base, h, 0, 0))

    def lead_spec(lead, n_here, rows):
        base = seq if n_here > 1 else 0
        return pl.BlockSpec((lead, 1, 1, rows, head_dim), lambda h: (0, base, h, 0, 0))

    return pl.pallas_call(
        functools.partial(body, nb),
        grid=(n_heads,),
        in_specs=[lead_spec(1, q.shape[1], q_rows)]
        + [lead_spec(2, kv.shape[1], kv.shape[3]) for kv in kvs]
        + [spec(state.shape[0], *state.shape[2:]) for state in states],
        out_specs=[spec(1, rows, width) for rows, width, _ in outs],
        out_shape=[jax.ShapeDtypeStruct((1, n_heads, rows, width), dtype) for rows, width, dtype in outs],
        scratch_shapes=[pltpu.VMEM(dims, dtype) for dims, dtype in scratch],
        cost_estimate=cost(4 * n_heads * pairs * head_dim, 2 * n_heads * head_dim * (q_rows + 2 * n_keys), n_heads * pairs),
    )(q, *kvs, *states)


def out_kernel(nb, o_low, o_high, w_ref, *refs):
    y_ref, mix, lhs = refs[-3:]
    n_tok = lhs.shape[0]

    @pl.when(pl.program_id(0) == 0)
    def _():
        back = onehot(transposed=True)
        for sub in range(n_tok // TILE):
            for res in range(8):
                for head in range(8):
                    pos = position(SLOT[res], SLOT[head])
                    ref, base = (o_low, 0) if pos < 4 else (o_high, 4)
                    first = (pos - base) * nb + sub * 32
                    piece = ref[0, head, first:first + 32, :]
                    mix[res * 32:(res + 1) * 32, head * piece.shape[1]:(head + 1) * piece.shape[1]] = piece
            lhs[sub * TILE:(sub + 1) * TILE, :] = jnp.dot(back, mix[...], preferred_element_type=F32).astype(BF16)

    y_ref[0] = jnp.dot(lhs[...], w_ref[...], preferred_element_type=F32).astype(BF16)


def out_project(o_low, o_high, w, nb, seq, n_seqs, y_prev):
    width, model_dim = w.shape
    n_tok = nb * 8
    n_cols = min(512, model_dim)
    in_specs = [pl.BlockSpec(a.shape, lambda i: (0, 0, 0, 0)) for a in (o_low, o_high)] + [pl.BlockSpec((width, n_cols), lambda i: (0, i))]
    more = () if y_prev is None else (y_prev,)
    return pl.pallas_call(
        functools.partial(out_kernel, nb),
        grid=(model_dim // n_cols,),
        in_specs=in_specs + [pl.BlockSpec(memory_space=pl.ANY) for _ in more],
        out_specs=pl.BlockSpec((1, n_tok, n_cols), lambda i: (seq, 0, i)),
        out_shape=jax.ShapeDtypeStruct((n_seqs, n_tok, model_dim), BF16),
        scratch_shapes=[pltpu.VMEM((TILE, width), BF16), pltpu.VMEM((n_tok, width), BF16)],
        input_output_aliases={3: 0} if more else {},
        cost_estimate=cost(2 * n_tok * width * model_dim, 4 * n_tok * width + 2 * w.size),
        name="out_project",
    )(o_low, o_high, w, *more)


def solution(mesh):
    n_dev = mesh.shape['sp']

    def swap(a, bit):
        return lax.ppermute(a, 'sp', [(d, d ^ bit) for d in range(n_dev)])

    def local_step(x_loc, w_q, w_k, w_v, w_o):
        n_seqs, n_tok, model_dim = x_loc.shape
        n_heads, head_dim = w_q.shape[1], w_q.shape[2]
        nb = n_tok // 8
        n_rows = n_seqs * n_tok
        after = lax.optimization_barrier

        def per_head(*ws):
            rows = [w.reshape(model_dim * n_heads, head_dim) for w in ws]
            return split_rows(rows, 8 if rows[0].shape[0] % (8 * TILE) == 0 else 1)

        xp, = split_rows((x_loc.reshape(n_rows, model_dim),), 1, SLOT)
        xp = xp.reshape(n_rows, model_dim)
        wk, wv = per_head(w_k, w_v)

        e, b = project(near_kernel, xp, (wk, wv), n_seqs, ((2, n_seqs, nb), (2, n_seqs, nb)), x_pair=True)
        wk, wv, e, b = after((wk, wv, e, b))
        y_e, z_e, c_e = swap(e, 2), swap(e, 4), swap(e, 1)
        y_b, z_b, c_b = swap(b, 2), swap(b, 4), swap(b, 1)
        *g, r = project(rest_kernel, xp, (wk, wv), n_seqs, ((2, 1, 2 * nb),) * n_seqs + ((2, n_seqs, 4 * nb),))
        w_q, g, r = after((w_q, g, r))
        y_g = [swap(g[0], 2)]
        c_g = [swap(g[0], 1), swap(g[1], 1)]
        c_r = swap(r, 1)
        wq, = per_head(w_q)
        q_all, *q_first = project(query_kernel, xp, (wq,), n_seqs, ((1, n_seqs, 8 * nb),) + ((1, 1, nb),) * n_seqs)

        q_all, q_first, y_e, z_e = after((q_all, q_first, y_e, z_e))
        zy_e, yc_e, zc_e = swap(y_e, 4), swap(y_e, 1), swap(z_e, 1)
        q_far = [swap(q_first[seq], 8) for seq in range(n_seqs)]

        def level0(seq, q):
            kvs = (e, c_e, b, c_b, g[seq], c_g[seq], r, c_r)
            keys = 16 * nb
            scratch = [((keys, head_dim), BF16), ((head_dim, keys), BF16)] + [((keys, 4 * nb), F32), ((keys, 4 * nb), BF16)] * 2
            return attend(level0_kernel, nb, q, 8 * nb, kvs, (),
                          ((4 * nb, head_dim, BF16), (head_dim, 4 * nb, F32), (8, 4 * nb, F32)), seq, scratch, 8 * nb * keys)

        near0 = level0(0, q_all)
        near0, q_all, y_b, z_b, g1 = after((near0, q_all, y_b, z_b, g[1]))
        zy_b, yc_b, zc_b = swap(z_b, 2), swap(y_b, 1), swap(z_b, 1)
        y_g.append(swap(g1, 2))
        near1 = level0(1, q_all)
        near1, q_all, q_far, zy_e, y_g[0] = after((near1, q_all, q_far, zy_e, y_g[0]))
        near = (near0, near1)
        zyc_e = swap(zy_e, 1)
        yc_g = [swap(y_g[0], 1)]
        far_in = []
        for seq in range(n_seqs):
            kvs = (e, c_e, y_e, yc_e, z_e, zc_e, zy_e, zyc_e)
            scratch = [((8 * nb, head_dim), BF16), ((head_dim, 8 * nb), BF16), ((8 * nb, nb), BF16)]
            far, = attend(far_kernel, nb, q_far[seq], nb, kvs, (), ((head_dim + 8, nb, F32),), seq, scratch, 8 * nb * nb)
            far_in.append(swap(far, 8))
        far, q_all, zy_b = after((far, q_all, zy_b))
        zyc_b = swap(zy_b, 1)
        y = None
        w_out = w_o.reshape(n_heads * head_dim, model_dim)
        for seq in range(n_seqs):
            o_high, acc, stat = near[seq]
            kvs = (y_e, yc_e, y_b, yc_b, y_g[seq], yc_g[seq], z_e, zc_e, zy_e, zyc_e, z_b, zc_b, zy_b, zyc_b)
            scratch = [((8 * nb, head_dim), BF16), ((head_dim, 8 * nb), BF16)] * 2 + [((8 * nb, 4 * nb), BF16), ((8 * nb, 2 * nb), BF16)]
            o_low, = attend(final_kernel, nb, q_all, 4 * nb, kvs, (acc, stat, far_in[seq]), ((4 * nb, head_dim, BF16),), seq,
                            scratch, 8 * nb * 6 * nb)
            if seq == 0:
                o_low, y_g[1] = after((o_low, y_g[1]))
                yc_g.append(swap(y_g[1], 1))
            y = out_project(o_low, o_high, w_out, nb, seq, n_seqs, y)
        return y

    return jax.shard_map(local_step, mesh=mesh, in_specs=(P('dp', 'sp', None), P(), P(), P(), P()), out_specs=P('dp', 'sp', None), check_vma=False)
```

time: 1690 us -> 475 us (0.28)
  local copies, waits for them, and re-layouts: 543 us -> 1.4 us
  matrix products: 450 us -> 0 us
  Pallas kernels: 0 us -> 280 us
  other arithmetic: 245 us -> 0 us
  waiting for transfers between devices: 368 us -> 175 us
  loops' own time: 54.8 us -> 0 us
    dot_general x64 -> x0, matrix products: 450 us -> none  [the longest x30 193 us: one_block(): jnp.einsum('qhd,khd->hqk', q_tile, k_seg, preferred_element_type=jnp.floa...]
    pallas_call x0 -> x14, Pallas kernels: none -> 280 us  [the longest x6 133 us: attend(): pl.pallas_call(functools.partial(body, nb), grid=(n_heads,), in_specs=[le...]
    ppermute x20 -> x25, waiting for transfers between devices: 368 us -> 175 us  [swap(): return lax.ppermute(a, 'sp', [(d, d ^ bit) for d in range(n_dev)])]
    concatenate x18 -> x0, other arithmetic: 144 us -> none  [the longest x9 73.6 us: gather_group(): v_part = jnp.concatenate([v_part, v_peer], axis=1)]
    unnamed x122 -> x12, local copies, waits for them, and re-layouts: 134 us -> 1.4 us
    another operation x14 -> x0, local copies, waits for them, and re-layouts: 97.8 us -> none  [the longest x6 86.6 us: pick_rows(): values.reshape(n_seqs, n_rows // dilation, dilation, n_heads // dilation,...]
    mul x14 -> x0, local copies, waits for them, and re-layouts: 90.9 us -> none  [spread_rows(): o_sp.reshape(n_seqs, n_rows, 1, n_heads // dilation, dilation, head_dim)]
    slice x9 -> x0, local copies, waits for them, and re-layouts: 60.4 us -> none  [pick_rows(): split_view[:, :, phase_idx, :, phase_idx, :]]
  transfers between devices with their start and end apart: 20 -> 25, of which waited for: 4 -> 7; matrix products, arithmetic and copies ran while one was open for 63% -> 0% of each run, Pallas kernels for 0% -> 35%
where the time goes in v2:
time: 475 us; the launch traced here: 474 us
  Pallas kernels  280 us (59%)
  waiting for transfers between devices  175 us (37%)
  starting transfers between devices  16.8 us (4%)
    ppermute x25, waiting for transfers between devices, swap(): return lax.ppermute(a, 'sp', [(d, d ^ bit) for d in range(n_dev)])  175 us
    pallas_call x6, Pallas kernels, attend(): pl.pallas_call(functools.partial(body, nb), grid=(n_heads,), in_specs=[le...  133 us
    pallas_call x3, Pallas kernels, project(): pl.pallas_call(functools.partial(kernel, n_seqs), grid=(n_heads,), in_spe...  81.1 us
    pallas_call x3, Pallas kernels, split_rows(): pl.pallas_call(functools.partial(split_kernel, n_sub, slots), grid=(n_row...  37.2 us
    pallas_call x2, Pallas kernels, out_project(): pl.pallas_call(functools.partial(out_kernel, nb), grid=(model_dim // n_co...  29 us
    ppermute x25, starting transfers between devices, swap(): return lax.ppermute(a, 'sp', [(d, d ^ bit) for d in range(n_dev)])  16.8 us
  transfers between devices with their start and end apart: 25, of which 7 were waited for; matrix products, arithmetic and copies ran while one was open for 0% of the time, Pallas kernels for 35%

profile of v2, /device:TPU:0, one launch (start us, length us, event | category | flops | bytes accessed | tf_op | source)
XLA Modules:
  0.0 473.5 jit_solution(13404051057168070364)
XLA Ops:
  0.0 10.4 %split_rows.3 = bf16[8,256,2048]{2,1,0:T(8,128)(2,1)} custom-call(bf16[2048,2048]{1,0:T(8,128)(2,1)} %bitcast.6), custom_call_target="tpu_custom_call" | custom-call | flops 2147483648 | bytes 16777216 | tf_op jit(solution)/shard_map/split_rows/pallas_call | solution.py:55
  10.4 15.7 %split_rows.4 = (bf16[8,2048,256]{2,1,0:T(8,128)(2,1)}, bf16[8,2048,256]{2,1,0:T(8,128)(2,1)}) custom-call(bf16[16384,256]{1,0:T(8,128)(2,1)} %bitcast.7, bf16[16384,256]{1,0:T(8,128)(2,1)} %bitcast.8), custom_call_target="tpu_custom_call" | custom-call | flops 4294967296 | bytes 33554432 | tf_op jit(solution)/shard_map/split_rows/pallas_call | solution.py:55
  26.1 23.6 %project.3 = (bf16[2,2,8,128,256]{4,3,2,1,0:T(8,128)(2,1)}, bf16[2,2,8,128,256]{4,3,2,1,0:T(8,128)(2,1)}) custom-call(bf16[2048,2048]{1,0:T(8,128)(2,1)} %bitcast.10, bf16[8,2048,256]{2,1,0:T(8,128)(2,1)} %get-tuple-element.57.refs_0_, bf16[8,2048,256]{2,1,0:T(8,128)(2,1)} %get-tuple-element.58.refs_1_), custom_call_target="tpu_custom_call" | custom-call | flops 8589934592 | bytes 29360128 | tf_op jit(solution)/shard_map/project/pallas_call | solution.py:123
  49.6 33.1 %project.4 = (bf16[2,1,8,256,256]{4,3,2,1,0:T(8,128)(2,1)}, bf16[2,1,8,256,256]{4,3,2,1,0:T(8,128)(2,1)}, bf16[2,2,8,512,256]{4,3,2,1,0:T(8,128)(2,1)}) custom-call(bf16[2048,2048]{1,0:T(8,128)(2,1)} %bitcast.11, bf16[8,2048,256]{2,1,0:T(8,128)(2,1)} %get-tuple-element.57.refs_0_, bf16[8,2048,256]{2,1,0:T(8,128)(2,1)} %get-tuple-element.58.refs_1_), custom_call_target="tpu_custom_call" | custom-call | flops 25769803776 | bytes 37748736 | tf_op jit(solution)/shard_map/project/pallas_call | solution.py:123
  82.7 0.5 collective-permute-start.5
  83.2 2.5 collective-permute-start
  85.7 1.6 collective-permute-start.1
  87.3 0.0 collective-permute-start.4
  87.3 0.5 collective-permute-start.2
  87.8 44.4 %collective-permute-done.refs_2_.refs_0_ = bf16[2,2,8,128,256]{4,3,2,1,0:T(8,128)(2,1)S(1)} collective-permute-done((bf16[2,2,8,128,256]{4,3,2,1,0:T(8,128)(2,1)}, bf16[2,2,8,128,256]{4,3,2,1,0:T(8,128)(2,1)S(1)}, u32[]{:S(2)}, u32[]{:S(2)}) %collective-permute-start) | collective-permute-done | bytes 2097184 | tf_op jit(solution)/shard_map/ppermute | solution.py:344
  132.2 0.0 collective-permute-start.3
  132.3 11.1 %split_rows.5.w_ref = bf16[8,2048,256]{2,1,0:T(8,128)(2,1)} custom-call(bf16[16384,256]{1,0:T(8,128)(2,1)} %bitcast.9), custom_call_target="tpu_custom_call" | custom-call | flops 2147483648 | bytes 16777216 | tf_op jit(solution)/shard_map/split_rows/pallas_call | solution.py:55
  143.4 0.0 collective-permute-done.1.refs_4_.refs_6_
  143.4 1.7 collective-permute-start.6
  145.1 0.0 collective-permute-done.4.refs_5_
  145.1 1.6 collective-permute-start.7
  146.7 0.0 collective-permute-done.2.refs_1_
  146.7 0.0 collective-permute-start.8
  146.7 24.5 %project.5 = (bf16[1,2,8,1024,256]{4,3,2,1,0:T(8,128)(2,1)}, bf16[1,1,8,128,256]{4,3,2,1,0:T(8,128)(2,1)}, bf16[1,1,8,128,256]{4,3,2,1,0:T(8,128)(2,1)}) custom-call(bf16[2048,2048]{1,0:T(8,128)(2,1)} %bitcast.12, bf16[8,2048,256]{2,1,0:T(8,128)(2,1)} %split_rows.5.w_ref), custom_call_target="tpu_custom_call" | custom-call | flops 19327352832 | bytes 26214400 | tf_op jit(solution)/shard_map/project/pallas_call | solution.py:123
  171.2 0.0 collective-permute-done.3.refs_3_
  171.2 0.5 collective-permute-start.12
  171.8 0.0 collective-permute-done.5.refs_7_
  171.8 0.2 collective-permute-start.11
  172.0 37.2 %shard_map.55 = (bf16[1,8,512,256]{3,2,1,0:T(8,128)(2,1)}, f32[1,8,256,512]{3,2,1,0:T(8,128)}, f32[1,8,8,512]{3,2,1,0:T(8,128)}) custom-call(bf16[1,2,8,1024,256]{4,3,2,1,0:T(8,128)(2,1)} %get-tuple-element.87.q_ref, bf16[2,2,8,128,256]{4,3,2,1,0:T(8,128)(2,1)} %get-tuple-element.66.refs_0_, bf16[2,2,8,128,256]{4,3,2,1,0:T(8,128)(2,1)} %collective-permute-done.2.refs_1_, ...), custom_call_target="tpu_custom_call" | custom-call | flops 17179869184 | bytes 20971520 | tf_op jit(solution)/shard_map/pallas_call | solution.py:288
  209.2 0.0 collective-permute-done.6.refs_2_
  209.3 0.1 collective-permute-start.13
  209.4 0.0 collective-permute-done.7.refs_10_
  209.4 2.8 collective-permute-start.10
  212.2 0.0 collective-permute-done.8.refs_5_
  212.2 0.2 collective-permute-start.9
  212.3 37.1 %shard_map.56 = (bf16[1,8,512,256]{3,2,1,0:T(8,128)(2,1)}, f32[1,8,256,512]{3,2,1,0:T(8,128)}, f32[1,8,8,512]{3,2,1,0:T(8,128)}) custom-call(bf16[1,2,8,1024,256]{4,3,2,1,0:T(8,128)(2,1)} %get-tuple-element.87.q_ref, bf16[2,2,8,128,256]{4,3,2,1,0:T(8,128)(2,1)} %get-tuple-element.66.refs_0_, bf16[2,2,8,128,256]{4,3,2,1,0:T(8,128)(2,1)} %collective-permute-done.2.refs_1_, ...), custom_call_target="tpu_custom_call" | custom-call | flops 17179869184 | bytes 20971520 | tf_op jit(solution)/shard_map/pallas_call | solution.py:288
  249.4 0.0 collective-permute-done.12.refs_4_
  249.4 0.1 collective-permute-start.14
  249.5 0.0 collective-permute-done.10.q_ref
  249.5 9.4 %collective-permute-done.9.q_ref = bf16[1,1,8,128,256]{4,3,2,1,0:T(8,128)(2,1)S(1)} collective-permute-done((bf16[1,1,8,128,256]{4,3,2,1,0:T(8,128)(2,1)}, bf16[1,1,8,128,256]{4,3,2,1,0:T(8,128)(2,1)S(1)}, u32[]{:S(2)}, u32[]{:S(2)}) %collective-permute-start.9) | collective-permute-done | bytes 524320 | tf_op jit(solution)/shard_map/ppermute | solution.py:344
  259.0 0.9 collective-permute-done.11.refs_6_.refs_8_
  259.9 0.0 collective-permute-start.15
  259.9 0.5 collective-permute-start.16
  260.4 0.2 collective-permute-start.18
  260.6 0.0 collective-permute-done.13.refs_3_.refs_1_
  260.6 0.3 collective-permute-start.19
  260.9 0.0 collective-permute-done.14.refs_5_.refs_7_
  260.9 0.2 collective-permute-start.17
  261.2 3.2 collective-permute-done.15.refs_7_.refs_9_
  264.4 10.6 %shard_map.57 = f32[1,8,264,128]{3,2,1,0:T(8,128)} custom-call(bf16[1,1,8,128,256]{4,3,2,1,0:T(8,128)(2,1)} %copy-done.5, bf16[2,2,8,128,256]{4,3,2,1,0:T(8,128)(2,1)} %get-tuple-element.66.refs_0_, bf16[2,2,8,128,256]{4,3,2,1,0:T(8,128)(2,1)} %collective-permute-done.2.refs_1_, bf16[2,2,8,128,256]{4,3,2,1,0:T(8,128)(2,1)} %copy-done, ...), custom_call_target="tpu_custom_call" | custom-call | flops 1073741824 | bytes 8912896 | tf_op jit(solution)/shard_map/pallas_call | solution.py:288
  275.0 33.2 %collective-permute-done.16.refs_12_ = bf16[2,2,8,128,256]{4,3,2,1,0:T(8,128)(2,1)} collective-permute-done((bf16[2,2,8,128,256]{4,3,2,1,0:T(8,128)(2,1)}, bf16[2,2,8,128,256]{4,3,2,1,0:T(8,128)(2,1)}, u32[]{:S(2)}, u32[]{:S(2)}) %collective-permute-start.16) | collective-permute-done | bytes 2097184 | tf_op jit(solution)/shard_map/ppermute | solution.py:344
  308.2 0.0 collective-permute-start.20
  308.2 0.5 collective-permute-start.22
  308.8 10.6 %shard_map.58 = f32[1,8,264,128]{3,2,1,0:T(8,128)} custom-call(bf16[1,1,8,128,256]{4,3,2,1,0:T(8,128)(2,1)} %copy-done.4, bf16[2,2,8,128,256]{4,3,2,1,0:T(8,128)(2,1)} %get-tuple-element.66.refs_0_, bf16[2,2,8,128,256]{4,3,2,1,0:T(8,128)(2,1)} %collective-permute-done.2.refs_1_, bf16[2,2,8,128,256]{4,3,2,1,0:T(8,128)(2,1)} %copy-done, ...), custom_call_target="tpu_custom_call" | custom-call | flops 1073741824 | bytes 8912896 | tf_op jit(solution)/shard_map/pallas_call | solution.py:288
  319.4 2.5 collective-permute-start.21
  321.9 0.0 collective-permute-done.17.refs_3_
  321.9 0.0 collective-permute-done.19.refs_11_
  321.9 47.9 %collective-permute-done.21.refs_16_ = f32[1,8,264,128]{3,2,1,0:T(8,128)} collective-permute-done((f32[1,8,264,128]{3,2,1,0:T(8,128)}, f32[1,8,264,128]{3,2,1,0:T(8,128)}, u32[]{:S(2)}, u32[]{:S(2)}) %collective-permute-start.21) | collective-permute-done | bytes 1081376 | tf_op jit(solution)/shard_map/ppermute | solution.py:344
  369.8 0.0 collective-permute-done.20.refs_13_
  369.8 18.8 %shard_map.59.o_low = bf16[1,8,512,256]{3,2,1,0:T(8,128)(2,1)} custom-call(bf16[1,2,8,1024,256]{4,3,2,1,0:T(8,128)(2,1)} %get-tuple-element.87.q_ref, bf16[2,2,8,128,256]{4,3,2,1,0:T(8,128)(2,1)} %copy-done, bf16[2,2,8,128,256]{4,3,2,1,0:T(8,128)(2,1)} %collective-permute-done.13.refs_3_.refs_1_, ...), custom_call_target="tpu_custom_call" | custom-call | flops 6442450944 | bytes 18874368 | tf_op jit(solution)/shard_map/pallas_call | solution.py:288
  388.6 0.0 collective-permute-done.22.refs_4_
  388.6 0.1 collective-permute-start.23
  388.6 0.1 collective-permute-start.24
  388.7 14.5 %out_project.2.refs_0_ = bf16[2,1024,2048]{2,1,0:T(8,128)(2,1)} custom-call(bf16[1,8,512,256]{3,2,1,0:T(8,128)(2,1)} %shard_map.59.o_low, bf16[1,8,512,256]{3,2,1,0:T(8,128)(2,1)} %get-tuple-element.100.o_high, bf16[2048,2048]{1,0:T(8,128)(2,1)} %bitcast.13), custom_call_target="tpu_custom_call" | custom-call | flops 8589934592 | bytes 16777216 | tf_op jit(solution)/shard_map/out_project/pallas_call | solution.py:327
  403.2 35.9 %collective-permute-done.24.refs_16_ = f32[1,8,264,128]{3,2,1,0:T(8,128)} collective-permute-done((f32[1,8,264,128]{3,2,1,0:T(8,128)S(1)}, f32[1,8,264,128]{3,2,1,0:T(8,128)}, u32[]{:S(2)}, u32[]{:S(2)}) %collective-permute-start.24) | collective-permute-done | bytes 1081376 | tf_op jit(solution)/shard_map/ppermute | solution.py:344
  439.1 0.0 collective-permute-done.23.refs_5_
  439.1 1.4 copy-done.2
  440.5 18.6 %shard_map.60.o_low = bf16[1,8,512,256]{3,2,1,0:T(8,128)(2,1)} custom-call(bf16[1,2,8,1024,256]{4,3,2,1,0:T(8,128)(2,1)} %get-tuple-element.87.q_ref, bf16[2,2,8,128,256]{4,3,2,1,0:T(8,128)(2,1)} %copy-done, bf16[2,2,8,128,256]{4,3,2,1,0:T(8,128)(2,1)} %collective-permute-done.13.refs_3_.refs_1_, ...), custom_call_target="tpu_custom_call" | custom-call | flops 6442450944 | bytes 18874368 | tf_op jit(solution)/shard_map/pallas_call | solution.py:288
  459.0 14.5 %out_project.3 = bf16[2,1024,2048]{2,1,0:T(8,128)(2,1)} custom-call(bf16[1,8,512,256]{3,2,1,0:T(8,128)(2,1)} %shard_map.60.o_low, bf16[1,8,512,256]{3,2,1,0:T(8,128)(2,1)} %get-tuple-element.98.o_high, bf16[2048,2048]{1,0:T(8,128)(2,1)} %bitcast.14, bf16[2,1024,2048]{2,1,0:T(8,128)(2,1)} %out_project.2.refs_0_), custom_call_target="tpu_custom_call", output_to_operand_aliasing={{}: (3, {})} | custom-call | flops 8589934592 | bytes 16777216 | tf_op jit(solution)/shard_map/out_project/pallas_call | solution.py:327
  (12 shorter events, 0.0 us)
Async XLA Ops:
  82.7 89.1 %collective-permute-start.5 = (bf16[2,2,8,512,256]{4,3,2,1,0:T(8,128)(2,1)}, bf16[2,2,8,512,256]{4,3,2,1,0:T(8,128)(2,1)}, u32[]{:S(2)}, u32[]{:S(2)}) collective-permute-start(bf16[2,2,8,512,256]{4,3,2,1,0:T(8,128)(2,1)} %get-tuple-element.70.refs_6_), channel_id=1, source_target_pairs={{0,1},{1,0},{2,3},{3,2},{4,5},{5,4},{6,7},{7,6},{8,9},{9,8},{10,11... | collective-permute-start | bytes 25165832 | tf_op jit(solution)/shard_map/ppermute | solution.py:344
  83.2 49.0 %collective-permute-start = (bf16[2,2,8,128,256]{4,3,2,1,0:T(8,128)(2,1)}, bf16[2,2,8,128,256]{4,3,2,1,0:T(8,128)(2,1)S(1)}, u32[]{:S(2)}, u32[]{:S(2)}) collective-permute-start(bf16[2,2,8,128,256]{4,3,2,1,0:T(8,128)(2,1)} %get-tuple-element.66.refs_0_), channel_id=1, source_target_pairs={{0,2},{1,3},{2,0},{3,1},{4,6},{5,7},{6,4},{7,5},{8,10},{9,11},{10,... | collective-permute-start | bytes 6291464 | tf_op jit(solution)/shard_map/ppermute | solution.py:344
  85.7 57.7 %collective-permute-start.1 = (bf16[2,2,8,128,256]{4,3,2,1,0:T(8,128)(2,1)}, bf16[2,2,8,128,256]{4,3,2,1,0:T(8,128)(2,1)}, u32[]{:S(2)}, u32[]{:S(2)}) collective-permute-start(bf16[2,2,8,128,256]{4,3,2,1,0:T(8,128)(2,1)} %get-tuple-element.66.refs_0_), channel_id=1, source_target_pairs={{0,4},{1,5},{2,6},{3,7},{4,0},{5,1},{6,2},{7,3},{8,12},{9,13},{10,... | collective-permute-start | bytes 6291464 | tf_op jit(solution)/shard_map/ppermute | solution.py:344
  87.3 57.8 %collective-permute-start.4 = (bf16[2,1,8,256,256]{4,3,2,1,0:T(8,128)(2,1)}, bf16[2,1,8,256,256]{4,3,2,1,0:T(8,128)(2,1)}, u32[]{:S(2)}, u32[]{:S(2)}) collective-permute-start(bf16[2,1,8,256,256]{4,3,2,1,0:T(8,128)(2,1)} %get-tuple-element.69.refs_4_), channel_id=1, source_target_pairs={{0,1},{1,0},{2,3},{3,2},{4,5},{5,4},{6,7},{7,6},{8,9},{9,8},{10,11... | collective-permute-start | bytes 6291464 | tf_op jit(solution)/shard_map/ppermute | solution.py:344
  87.3 59.4 %collective-permute-start.2 = (bf16[2,2,8,128,256]{4,3,2,1,0:T(8,128)(2,1)}, bf16[2,2,8,128,256]{4,3,2,1,0:T(8,128)(2,1)}, u32[]{:S(2)}, u32[]{:S(2)}) collective-permute-start(bf16[2,2,8,128,256]{4,3,2,1,0:T(8,128)(2,1)} %get-tuple-element.66.refs_0_), channel_id=1, source_target_pairs={{0,1},{1,0},{2,3},{3,2},{4,5},{5,4},{6,7},{7,6},{8,9},{9,8},{10,11... | collective-permute-start | bytes 6291464 | tf_op jit(solution)/shard_map/ppermute | solution.py:344
  132.2 77.0 %copy-start = (bf16[2,2,8,128,256]{4,3,2,1,0:T(8,128)(2,1)}, bf16[2,2,8,128,256]{4,3,2,1,0:T(8,128)(2,1)S(1)}, u32[]{:S(2)}) copy-start(bf16[2,2,8,128,256]{4,3,2,1,0:T(8,128)(2,1)S(1)} %collective-permute-done.refs_2_.refs_0_) | copy-start | bytes 6291460
  132.2 39.0 %collective-permute-start.3 = (bf16[2,2,8,128,256]{4,3,2,1,0:T(8,128)(2,1)}, bf16[2,2,8,128,256]{4,3,2,1,0:T(8,128)(2,1)}, u32[]{:S(2)}, u32[]{:S(2)}) collective-permute-start(bf16[2,2,8,128,256]{4,3,2,1,0:T(8,128)(2,1)} %get-tuple-element.68.refs_2_), channel_id=1, source_target_pairs={{0,1},{1,0},{2,3},{3,2},{4,5},{5,4},{6,7},{7,6},{8,9},{9,8},{10,11... | collective-permute-start | bytes 6291464 | tf_op jit(solution)/shard_map/ppermute | solution.py:344
  143.4 65.8 %collective-permute-start.6 = (bf16[2,2,8,128,256]{4,3,2,1,0:T(8,128)(2,1)}, bf16[2,2,8,128,256]{4,3,2,1,0:T(8,128)(2,1)}, u32[]{:S(2)}, u32[]{:S(2)}) collective-permute-start(bf16[2,2,8,128,256]{4,3,2,1,0:T(8,128)(2,1)} %get-tuple-element.68.refs_2_), channel_id=1, source_target_pairs={{0,2},{1,3},{2,0},{3,1},{4,6},{5,7},{6,4},{7,5},{8,10},{9,11},{10,... | collective-permute-start | bytes 6291464 | tf_op jit(solution)/shard_map/ppermute | solution.py:344
  145.1 64.2 %collective-permute-start.7 = (bf16[2,2,8,128,256]{4,3,2,1,0:T(8,128)(2,1)}, bf16[2,2,8,128,256]{4,3,2,1,0:T(8,128)(2,1)}, u32[]{:S(2)}, u32[]{:S(2)}) collective-permute-start(bf16[2,2,8,128,256]{4,3,2,1,0:T(8,128)(2,1)} %get-tuple-element.68.refs_2_), channel_id=1, source_target_pairs={{0,4},{1,5},{2,6},{3,7},{4,0},{5,1},{6,2},{7,3},{8,12},{9,13},{10,... | collective-permute-start | bytes 6291464 | tf_op jit(solution)/shard_map/ppermute | solution.py:344
  146.7 65.4 %collective-permute-start.8 = (bf16[2,1,8,256,256]{4,3,2,1,0:T(8,128)(2,1)}, bf16[2,1,8,256,256]{4,3,2,1,0:T(8,128)(2,1)}, u32[]{:S(2)}, u32[]{:S(2)}) collective-permute-start(bf16[2,1,8,256,256]{4,3,2,1,0:T(8,128)(2,1)} %get-tuple-element.94.refs_4_), channel_id=1, source_target_pairs={{0,1},{1,0},{2,3},{3,2},{4,5},{5,4},{6,7},{7,6},{8,9},{9,8},{10,11... | collective-permute-start | bytes 6291464 | tf_op jit(solution)/shard_map/ppermute | solution.py:344
  171.2 78.2 %collective-permute-start.12 = (bf16[2,1,8,256,256]{4,3,2,1,0:T(8,128)(2,1)}, bf16[2,1,8,256,256]{4,3,2,1,0:T(8,128)(2,1)}, u32[]{:S(2)}, u32[]{:S(2)}) collective-permute-start(bf16[2,1,8,256,256]{4,3,2,1,0:T(8,128)(2,1)} %get-tuple-element.69.refs_4_), channel_id=1, source_target_pairs={{0,2},{1,3},{2,0},{3,1},{4,6},{5,7},{6,4},{7,5},{8,10},{9,11},{10,... | collective-permute-start | bytes 6291464 | tf_op jit(solution)/shard_map/ppermute | solution.py:344
  171.8 88.1 %collective-permute-start.11 = (bf16[2,2,8,128,256]{4,3,2,1,0:T(8,128)(2,1)S(1)}, bf16[2,2,8,128,256]{4,3,2,1,0:T(8,128)(2,1)}, u32[]{:S(2)}, u32[]{:S(2)}) collective-permute-start(bf16[2,2,8,128,256]{4,3,2,1,0:T(8,128)(2,1)S(1)} %collective-permute-done.refs_2_.refs_0_), channel_id=1, source_target_pairs={{0,4},{1,5},{2,6},{3,7},{4,0},{5,1},{6,2},{7,3},{8,12},{9,13},{10,... | collective-permute-start | bytes 6291464 | tf_op jit(solution)/shard_map/ppermute | solution.py:344
  209.3 51.4 %collective-permute-start.13 = (bf16[2,2,8,128,256]{4,3,2,1,0:T(8,128)(2,1)S(1)}, bf16[2,2,8,128,256]{4,3,2,1,0:T(8,128)(2,1)}, u32[]{:S(2)}, u32[]{:S(2)}) collective-permute-start(bf16[2,2,8,128,256]{4,3,2,1,0:T(8,128)(2,1)S(1)} %collective-permute-done.refs_2_.refs_0_), channel_id=1, source_target_pairs={{0,1},{1,0},{2,3},{3,2},{4,5},{5,4},{6,7},{7,6},{8,9},{9,8},{10,11... | collective-permute-start | bytes 6291464 | tf_op jit(solution)/shard_map/ppermute | solution.py:344
  209.4 40.2 %collective-permute-start.10 = (bf16[1,1,8,128,256]{4,3,2,1,0:T(8,128)(2,1)}, bf16[1,1,8,128,256]{4,3,2,1,0:T(8,128)(2,1)S(1)}, u32[]{:S(2)}, u32[]{:S(2)}) collective-permute-start(bf16[1,1,8,128,256]{4,3,2,1,0:T(8,128)(2,1)} %get-tuple-element.80), channel_id=1, source_target_pairs={{0,8},{1,9},{2,10},{3,11},{4,12},{5,13},{6,14},{7,15},{8,0},{9,1},... | collective-permute-start | bytes 1572872 | tf_op jit(solution)/shard_map/ppermute | solution.py:344
  212.2 46.8 %collective-permute-start.9 = (bf16[1,1,8,128,256]{4,3,2,1,0:T(8,128)(2,1)}, bf16[1,1,8,128,256]{4,3,2,1,0:T(8,128)(2,1)S(1)}, u32[]{:S(2)}, u32[]{:S(2)}) collective-permute-start(bf16[1,1,8,128,256]{4,3,2,1,0:T(8,128)(2,1)} %get-tuple-element.79), channel_id=1, source_target_pairs={{0,8},{1,9},{2,10},{3,11},{4,12},{5,13},{6,14},{7,15},{8,0},{9,1},... | collective-permute-start | bytes 1572872 | tf_op jit(solution)/shard_map/ppermute | solution.py:344
  249.4 11.5 %collective-permute-start.14 = (bf16[2,2,8,128,256]{4,3,2,1,0:T(8,128)(2,1)}, bf16[2,2,8,128,256]{4,3,2,1,0:T(8,128)(2,1)}, u32[]{:S(2)}, u32[]{:S(2)}) collective-permute-start(bf16[2,2,8,128,256]{4,3,2,1,0:T(8,128)(2,1)} %collective-permute-done.1.refs_4_.refs_6_), channel_id=1, source_target_pairs={{0,1},{1,0},{2,3},{3,2},{4,5},{5,4},{6,7},{7,6},{8,9},{9,8},{10,11... | collective-permute-start | bytes 6291464 | tf_op jit(solution)/shard_map/ppermute | solution.py:344
  249.5 14.8 %copy-start.5 = (bf16[1,1,8,128,256]{4,3,2,1,0:T(8,128)(2,1)}, bf16[1,1,8,128,256]{4,3,2,1,0:T(8,128)(2,1)S(1)}, u32[]{:S(2)}) copy-start(bf16[1,1,8,128,256]{4,3,2,1,0:T(8,128)(2,1)S(1)} %collective-permute-done.10.q_ref) | copy-start | bytes 1572868
  259.0 16.0 %copy-start.4 = (bf16[1,1,8,128,256]{4,3,2,1,0:T(8,128)(2,1)}, bf16[1,1,8,128,256]{4,3,2,1,0:T(8,128)(2,1)S(1)}, u32[]{:S(2)}) copy-start(bf16[1,1,8,128,256]{4,3,2,1,0:T(8,128)(2,1)S(1)} %collective-permute-done.9.q_ref) | copy-start | bytes 1572868
  259.9 4.5 collective-permute-start.15
  259.9 48.4 %collective-permute-start.16 = (bf16[2,2,8,128,256]{4,3,2,1,0:T(8,128)(2,1)}, bf16[2,2,8,128,256]{4,3,2,1,0:T(8,128)(2,1)}, u32[]{:S(2)}, u32[]{:S(2)}) collective-permute-start(bf16[2,2,8,128,256]{4,3,2,1,0:T(8,128)(2,1)} %collective-permute-done.7.refs_10_), channel_id=1, source_target_pairs={{0,2},{1,3},{2,0},{3,1},{4,6},{5,7},{6,4},{7,5},{8,10},{9,11},{10,... | collective-permute-start | bytes 6291464 | tf_op jit(solution)/shard_map/ppermute | solution.py:344
  260.4 59.0 %collective-permute-start.18 = (bf16[2,1,8,256,256]{4,3,2,1,0:T(8,128)(2,1)}, bf16[2,1,8,256,256]{4,3,2,1,0:T(8,128)(2,1)}, u32[]{:S(2)}, u32[]{:S(2)}) collective-permute-start(bf16[2,1,8,256,256]{4,3,2,1,0:T(8,128)(2,1)} %collective-permute-done.12.refs_4_), channel_id=1, source_target_pairs={{0,1},{1,0},{2,3},{3,2},{4,5},{5,4},{6,7},{7,6},{8,9},{9,8},{10,11... | collective-permute-start | bytes 6291464 | tf_op jit(solution)/shard_map/ppermute | solution.py:344
  260.6 61.2 %collective-permute-start.19 = (bf16[2,2,8,128,256]{4,3,2,1,0:T(8,128)(2,1)}, bf16[2,2,8,128,256]{4,3,2,1,0:T(8,128)(2,1)S(1)}, u32[]{:S(2)}, u32[]{:S(2)}) collective-permute-start(bf16[2,2,8,128,256]{4,3,2,1,0:T(8,128)(2,1)} %collective-permute-done.7.refs_10_), channel_id=1, source_target_pairs={{0,1},{1,0},{2,3},{3,2},{4,5},{5,4},{6,7},{7,6},{8,9},{9,8},{10,11... | collective-permute-start | bytes 6291464 | tf_op jit(solution)/shard_map/ppermute | solution.py:344
  260.9 60.9 %collective-permute-start.17 = (bf16[2,2,8,128,256]{4,3,2,1,0:T(8,128)(2,1)}, bf16[2,2,8,128,256]{4,3,2,1,0:T(8,128)(2,1)}, u32[]{:S(2)}, u32[]{:S(2)}) collective-permute-start(bf16[2,2,8,128,256]{4,3,2,1,0:T(8,128)(2,1)} %collective-permute-done.6.refs_2_), channel_id=1, source_target_pairs={{0,1},{1,0},{2,3},{3,2},{4,5},{5,4},{6,7},{7,6},{8,9},{9,8},{10,11... | collective-permute-start | bytes 6291464 | tf_op jit(solution)/shard_map/ppermute | solution.py:344
  308.2 61.6 %collective-permute-start.20 = (bf16[2,2,8,128,256]{4,3,2,1,0:T(8,128)(2,1)}, bf16[2,2,8,128,256]{4,3,2,1,0:T(8,128)(2,1)}, u32[]{:S(2)}, u32[]{:S(2)}) collective-permute-start(bf16[2,2,8,128,256]{4,3,2,1,0:T(8,128)(2,1)} %collective-permute-done.16.refs_12_), channel_id=1, source_target_pairs={{0,1},{1,0},{2,3},{3,2},{4,5},{5,4},{6,7},{7,6},{8,9},{9,8},{10,11... | collective-permute-start | bytes 6291464 | tf_op jit(solution)/shard_map/ppermute | solution.py:344
  308.2 80.3 %collective-permute-start.22 = (bf16[2,1,8,256,256]{4,3,2,1,0:T(8,128)(2,1)}, bf16[2,1,8,256,256]{4,3,2,1,0:T(8,128)(2,1)}, u32[]{:S(2)}, u32[]{:S(2)}) collective-permute-start(bf16[2,1,8,256,256]{4,3,2,1,0:T(8,128)(2,1)} %get-tuple-element.94.refs_4_), channel_id=1, source_target_pairs={{0,2},{1,3},{2,0},{3,1},{4,6},{5,7},{6,4},{7,5},{8,10},{9,11},{10,... | collective-permute-start | bytes 6291464 | tf_op jit(solution)/shard_map/ppermute | solution.py:344
  319.4 69.3 %copy-start.3 = (f32[1,8,264,128]{3,2,1,0:T(8,128)S(1)}, f32[1,8,264,128]{3,2,1,0:T(8,128)}, u32[]{:S(2)}) copy-start(f32[1,8,264,128]{3,2,1,0:T(8,128)} %shard_map.57) | copy-start | bytes 3244036
  319.4 50.4 %collective-permute-start.21 = (f32[1,8,264,128]{3,2,1,0:T(8,128)}, f32[1,8,264,128]{3,2,1,0:T(8,128)}, u32[]{:S(2)}, u32[]{:S(2)}) collective-permute-start(f32[1,8,264,128]{3,2,1,0:T(8,128)} %shard_map.58), channel_id=1, source_target_pairs={{0,8},{1,9},{2,10},{3,11},{4,12},{5,13},{6,14},{7,15},{8,0},{9,1},... | collective-permute-start | bytes 3244040 | tf_op jit(solution)/shard_map/ppermute | solution.py:344
  321.9 47.9 %copy-start.1 = (bf16[2,2,8,128,256]{4,3,2,1,0:T(8,128)(2,1)}, bf16[2,2,8,128,256]{4,3,2,1,0:T(8,128)(2,1)S(1)}, u32[]{:S(2)}) copy-start(bf16[2,2,8,128,256]{4,3,2,1,0:T(8,128)(2,1)S(1)} %collective-permute-done.19.refs_11_) | copy-start | bytes 6291460
  388.6 50.5 %collective-permute-start.23 = (bf16[2,1,8,256,256]{4,3,2,1,0:T(8,128)(2,1)}, bf16[2,1,8,256,256]{4,3,2,1,0:T(8,128)(2,1)S(1)}, u32[]{:S(2)}, u32[]{:S(2)}) collective-permute-start(bf16[2,1,8,256,256]{4,3,2,1,0:T(8,128)(2,1)} %collective-permute-done.22.refs_4_), channel_id=1, source_target_pairs={{0,1},{1,0},{2,3},{3,2},{4,5},{5,4},{6,7},{7,6},{8,9},{9,8},{10,11... | collective-permute-start | bytes 6291464 | tf_op jit(solution)/shard_map/ppermute | solution.py:344
  388.6 50.4 %collective-permute-start.24 = (f32[1,8,264,128]{3,2,1,0:T(8,128)S(1)}, f32[1,8,264,128]{3,2,1,0:T(8,128)}, u32[]{:S(2)}, u32[]{:S(2)}) collective-permute-start(f32[1,8,264,128]{3,2,1,0:T(8,128)S(1)} %copy-done.3), channel_id=1, source_target_pairs={{0,8},{1,9},{2,10},{3,11},{4,12},{5,13},{6,14},{7,15},{8,0},{9,1},... | collective-permute-start | bytes 3244040 | tf_op jit(solution)/shard_map/ppermute | solution.py:344
  439.1 1.4 copy-start.2

commit v3 on v2

v3 whole, which is shorter than its diff:
```python
import functools
import math

import jax
import jax.numpy as jnp
from jax import lax
from jax.experimental import pallas as pl
from jax.experimental.pallas import tpu as pltpu
from jax.sharding import PartitionSpec as P


SLOT = (0, 4, 2, 6, 1, 5, 3, 7)
LOG2E = 1.4426950408889634
F32 = jnp.float32
BF16 = jnp.bfloat16
TILE = 256
PARTS = 2


def cost(flops, bytes_accessed, transcendentals=0):
    return pl.CostEstimate(flops=int(flops), bytes_accessed=int(bytes_accessed), transcendentals=int(transcendentals))


def swap_bits(head):
    return (head % 2) * 4 + (head // 2 % 2) * 2 + head // 4


def position(slot, own):
    if slot // 2 == own // 2:
        return int(slot != own)
    return 2 + slot % 2 if slot // 4 == own // 4 else 4 + slot % 4


def onehot(transposed=False):
    dims = (1, 0) if transposed else (0, 1)
    out_row = lax.broadcasted_iota(jnp.int32, (TILE, TILE), dims[0])
    in_row = lax.broadcasted_iota(jnp.int32, (TILE, TILE), dims[1])
    hit = in_row == (out_row % 32) * 8 + out_row // 32
    return jnp.where(hit, 1.0, 0.0).astype(BF16)


def split_block(take, a_refs, o_ref, slots):
    at = 0
    for a_ref in a_refs:
        for start in range(0, a_ref.shape[0], TILE):
            rows = jnp.dot(take, a_ref[start:start + TILE, :], preferred_element_type=F32).astype(BF16)
            for res in range(8):
                o_ref[slots[res], at:at + 32, :] = rows[res * 32:(res + 1) * 32]
            at += 32


def split_kernel(slots, *refs):
    take = onehot()
    n = len(slots)
    parts = len(refs) // n - 1
    for i in range(n):
        split_block(take, refs[i * parts:(i + 1) * parts], refs[n * parts + i], slots[i])


def part_spec(block, parts, part):
    return pl.BlockSpec(block, lambda i: (i * parts + part, 0))


def split_rows(arrays, slots, steps):
    parts = PARTS if all(a.shape[0] // steps % (PARTS * TILE) == 0 for a in arrays) else 1
    return pl.pallas_call(
        functools.partial(split_kernel, slots),
        grid=(steps,),
        in_specs=[part_spec((a.shape[0] // (steps * parts), a.shape[1]), parts, part) for a in arrays for part in range(parts)],
        out_specs=[pl.BlockSpec((8, a.shape[0] // (8 * steps), a.shape[1]), lambda i: (0, i, 0)) for a in arrays],
        out_shape=[jax.ShapeDtypeStruct((8, a.shape[0] // 8, a.shape[1]), BF16) for a in arrays],
        cost_estimate=cost(sum(2 * a.size * TILE for a in arrays), sum(4 * a.size for a in arrays)),
        name="split_rows",
    )(*[a for a in arrays for _ in range(parts)])


def slot_copy(x_hbm, x_scr, sems, slot):
    rows = x_scr.shape[0] // 8
    part = pl.ds(slot * rows if isinstance(slot, int) else pl.multiple_of(slot * rows, rows), rows)
    return pltpu.make_async_copy(x_hbm.at[part, :], x_scr.at[part, :], sems.at[slot])


def joined(w_refs, wi):
    return jnp.concatenate([ref[0] for ref in w_refs[wi * PARTS:(wi + 1) * PARTS]], axis=0)


def near_kernel(n_seqs, x_hbm, *refs):
    w_refs, refs = refs[:2 * PARTS], refs[2 * PARTS:]
    e_ref, b_refs, (x_scr, sems) = refs[0], refs[1:1 + n_seqs], refs[1 + n_seqs:]
    rows = x_scr.shape[0] // 8
    nb = rows // n_seqs
    own = pl.program_id(0)

    @pl.when(own == 0)
    def _():
        for slot in range(8):
            slot_copy(x_hbm, x_scr, sems, slot).start()

    @pl.when(own % 2 == 0)
    def _():
        slot_copy(x_hbm, x_scr, sems, own).wait()
        slot_copy(x_hbm, x_scr, sems, own + 1).wait()

    mine = x_scr[pl.ds(pl.multiple_of(own * rows, rows), rows), :]
    other = x_scr[pl.ds(pl.multiple_of((own + 1 - 2 * (own % 2)) * rows, rows), rows), :]
    both = jnp.concatenate([mine, other], axis=0)
    for wi in range(2):
        out = jnp.dot(both, joined(w_refs, wi), preferred_element_type=F32).astype(BF16)
        for seq in range(n_seqs):
            e_ref[wi, seq] = out[seq * nb:(seq + 1) * nb]
            b_refs[seq][wi, 0] = out[rows + seq * nb:rows + (seq + 1) * nb]


def rest_kernel(n_seqs, x_hbm, *refs):
    w_refs, wq_ref, refs = refs[:2 * PARTS], refs[2 * PARTS], refs[2 * PARTS + 1:]
    g_refs, r_ref, wq_out, (x_scr, sems) = refs[:n_seqs], refs[n_seqs], refs[n_seqs + 1], refs[n_seqs + 2:]
    rows = x_scr.shape[0] // 8
    nb = rows // n_seqs
    own = pl.program_id(0)

    @pl.when(own == 0)
    def _():
        for slot in (2, 3, 4, 5, 6, 7, 0, 1):
            slot_copy(x_hbm, x_scr, sems, slot).start()
        for slot in range(2, 8):
            slot_copy(x_hbm, x_scr, sems, slot).wait()

    @pl.when(own == 2)
    def _():
        for slot in range(2):
            slot_copy(x_hbm, x_scr, sems, slot).wait()

    split_block(onehot(), (wq_ref,), wq_out, tuple(range(8)))
    pair = pl.ds(pl.multiple_of((own // 2 + 1 - 2 * (own // 2 % 2)) * 2 * rows, 2 * rows), 2 * rows)
    half = pl.ds(pl.multiple_of((1 - own // 4) * 4 * rows, 4 * rows), 4 * rows)
    for wi in range(2):
        weight = joined(w_refs, wi)
        out = jnp.dot(x_scr[pair, :], weight, preferred_element_type=F32).astype(BF16)
        for slot in range(2):
            for seq in range(n_seqs):
                at = (slot * n_seqs + seq) * nb
                g_refs[seq][wi, 0, slot * nb:(slot + 1) * nb, :] = out[at:at + nb]
        out = jnp.dot(x_scr[half, :], weight, preferred_element_type=F32).astype(BF16)
        for slot in range(4):
            for seq in range(n_seqs):
                at = (slot * n_seqs + seq) * nb
                r_ref[wi, seq, slot * nb:(slot + 1) * nb, :] = out[at:at + nb]


def query_kernel(n_seqs, x_hbm, *refs):
    w_refs, q_ref, refs = refs[:PARTS], refs[PARTS], refs[PARTS + 1:]
    first_refs, (x_scr, sems) = refs[:n_seqs], refs[n_seqs:]
    rows = x_scr.shape[0] // 8
    nb = rows // n_seqs
    own = pl.program_id(0)

    @pl.when(own == 0)
    def _():
        for slot in range(8):
            slot_copy(x_hbm, x_scr, sems, slot).start()
        for slot in range(8):
            slot_copy(x_hbm, x_scr, sems, slot).wait()

    out = jnp.dot(x_scr[...], joined(w_refs, 0), preferred_element_type=F32).astype(BF16)
    for slot in range(8):
        far_pos = jnp.where(slot // 4 == own // 4, 2 + slot % 2, 4 + slot % 4)
        pos = jnp.where(slot == own, 0, jnp.where(slot // 2 == own // 2, 1, far_pos))
        for seq in range(n_seqs):
            at = (slot * n_seqs + seq) * nb
            q_ref[0, seq, pl.ds(pl.multiple_of(pos * nb, nb), nb), :] = out[at:at + nb]
    for seq in range(n_seqs):
        first_refs[seq][0, 0] = q_ref[0, seq, :nb, :]


def w_spec(block, part):
    return pl.BlockSpec(block, lambda g: (swap_bits(g), part, 0))


def project(kernel, xp, ws, n_seqs, outs, natural=None):
    n_heads, model_dim, head_dim = ws[0].shape
    out_rows = sum(n_w * seqs * n for n_w, seqs, n in outs)
    out_specs = [pl.BlockSpec((n_w, seqs, None, n, head_dim), lambda g: (0, 0, swap_bits(g), 0, 0)) for n_w, seqs, n in outs]
    out_shape = [jax.ShapeDtypeStruct((n_w, seqs, n_heads, n, head_dim), BF16) for n_w, seqs, n in outs]
    in_specs = [pl.BlockSpec(memory_space=pl.ANY)]
    in_specs += [w_spec((1, model_dim // PARTS, head_dim), part) for _ in ws for part in range(PARTS)]
    more = ()
    if natural is not None:
        more = (natural,)
        in_specs.append(pl.BlockSpec((natural.shape[0] // n_heads, head_dim), lambda g: (g, 0)))
        out_specs.append(pl.BlockSpec((8, model_dim // n_heads, head_dim), lambda g: (0, g, 0)))
        out_shape.append(jax.ShapeDtypeStruct((8, model_dim, head_dim), BF16))
    return pl.pallas_call(
        functools.partial(kernel, n_seqs),
        grid=(n_heads,),
        in_specs=in_specs,
        out_specs=out_specs,
        out_shape=out_shape,
        scratch_shapes=[pltpu.VMEM(xp.shape, BF16), pltpu.SemaphoreType.DMA((8,))],
        cost_estimate=cost(2 * n_heads * out_rows * model_dim * head_dim, 2 * (xp.size + len(ws) * ws[0].size) + 2 * n_heads * out_rows * head_dim),
        name="project",
    )(xp, *[w for w in ws for _ in range(PARTS)], *more)


def mult_of(group, key_group, level):
    return min(group, key_group) - level + 1


def by_group(groups, key_group, level, log=False):
    mults = [mult_of(group, key_group, level) for group, _ in groups]
    if all(mult == 1 for mult in mults):
        return None
    values = [math.log2(mult) if log else float(mult) for mult in mults]
    n_cols = sum(cols for _, cols in groups)
    col = lax.broadcasted_iota(jnp.int32, (1, n_cols), 1)
    row, base = jnp.full((1, n_cols), values[-1], F32), n_cols
    for value, (_, cols) in list(zip(values, groups))[::-1]:
        row = jnp.where(col < base, value, row)
        base -= cols
    return row


def scores(keys, q):
    return lax.dot_general(keys, q, (((1,), (1,)), ((), ())), preferred_element_type=F32)


def fold(op, p):
    return op(p.reshape(p.shape[0] // 8, 8, p.shape[1]), axis=0)


def gather_keys(kv_refs, k_scr, v_scr):
    off = 0
    for ref in kv_refs:
        rows = ref.shape[1]
        k_scr[off:off + rows, :] = ref[0]
        v_scr[:, off:off + rows] = jnp.transpose(ref[1])
        off += rows


def branch0_stages(q, k_scr, v_scr, segs, step, groups, s_scr, p_scr, result):
    scale = LOG2E * q.shape[1] ** -0.5
    peak = None
    for start in range(0, k_scr.shape[0], step):
        s = scores(k_scr[start:start + step, :], q)
        s_scr[start:start + step, :] = s
        top = fold(jnp.max, s)
        peak = top if peak is None else jnp.maximum(peak, top)
        yield
    shift = jnp.max(peak, axis=0, keepdims=True) * scale
    sums, start = [], 0
    for length, _ in segs:
        p = jnp.exp2(s_scr[start:start + length, :] * scale - shift)
        s_scr[start:start + length, :] = p
        sums.append(jnp.sum(fold(jnp.sum, p), axis=0, keepdims=True))
        start += length
        yield
    total = functools.reduce(jnp.add, sums)
    inverse = 1.0 / total
    weight, start = None, 0
    for (length, key_group), part in zip(segs, sums):
        mult = by_group(groups, key_group, 0)
        factor = inverse if mult is None else inverse * mult
        p_scr[start:start + length, :] = (s_scr[start:start + length, :] * factor).astype(BF16)
        weight = part * factor if weight is None else weight + part * factor
        start += length
        yield
    acc = jnp.dot(v_scr[...], p_scr[...], preferred_element_type=F32)
    result.extend((shift + jnp.log2(total), weight, acc))
    yield


def level0_kernel(nb, q_ref, *refs):
    kv_refs, (o_ref, acc_ref, stat_ref, k_scr, v_scr, s_scr, p_scr, s_scr2, p_scr2) = refs[:8], refs[8:]
    gather_keys(kv_refs, k_scr, v_scr)
    segs = ((2 * nb, 3), (2 * nb, 2), (4 * nb, 1), (4 * nb, 0), (4 * nb, 0))
    groups = ((3, nb), (2, nb), (1, 2 * nb))
    high, low = [], []
    lead = branch0_stages(q_ref[4 * nb:, :], k_scr, v_scr, segs, 4 * nb, ((0, 4 * nb),), s_scr2, p_scr2, high)
    trail = branch0_stages(q_ref[:4 * nb, :], k_scr, v_scr, segs, 4 * nb, groups, s_scr, p_scr, low)
    for _ in range(4):
        next(lead)
    while not low:
        next(lead, None)
        next(trail)
    shift, weight, acc = low
    acc_ref[...] = acc
    stat_ref[0:1, :] = shift
    stat_ref[1:2, :] = weight
    o_ref[...] = jnp.transpose(high[2]).astype(BF16)


def weights(s, shift, scale, segs, groups, level, p_scr):
    start, total = 0, None
    for length, key_group in segs:
        mult = by_group(groups, key_group, level, log=True)
        local = shift if mult is None else shift - mult
        p = jnp.exp2(s[start:start + length, :] * scale - local)
        p_scr[start:start + length, :] = p.astype(BF16)
        part = fold(jnp.sum, p)
        total = part if total is None else total + part
        start += length
    return jnp.sum(total, axis=0, keepdims=True)


def peak_of(s, scale):
    return jnp.max(fold(jnp.max, s), axis=0, keepdims=True) * scale


def upper(op, low, row):
    n_cols = low.shape[1]
    return jnp.concatenate([op(row[:, :n_cols], low), row[:, n_cols:]], axis=1)


def level1_kernel(nb, q_ref, *refs):
    kv_refs, (acc_in, stat_in, o_ref, acc_ref, stat_ref, k_scr, v_scr, p_scr) = refs[:6], refs[6:]
    gather_keys(kv_refs, k_scr, v_scr)
    scale = LOG2E * q_ref.shape[1] ** -0.5
    s = scores(k_scr[...], q_ref[...])
    shift_near, sum_near = stat_in[0:1, :], stat_in[1:2, :]
    shift = jnp.maximum(shift_near, peak_of(s, scale))
    total = weights(s, shift, scale, ((2 * nb, 3), (2 * nb, 2), (4 * nb, 1)), ((3, nb), (2, nb), (1, 2 * nb)), 1, p_scr)
    near_scale = jnp.exp2(shift_near - shift)
    total = sum_near * near_scale + total
    acc = acc_in[...] * near_scale + jnp.dot(v_scr[...], p_scr[...], preferred_element_type=F32)
    acc_ref[...] = acc[:, :2 * nb]
    stat_ref[0:1, :] = shift[:, :2 * nb]
    stat_ref[1:2, :] = total[:, :2 * nb]
    o_ref[...] = jnp.transpose(acc[:, 2 * nb:] * (1.0 / total[:, 2 * nb:])).astype(BF16)


def level2_kernel(nb, q_ref, *refs):
    kv_refs, (acc_in, stat_in, far_ref, o_ref, k_scr, v_scr, p_scr) = refs[:8], refs[8:]
    gather_keys(kv_refs, k_scr, v_scr)
    head_dim = q_ref.shape[1]
    scale = LOG2E * head_dim ** -0.5
    s = scores(k_scr[...], q_ref[...])
    shift_near, sum_near = stat_in[0:1, :], stat_in[1:2, :]
    shift_far, sum_far = far_ref[head_dim:head_dim + 1, :], far_ref[head_dim + 1:head_dim + 2, :]
    shift = upper(jnp.maximum, shift_far, jnp.maximum(shift_near, peak_of(s, scale)))
    total = weights(s, shift, scale, ((4 * nb, 3), (4 * nb, 2)), ((3, nb), (2, nb)), 2, p_scr)
    near_scale = jnp.exp2(shift_near - shift)
    far_scale = jnp.exp2(shift_far - shift[:, :nb])
    total = upper(jnp.add, sum_far * far_scale, sum_near * near_scale + total)
    acc = acc_in[...] * near_scale + jnp.dot(v_scr[...], p_scr[...], preferred_element_type=F32)
    acc = upper(jnp.add, far_ref[:head_dim, :] * far_scale, acc)
    o_ref[...] = jnp.transpose(acc * (1.0 / total)).astype(BF16)


def far_kernel(nb, q_ref, *refs):
    kv_refs, (far_ref, k_scr, v_scr, p_scr) = refs[:8], refs[8:]
    gather_keys(kv_refs, k_scr, v_scr)
    head_dim = q_ref.shape[1]
    scale = LOG2E * head_dim ** -0.5
    s = scores(k_scr[...], q_ref[...])
    shift = peak_of(s, scale)
    total = weights(s, shift, scale, ((8 * nb, 3),), ((3, nb),), 3, p_scr)
    far_ref[:head_dim, :] = jnp.dot(v_scr[...], p_scr[...], preferred_element_type=F32)
    far_ref[head_dim:, :] = jnp.concatenate([shift, total] + [jnp.zeros_like(shift)] * 6, axis=0)


def attend(body, nb, q, q_rows, kvs, states, outs, seq, scratch, pairs):
    n_heads, head_dim = q.shape[2], q.shape[4]
    n_keys = sum(kv.shape[3] for kv in kvs)

    def spec(n_here, *dims):
        base = seq if n_here > 1 else 0
        return pl.BlockSpec((None, None, *dims), lambda h: (base, h, 0, 0))

    def lead_spec(lead, n_here, rows):
        base = seq if n_here > 1 else 0
        return pl.BlockSpec((lead, None, None, rows, head_dim), lambda h: (0, base, h, 0, 0))

    return pl.pallas_call(
        functools.partial(body, nb),
        grid=(n_heads,),
        in_specs=[lead_spec(None, q.shape[1], q_rows)]
        + [lead_spec(2, kv.shape[1], kv.shape[3]) for kv in kvs]
        + [spec(state.shape[0], *state.shape[2:]) for state in states],
        out_specs=[spec(1, rows, width) for rows, width, _ in outs],
        out_shape=[jax.ShapeDtypeStruct((1, n_heads, rows, width), dtype) for rows, width, dtype in outs],
        scratch_shapes=[pltpu.VMEM(dims, dtype) for dims, dtype in scratch],
        cost_estimate=cost(4 * n_heads * pairs * head_dim, 2 * n_heads * head_dim * (q_rows + 2 * n_keys), n_heads * pairs),
    )(q, *kvs, *states)


def out_kernel(nb, o_low, o_mid, o_high, w_ref, *refs):
    y_ref, mix, lhs = refs[-3:]
    n_tok = lhs.shape[0]

    @pl.when(pl.program_id(0) == 0)
    def _():
        back = onehot(transposed=True)
        for sub in range(n_tok // TILE):
            for res in range(8):
                for head in range(8):
                    pos = position(SLOT[res], SLOT[head])
                    ref, base = (o_low, 0) if pos < 2 else (o_mid, 2) if pos < 4 else (o_high, 4)
                    first = (pos - base) * nb + sub * 32
                    piece = ref[0, head, first:first + 32, :]
                    mix[res * 32:(res + 1) * 32, head * piece.shape[1]:(head + 1) * piece.shape[1]] = piece
            lhs[sub * TILE:(sub + 1) * TILE, :] = jnp.dot(back, mix[...], preferred_element_type=F32).astype(BF16)

    y_ref[0] = jnp.dot(lhs[...], w_ref[...], preferred_element_type=F32).astype(BF16)


def out_project(o_low, o_mid, o_high, w, nb, seq, n_seqs, y_prev):
    width, model_dim = w.shape
    n_tok = nb * 8
    n_cols = min(512, model_dim)
    in_specs = [pl.BlockSpec(a.shape, lambda i: (0, 0, 0, 0)) for a in (o_low, o_mid, o_high)] + [pl.BlockSpec((width, n_cols), lambda i: (0, i))]
    more = () if y_prev is None else (y_prev,)
    return pl.pallas_call(
        functools.partial(out_kernel, nb),
        grid=(model_dim // n_cols,),
        in_specs=in_specs + [pl.BlockSpec(memory_space=pl.ANY) for _ in more],
        out_specs=pl.BlockSpec((1, n_tok, n_cols), lambda i: (seq, 0, i)),
        out_shape=jax.ShapeDtypeStruct((n_seqs, n_tok, model_dim), BF16),
        scratch_shapes=[pltpu.VMEM((TILE, width), BF16), pltpu.VMEM((n_tok, width), BF16)],
        input_output_aliases={4: 0} if more else {},
        cost_estimate=cost(2 * n_tok * width * model_dim, 4 * n_tok * width + 2 * w.size),
        name="out_project",
    )(o_low, o_mid, o_high, w, *more)


def solution(mesh):
    n_dev = mesh.shape['sp']

    def swap(a, bit):
        return lax.ppermute(a, 'sp', [(d, d ^ bit) for d in range(n_dev)])

    def local_step(x_loc, w_q, w_k, w_v, w_o):
        n_seqs, n_tok, model_dim = x_loc.shape
        n_heads, head_dim = w_q.shape[1], w_q.shape[2]
        nb = n_tok // 8
        n_rows = n_seqs * n_tok
        after = lax.optimization_barrier

        seqs = range(n_seqs)
        natural = [w.reshape(model_dim * n_heads, head_dim) for w in (w_q, w_k, w_v)]
        plain = tuple(range(8))
        xp, wk, wv = split_rows((x_loc.reshape(n_rows, model_dim), *natural[1:]), (SLOT, plain, plain), 2 if n_rows < 8 * TILE else 8)
        xp = xp.reshape(n_rows, model_dim)

        e, *b = project(near_kernel, xp, (wk, wv), n_seqs, ((2, n_seqs, nb),) + ((2, 1, nb),) * n_seqs)
        wk, wv, e, b = after((wk, wv, e, b))
        y_e, z_e, c_e = swap(e, 2), swap(e, 4), swap(e, 1)
        y_b, c_b = [swap(b[seq], 2) for seq in seqs], [swap(b[seq], 1) for seq in seqs]
        *g, r, wq = project(rest_kernel, xp, (wk, wv), n_seqs, ((2, 1, 2 * nb),) * n_seqs + ((2, n_seqs, 4 * nb),), natural[0])
        wq, g, r = after((wq, g, r))
        y_g, c_g = [swap(g[seq], 2) for seq in seqs], [swap(g[seq], 1) for seq in seqs]
        c_r = swap(r, 1)
        q_all, *q_first = project(query_kernel, xp, (wq,), n_seqs, ((1, n_seqs, 8 * nb),) + ((1, 1, nb),) * n_seqs)

        q_all, q_first, y_e, z_e, b_late = after((q_all, q_first, y_e, z_e, b))
        q_far = [swap(q_first[seq], 8) for seq in seqs]
        zy_e, yc_e, zc_e = swap(y_e, 4), swap(y_e, 1), swap(z_e, 1)
        z_b = [swap(b_late[seq], 4) for seq in seqs]

        near = []
        for seq in seqs:
            kvs = (e, c_e, b[seq], c_b[seq], g[seq], c_g[seq], r, c_r)
            keys = 16 * nb
            scratch = [((keys, head_dim), BF16), ((head_dim, keys), BF16)] + [((keys, 4 * nb), F32), ((keys, 4 * nb), BF16)] * 2
            near.append(attend(level0_kernel, nb, q_all, 8 * nb, kvs, (),
                               ((4 * nb, head_dim, BF16), (head_dim, 4 * nb, F32), (8, 4 * nb, F32)), seq, scratch, 8 * nb * keys))
            near[seq], q_all = after((near[seq], q_all))
        near, q_all, q_far, zy_e, y_b = after((near, q_all, q_far, zy_e, y_b))
        zyc_e = swap(zy_e, 1)
        yc_b = [swap(y_b[seq], 1) for seq in seqs]
        far_in = []
        for seq in seqs:
            kvs = (e, c_e, y_e, yc_e, z_e, zc_e, zy_e, zyc_e)
            scratch = [((8 * nb, head_dim), BF16), ((head_dim, 8 * nb), BF16), ((8 * nb, nb), BF16)]
            far, = attend(far_kernel, nb, q_far[seq], nb, kvs, (), ((head_dim + 8, nb, F32),), seq, scratch, 8 * nb * nb)
            far_in.append(swap(far, 8))
        zy_b, zc_b, yc_g, one, token = [], [], [], [], far
        for seq in seqs:
            token, z_b[seq], y_g[seq], q_all = after((token, z_b[seq], y_g[seq], q_all))
            zy_b.append(swap(z_b[seq], 2))
            zc_b.append(swap(z_b[seq], 1))
            yc_g.append(swap(y_g[seq], 1))
            kvs = (y_e, yc_e, y_b[seq], yc_b[seq], y_g[seq], yc_g[seq])
            scratch = [((8 * nb, head_dim), BF16), ((head_dim, 8 * nb), BF16), ((8 * nb, 4 * nb), BF16)]
            one.append(attend(level1_kernel, nb, q_all, 4 * nb, kvs, near[seq][1:],
                              ((2 * nb, head_dim, BF16), (head_dim, 2 * nb, F32), (8, 2 * nb, F32)), seq, scratch, 8 * nb * 4 * nb))
            token = one[seq][2]
        y = None
        w_out = w_o.reshape(n_heads * head_dim, model_dim)
        zyc_b = []
        for seq in seqs:
            token, zy_b[seq] = after((token, zy_b[seq]))
            zyc_b.append(swap(zy_b[seq], 1))
            if seq > 0:
                y = out_project(o_low, one[seq - 1][0], near[seq - 1][0], w_out, nb, seq - 1, n_seqs, y)
            kvs = (z_e, zc_e, zy_e, zyc_e, z_b[seq], zc_b[seq], zy_b[seq], zyc_b[seq])
            scratch = [((8 * nb, head_dim), BF16), ((head_dim, 8 * nb), BF16), ((8 * nb, 2 * nb), BF16)]
            o_low, = attend(level2_kernel, nb, q_all, 2 * nb, kvs, (*one[seq][1:], far_in[seq]), ((2 * nb, head_dim, BF16),), seq,
                            scratch, 8 * nb * 2 * nb)
            token = o_low
        y = out_project(o_low, one[-1][0], near[-1][0], w_out, nb, n_seqs - 1, n_seqs, y)
        return y

    return jax.shard_map(local_step, mesh=mesh, in_specs=(P('dp', 'sp', None), P(), P(), P(), P()), out_specs=P('dp', 'sp', None), check_vma=False)
```

time: 475 us -> 477 us (level)
  Pallas kernels: 280 us -> 270 us
  starting transfers between devices: 16.8 us -> 21.8 us
    pallas_call x3 -> x1, Pallas kernels: 37.2 us -> 20.8 us  [split_rows(): pl.pallas_call(functools.partial(split_kernel, slots), grid=(steps,), in_...]
    pallas_call x6 -> x8, Pallas kernels: 133 us -> 141 us  [attend(): pl.pallas_call(functools.partial(body, nb), grid=(n_heads,), in_specs=[le...]
    ppermute x25 -> x32, starting transfers between devices: 16.8 us -> 21.8 us  [swap(): return lax.ppermute(a, 'sp', [(d, d ^ bit) for d in range(n_dev)])]
    ppermute x25 -> x32, waiting for transfers between devices: 175 us -> 179 us  [swap(): return lax.ppermute(a, 'sp', [(d, d ^ bit) for d in range(n_dev)])]
  transfers between devices with their start and end apart: 25 -> 32, of which waited for: 7 -> 9; matrix products, arithmetic and copies ran while one was open for 0% -> 0% of each run, Pallas kernels for 35% -> 36%
where the time goes in v3:
time: 477 us; the launch traced here: 475 us
  Pallas kernels  270 us (57%)
  waiting for transfers between devices  179 us (38%)
  starting transfers between devices  21.8 us (5%)
    ppermute x32, waiting for transfers between devices, swap(): return lax.ppermute(a, 'sp', [(d, d ^ bit) for d in range(n_dev)])  179 us
    pallas_call x8, Pallas kernels, attend(): pl.pallas_call(functools.partial(body, nb), grid=(n_heads,), in_specs=[le...  141 us
    pallas_call x3, Pallas kernels, project(): pl.pallas_call(functools.partial(kernel, n_seqs), grid=(n_heads,), in_spe...  79.1 us
    pallas_call x2, Pallas kernels, out_project(): pl.pallas_call(functools.partial(out_kernel, nb), grid=(model_dim // n_co...  29.2 us
    ppermute x32, starting transfers between devices, swap(): return lax.ppermute(a, 'sp', [(d, d ^ bit) for d in range(n_dev)])  21.8 us
    pallas_call x1, Pallas kernels, split_rows(): pl.pallas_call(functools.partial(split_kernel, slots), grid=(steps,), in_...  20.8 us
  transfers between devices with their start and end apart: 32, of which 9 were waited for; matrix products, arithmetic and copies ran while one was open for 0% of the time, Pallas kernels for 36%

profile of v3, /device:TPU:0, one launch (start us, length us, event | category | flops | bytes accessed | tf_op | source)
XLA Modules:
  0.0 475.4 jit_solution(10726788483014283512)
XLA Ops:
  0.0 20.8 %split_rows.1 = (bf16[8,256,2048]{2,1,0:T(8,128)(2,1)}, bf16[8,2048,256]{2,1,0:T(8,128)(2,1)}, bf16[8,2048,256]{2,1,0:T(8,128)(2,1)}) custom-call(bf16[2048,2048]{1,0:T(8,128)(2,1)} %bitcast.6, bf16[16384,256]{1,0:T(8,128)(2,1)} %bitcast.7, bf16[16384,256]{1,0:T(8,128)(2,1)} %bitcast.8), custom_call_target="tpu_custom_call" | custom-call | flops 6442450944 | bytes 50331648 | tf_op jit(solution)/shard_map/split_rows/pallas_call | solution.py:66
  20.8 16.0 %project.3 = (bf16[2,2,8,128,256]{4,3,2,1,0:T(8,128)(2,1)}, bf16[2,1,8,128,256]{4,3,2,1,0:T(8,128)(2,1)}, bf16[2,1,8,128,256]{4,3,2,1,0:T(8,128)(2,1)}) custom-call(bf16[2048,2048]{1,0:T(8,128)(2,1)} %bitcast.9, bf16[8,2048,256]{2,1,0:T(8,128)(2,1)} %get-tuple-element.80.refs_0_.refs_1_, bf16[8,2048,256]{2,1,0:T(8,128)(2,1)} %get-tuple-element.80.refs_0_.refs_1_, ...), custom_call_target="tpu_custom_call" | custom-call | flops 8589934592 | bytes 29360128 | tf_op jit(solution)/shard_map/project/pallas_call | solution.py:192
  36.8 36.8 %project.4 = (bf16[2,1,8,256,256]{4,3,2,1,0:T(8,128)(2,1)}, bf16[2,1,8,256,256]{4,3,2,1,0:T(8,128)(2,1)}, bf16[2,2,8,512,256]{4,3,2,1,0:T(8,128)(2,1)}, bf16[8,2048,256]{2,1,0:T(8,128)(2,1)}) custom-call(bf16[2048,2048]{1,0:T(8,128)(2,1)} %bitcast.10, bf16[8,2048,256]{2,1,0:T(8,128)(2,1)} %get-tuple-element.80.refs_0_.refs_1_, ...), custom_call_target="tpu_custom_call" | custom-call | flops 25769803776 | bytes 37748736 | tf_op jit(solution)/shard_map/project/pallas_call | solution.py:192
  73.6 0.6 collective-permute-start.5
  74.2 2.6 collective-permute-start
  76.7 1.6 collective-permute-start.1
  78.3 0.5 collective-permute-start.4
  78.8 44.3 %collective-permute-done.refs_2_.refs_0_ = bf16[2,2,8,128,256]{4,3,2,1,0:T(8,128)(2,1)S(1)} collective-permute-done((bf16[2,2,8,128,256]{4,3,2,1,0:T(8,128)(2,1)}, bf16[2,2,8,128,256]{4,3,2,1,0:T(8,128)(2,1)S(1)}, u32[]{:S(2)}, u32[]{:S(2)}) %collective-permute-start) | collective-permute-done | bytes 2097184 | tf_op jit(solution)/shard_map/ppermute | solution.py:428
  123.2 0.0 collective-permute-start.3
  123.2 1.5 collective-permute-done.1.refs_4_.refs_0_
  124.6 0.0 collective-permute-start.7
  124.7 26.3 %project.5 = (bf16[1,2,8,1024,256]{4,3,2,1,0:T(8,128)(2,1)}, bf16[1,1,8,128,256]{4,3,2,1,0:T(8,128)(2,1)}, bf16[1,1,8,128,256]{4,3,2,1,0:T(8,128)(2,1)}) custom-call(bf16[2048,2048]{1,0:T(8,128)(2,1)} %bitcast.11, bf16[8,2048,256]{2,1,0:T(8,128)(2,1)} %get-tuple-element.86.refs_0_.refs_1_, bf16[8,2048,256]{2,1,0:T(8,128)(2,1)} %get-tuple-element.86.refs_0_.refs_1_), custom_call_target="tpu_custom_call" | custom-call | flops 19327352832 | bytes 26214400 | tf_op jit(solution)/shard_map/project/pallas_call | solution.py:192
  150.9 0.1 collective-permute-start.6
  151.0 1.7 collective-permute-start.11
  152.7 0.0 collective-permute-done.4.refs_5_
  152.8 0.4 collective-permute-start.12
  153.1 1.7 collective-permute-start.10
  154.8 34.2 %shard_map.55 = (bf16[1,8,512,256]{3,2,1,0:T(8,128)(2,1)}, f32[1,8,256,512]{3,2,1,0:T(8,128)}, f32[1,8,8,512]{3,2,1,0:T(8,128)}) custom-call(bf16[1,2,8,1024,256]{4,3,2,1,0:T(8,128)(2,1)} %get-tuple-element.126.q_ref, bf16[2,2,8,128,256]{4,3,2,1,0:T(8,128)(2,1)} %get-tuple-element.90.refs_0_, bf16[2,2,8,128,256]{4,3,2,1,0:T(8,128)(2,1)} %collective-permute-done.2.refs_1_, ...), custom_call_target="tpu_custom_call" | custom-call | flops 17179869184 | bytes 20971520 | tf_op jit(solution)/shard_map/pallas_call | solution.py:372
  189.1 0.0 collective-permute-done.6.refs_3_
  189.1 2.7 collective-permute-start.8
  191.8 0.0 collective-permute-done.7.refs_5_
  191.8 0.3 collective-permute-start.9
  192.1 34.3 %shard_map.56 = (bf16[1,8,512,256]{3,2,1,0:T(8,128)(2,1)}, f32[1,8,256,512]{3,2,1,0:T(8,128)}, f32[1,8,8,512]{3,2,1,0:T(8,128)}) custom-call(bf16[1,2,8,1024,256]{4,3,2,1,0:T(8,128)(2,1)} %get-tuple-element.126.q_ref, bf16[2,2,8,128,256]{4,3,2,1,0:T(8,128)(2,1)} %get-tuple-element.90.refs_0_, bf16[2,2,8,128,256]{4,3,2,1,0:T(8,128)(2,1)} %collective-permute-done.2.refs_1_, ...), custom_call_target="tpu_custom_call" | custom-call | flops 17179869184 | bytes 20971520 | tf_op jit(solution)/shard_map/pallas_call | solution.py:372
  226.4 0.0 collective-permute-done.11.refs_2_
  226.4 0.1 collective-permute-start.13
  226.5 0.5 collective-permute-start.14
  227.0 0.6 collective-permute-done.8.q_ref
  227.6 9.9 %collective-permute-done.9.q_ref = bf16[1,1,8,128,256]{4,3,2,1,0:T(8,128)(2,1)} collective-permute-done((bf16[1,1,8,128,256]{4,3,2,1,0:T(8,128)(2,1)}, bf16[1,1,8,128,256]{4,3,2,1,0:T(8,128)(2,1)}, u32[]{:S(2)}, u32[]{:S(2)}) %collective-permute-start.9) | collective-permute-done | bytes 524320 | tf_op jit(solution)/shard_map/ppermute | solution.py:428
  237.5 1.5 collective-permute-start.17
  239.1 0.0 collective-permute-done.14.refs_5_.refs_1_
  239.1 1.3 copy-done.3
  240.4 1.4 copy-done.1
  241.8 0.3 collective-permute-done.15.refs_7_.refs_3_
  242.0 10.6 %shard_map.57 = f32[1,8,264,128]{3,2,1,0:T(8,128)} custom-call(bf16[1,1,8,128,256]{4,3,2,1,0:T(8,128)(2,1)} %collective-permute-done.9.q_ref, bf16[2,2,8,128,256]{4,3,2,1,0:T(8,128)(2,1)} %get-tuple-element.90.refs_0_, bf16[2,2,8,128,256]{4,3,2,1,0:T(8,128)(2,1)} %collective-permute-done.2.refs_1_, bf16[2,2,8,128,256]{4,3,2,1,0:T(8,128)(2,1)} %copy-done.2, ...), custom_call_target="tpu_custom_call" | custom-call | flops 1073741824 | bytes 8912896 | tf_op jit(solution)/shard_map/pallas_call | solution.py:372
  252.6 33.3 %collective-permute-done.17.refs_4_ = bf16[2,1,8,256,256]{4,3,2,1,0:T(8,128)(2,1)} collective-permute-done((bf16[2,1,8,256,256]{4,3,2,1,0:T(8,128)(2,1)}, bf16[2,1,8,256,256]{4,3,2,1,0:T(8,128)(2,1)}, u32[]{:S(2)}, u32[]{:S(2)}) %collective-permute-start.17) | collective-permute-done | bytes 2097184 | tf_op jit(solution)/shard_map/ppermute | solution.py:428
  285.9 0.0 collective-permute-done.16.refs_4_
  285.9 0.0 collective-permute-start.19
  285.9 1.5 collective-permute-start.21
  287.4 0.2 collective-permute-start.18
  287.7 4.2 collective-permute-done.18.refs_3_
  291.9 0.0 collective-permute-done.19.refs_5_
  291.9 13.6 %shard_map.58 = (bf16[1,8,256,256]{3,2,1,0:T(8,128)(2,1)}, f32[1,8,256,256]{3,2,1,0:T(8,128)}, f32[1,8,8,256]{3,2,1,0:T(8,128)}) custom-call(bf16[1,2,8,1024,256]{4,3,2,1,0:T(8,128)(2,1)} %get-tuple-element.126.q_ref, bf16[2,2,8,128,256]{4,3,2,1,0:T(8,128)(2,1)} %copy-done.2, bf16[2,2,8,128,256]{4,3,2,1,0:T(8,128)(2,1)} %copy-done.3, ...), custom_call_target="tpu_custom_call" | custom-call | flops 4294967296 | bytes 10485760 | tf_op jit(solution)/shard_map/pallas_call | solution.py:372
  305.5 28.7 %collective-permute-done.21.refs_4_ = bf16[2,1,8,256,256]{4,3,2,1,0:T(8,128)(2,1)S(1)} collective-permute-done((bf16[2,1,8,256,256]{4,3,2,1,0:T(8,128)(2,1)}, bf16[2,1,8,256,256]{4,3,2,1,0:T(8,128)(2,1)S(1)}, u32[]{:S(2)}, u32[]{:S(2)}) %collective-permute-start.21) | collective-permute-done | bytes 2097184 | tf_op jit(solution)/shard_map/ppermute | solution.py:428
  334.2 0.1 collective-permute-start.25
  334.2 0.5 collective-permute-start.24
  334.7 1.5 collective-permute-start.26
  336.3 0.0 collective-permute-start.23
  336.3 10.6 %shard_map.60 = f32[1,8,264,128]{3,2,1,0:T(8,128)} custom-call(bf16[1,1,8,128,256]{4,3,2,1,0:T(8,128)(2,1)} %collective-permute-done.8.q_ref, bf16[2,2,8,128,256]{4,3,2,1,0:T(8,128)(2,1)} %get-tuple-element.90.refs_0_, bf16[2,2,8,128,256]{4,3,2,1,0:T(8,128)(2,1)} %collective-permute-done.2.refs_1_, bf16[2,2,8,128,256]{4,3,2,1,0:T(8,128)(2,1)} %copy-done.2, ...), custom_call_target="tpu_custom_call" | custom-call | flops 1073741824 | bytes 8912896 | tf_op jit(solution)/shard_map/pallas_call | solution.py:372
  346.9 0.1 collective-permute-start.28
  347.0 0.0 collective-permute-done.25.refs_5_
  347.0 13.7 %shard_map.59 = (bf16[1,8,256,256]{3,2,1,0:T(8,128)(2,1)}, f32[1,8,256,256]{3,2,1,0:T(8,128)}, f32[1,8,8,256]{3,2,1,0:T(8,128)}) custom-call(bf16[1,2,8,1024,256]{4,3,2,1,0:T(8,128)(2,1)} %get-tuple-element.126.q_ref, bf16[2,2,8,128,256]{4,3,2,1,0:T(8,128)(2,1)} %copy-done.2, bf16[2,2,8,128,256]{4,3,2,1,0:T(8,128)(2,1)} %copy-done.3, ...), custom_call_target="tpu_custom_call" | custom-call | flops 4294967296 | bytes 10485760 | tf_op jit(solution)/shard_map/pallas_call | solution.py:372
  360.7 0.0 collective-permute-done.26.refs_6_
  360.7 0.6 collective-permute-start.27
  361.3 0.5 collective-permute-start.29
  361.8 2.6 collective-permute-start.31
  364.3 0.0 collective-permute-start.22
  364.3 56.4 %collective-permute-done.28.refs_10_ = f32[1,8,264,128]{3,2,1,0:T(8,128)} collective-permute-done((f32[1,8,264,128]{3,2,1,0:T(8,128)}, f32[1,8,264,128]{3,2,1,0:T(8,128)}, u32[]{:S(2)}, u32[]{:S(2)}) %collective-permute-start.28) | collective-permute-done | bytes 1081376 | tf_op jit(solution)/shard_map/ppermute | solution.py:428
  420.7 12.2 %shard_map.61.o_low = bf16[1,8,256,256]{3,2,1,0:T(8,128)(2,1)} custom-call(bf16[1,2,8,1024,256]{4,3,2,1,0:T(8,128)(2,1)} %get-tuple-element.126.q_ref, bf16[2,2,8,128,256]{4,3,2,1,0:T(8,128)(2,1)} %copy-done, bf16[2,2,8,128,256]{4,3,2,1,0:T(8,128)(2,1)} %copy-done.1, bf16[2,2,8,128,256]{4,3,2,1,0:T(8,128)(2,1)} %collective-permute-done.10.refs_6_.refs_2_, ...), custom_call_target="tpu_custom_call" | custom-call | flops 2147483648 | bytes 9437184 | tf_op jit(solution)/shard_map/pallas_call | solution.py:372
  432.9 0.0 collective-permute-done.29.refs_6_
  432.9 0.1 collective-permute-start.30
  433.0 14.7 %out_project.2.refs_0_ = bf16[2,1024,2048]{2,1,0:T(8,128)(2,1)} custom-call(bf16[1,8,256,256]{3,2,1,0:T(8,128)(2,1)} %shard_map.61.o_low, bf16[1,8,256,256]{3,2,1,0:T(8,128)(2,1)} %get-tuple-element.141.o_mid, bf16[1,8,512,256]{3,2,1,0:T(8,128)(2,1)} %get-tuple-element.142.o_high, bf16[2048,2048]{1,0:T(8,128)(2,1)} %bitcast.13), custom_call_target="tpu_custom_call" | custom-call | flops 8589934592 | bytes 16777216 | tf_op jit(solution)/shard_map/out_project/pallas_call | solution.py:411
  447.8 1.0 copy-done.6
  448.7 12.2 %shard_map.62.o_low = bf16[1,8,256,256]{3,2,1,0:T(8,128)(2,1)} custom-call(bf16[1,2,8,1024,256]{4,3,2,1,0:T(8,128)(2,1)} %get-tuple-element.126.q_ref, bf16[2,2,8,128,256]{4,3,2,1,0:T(8,128)(2,1)} %copy-done, bf16[2,2,8,128,256]{4,3,2,1,0:T(8,128)(2,1)} %copy-done.1, bf16[2,2,8,128,256]{4,3,2,1,0:T(8,128)(2,1)} %collective-permute-done.10.refs_6_.refs_2_, ...), custom_call_target="tpu_custom_call" | custom-call | flops 2147483648 | bytes 9437184 | tf_op jit(solution)/shard_map/pallas_call | solution.py:372
  460.9 14.5 %out_project.3 = bf16[2,1024,2048]{2,1,0:T(8,128)(2,1)} custom-call(bf16[1,8,256,256]{3,2,1,0:T(8,128)(2,1)} %shard_map.62.o_low, bf16[1,8,256,256]{3,2,1,0:T(8,128)(2,1)} %get-tuple-element.139.o_mid, bf16[1,8,512,256]{3,2,1,0:T(8,128)(2,1)} %get-tuple-element.140.o_high, bf16[2048,2048]{1,0:T(8,128)(2,1)} %bitcast.14, ...), custom_call_target="tpu_custom_call", output_to_operand_aliasing={{}: (4, {})} | custom-call | flops 8589934592 | bytes 16777216 | tf_op jit(solution)/shard_map/out_project/pallas_call | solution.py:411
  (36 shorter events, 0.1 us)
Async XLA Ops:
  36.7 86.4 %copy-start.10 = (bf16[2,1,8,128,256]{4,3,2,1,0:T(8,128)(2,1)S(1)}, bf16[2,1,8,128,256]{4,3,2,1,0:T(8,128)(2,1)}, u32[]{:S(2)}) copy-start(bf16[2,1,8,128,256]{4,3,2,1,0:T(8,128)(2,1)} %get-tuple-element.117.refs_2_) | copy-start | bytes 3145732
  73.6 79.5 %collective-permute-start.5 = (bf16[2,2,8,512,256]{4,3,2,1,0:T(8,128)(2,1)}, bf16[2,2,8,512,256]{4,3,2,1,0:T(8,128)(2,1)}, u32[]{:S(2)}, u32[]{:S(2)}) collective-permute-start(bf16[2,2,8,512,256]{4,3,2,1,0:T(8,128)(2,1)} %get-tuple-element.95.refs_6_), channel_id=1, source_target_pairs={{0,1},{1,0},{2,3},{3,2},{4,5},{5,4},{6,7},{7,6},{8,9},{9,8},{10,11... | collective-permute-start | bytes 25165832 | tf_op jit(solution)/shard_map/ppermute | solution.py:428
  74.2 49.0 %collective-permute-start = (bf16[2,2,8,128,256]{4,3,2,1,0:T(8,128)(2,1)}, bf16[2,2,8,128,256]{4,3,2,1,0:T(8,128)(2,1)S(1)}, u32[]{:S(2)}, u32[]{:S(2)}) collective-permute-start(bf16[2,2,8,128,256]{4,3,2,1,0:T(8,128)(2,1)} %get-tuple-element.90.refs_0_), channel_id=1, source_target_pairs={{0,2},{1,3},{2,0},{3,1},{4,6},{5,7},{6,4},{7,5},{8,10},{9,11},{10,... | collective-permute-start | bytes 6291464 | tf_op jit(solution)/shard_map/ppermute | solution.py:428
  76.7 47.9 %collective-permute-start.1 = (bf16[2,2,8,128,256]{4,3,2,1,0:T(8,128)(2,1)}, bf16[2,2,8,128,256]{4,3,2,1,0:T(8,128)(2,1)S(1)}, u32[]{:S(2)}, u32[]{:S(2)}) collective-permute-start(bf16[2,2,8,128,256]{4,3,2,1,0:T(8,128)(2,1)} %get-tuple-element.90.refs_0_), channel_id=1, source_target_pairs={{0,4},{1,5},{2,6},{3,7},{4,0},{5,1},{6,2},{7,3},{8,12},{9,13},{10,... | collective-permute-start | bytes 6291464 | tf_op jit(solution)/shard_map/ppermute | solution.py:428
  78.3 72.7 %collective-permute-start.2 = (bf16[2,2,8,128,256]{4,3,2,1,0:T(8,128)(2,1)}, bf16[2,2,8,128,256]{4,3,2,1,0:T(8,128)(2,1)}, u32[]{:S(2)}, u32[]{:S(2)}) collective-permute-start(bf16[2,2,8,128,256]{4,3,2,1,0:T(8,128)(2,1)} %get-tuple-element.90.refs_0_), channel_id=1, source_target_pairs={{0,1},{1,0},{2,3},{3,2},{4,5},{5,4},{6,7},{7,6},{8,9},{9,8},{10,11... | collective-permute-start | bytes 6291464 | tf_op jit(solution)/shard_map/ppermute | solution.py:428
  78.3 74.4 %collective-permute-start.4 = (bf16[2,1,8,256,256]{4,3,2,1,0:T(8,128)(2,1)}, bf16[2,1,8,256,256]{4,3,2,1,0:T(8,128)(2,1)}, u32[]{:S(2)}, u32[]{:S(2)}) collective-permute-start(bf16[2,1,8,256,256]{4,3,2,1,0:T(8,128)(2,1)} %get-tuple-element.94.refs_4_), channel_id=1, source_target_pairs={{0,1},{1,0},{2,3},{3,2},{4,5},{5,4},{6,7},{7,6},{8,9},{9,8},{10,11... | collective-permute-start | bytes 6291464 | tf_op jit(solution)/shard_map/ppermute | solution.py:428
  123.2 1.5 copy-start.2
  123.2 27.8 %collective-permute-start.3 = (bf16[2,1,8,128,256]{4,3,2,1,0:T(8,128)(2,1)S(1)}, bf16[2,1,8,128,256]{4,3,2,1,0:T(8,128)(2,1)}, u32[]{:S(2)}, u32[]{:S(2)}) collective-permute-start(bf16[2,1,8,128,256]{4,3,2,1,0:T(8,128)(2,1)S(1)} %copy-done.10), channel_id=1, source_target_pairs={{0,1},{1,0},{2,3},{3,2},{4,5},{5,4},{6,7},{7,6},{8,9},{9,8},{10,11... | collective-permute-start | bytes 3145736 | tf_op jit(solution)/shard_map/ppermute | solution.py:428
  124.6 101.9 %copy-start = (bf16[2,2,8,128,256]{4,3,2,1,0:T(8,128)(2,1)}, bf16[2,2,8,128,256]{4,3,2,1,0:T(8,128)(2,1)S(1)}, u32[]{:S(2)}) copy-start(bf16[2,2,8,128,256]{4,3,2,1,0:T(8,128)(2,1)S(1)} %collective-permute-done.1.refs_4_.refs_0_) | copy-start | bytes 6291460
  124.6 67.1 %collective-permute-start.7 = (bf16[2,1,8,256,256]{4,3,2,1,0:T(8,128)(2,1)}, bf16[2,1,8,256,256]{4,3,2,1,0:T(8,128)(2,1)}, u32[]{:S(2)}, u32[]{:S(2)}) collective-permute-start(bf16[2,1,8,256,256]{4,3,2,1,0:T(8,128)(2,1)} %get-tuple-element.103.refs_4_), channel_id=1, source_target_pairs={{0,1},{1,0},{2,3},{3,2},{4,5},{5,4},{6,7},{7,6},{8,9},{9,8},{10,11... | collective-permute-start | bytes 6291464 | tf_op jit(solution)/shard_map/ppermute | solution.py:428
  150.9 38.1 %collective-permute-start.6 = (bf16[2,1,8,128,256]{4,3,2,1,0:T(8,128)(2,1)}, bf16[2,1,8,128,256]{4,3,2,1,0:T(8,128)(2,1)}, u32[]{:S(2)}, u32[]{:S(2)}) collective-permute-start(bf16[2,1,8,128,256]{4,3,2,1,0:T(8,128)(2,1)} %get-tuple-element.125.refs_2_), channel_id=1, source_target_pairs={{0,1},{1,0},{2,3},{3,2},{4,5},{5,4},{6,7},{7,6},{8,9},{9,8},{10,11... | collective-permute-start | bytes 3145736 | tf_op jit(solution)/shard_map/ppermute | solution.py:428
  151.0 75.4 %collective-permute-start.11 = (bf16[2,1,8,128,256]{4,3,2,1,0:T(8,128)(2,1)}, bf16[2,1,8,128,256]{4,3,2,1,0:T(8,128)(2,1)S(1)}, u32[]{:S(2)}, u32[]{:S(2)}) collective-permute-start(bf16[2,1,8,128,256]{4,3,2,1,0:T(8,128)(2,1)} %get-tuple-element.117.refs_2_), channel_id=1, source_target_pairs={{0,2},{1,3},{2,0},{3,1},{4,6},{5,7},{6,4},{7,5},{8,10},{9,11},{10,... | collective-permute-start | bytes 3145736 | tf_op jit(solution)/shard_map/ppermute | solution.py:428
  152.8 73.8 %collective-permute-start.12 = (bf16[2,1,8,128,256]{4,3,2,1,0:T(8,128)(2,1)}, bf16[2,1,8,128,256]{4,3,2,1,0:T(8,128)(2,1)}, u32[]{:S(2)}, u32[]{:S(2)}) collective-permute-start(bf16[2,1,8,128,256]{4,3,2,1,0:T(8,128)(2,1)} %get-tuple-element.125.refs_2_), channel_id=1, source_target_pairs={{0,2},{1,3},{2,0},{3,1},{4,6},{5,7},{6,4},{7,5},{8,10},{9,11},{10,... | collective-permute-start | bytes 3145736 | tf_op jit(solution)/shard_map/ppermute | solution.py:428
  153.1 84.4 %collective-permute-start.10 = (bf16[2,2,8,128,256]{4,3,2,1,0:T(8,128)(2,1)}, bf16[2,2,8,128,256]{4,3,2,1,0:T(8,128)(2,1)}, u32[]{:S(2)}, u32[]{:S(2)}) collective-permute-start(bf16[2,2,8,128,256]{4,3,2,1,0:T(8,128)(2,1)} %copy-done.2), channel_id=1, source_target_pairs={{0,4},{1,5},{2,6},{3,7},{4,0},{5,1},{6,2},{7,3},{8,12},{9,13},{10,... | collective-permute-start | bytes 6291464 | tf_op jit(solution)/shard_map/ppermute | solution.py:428
  189.1 38.5 %collective-permute-start.8 = (bf16[1,1,8,128,256]{4,3,2,1,0:T(8,128)(2,1)}, bf16[1,1,8,128,256]{4,3,2,1,0:T(8,128)(2,1)}, u32[]{:S(2)}, u32[]{:S(2)}) collective-permute-start(bf16[1,1,8,128,256]{4,3,2,1,0:T(8,128)(2,1)} %get-tuple-element.111), channel_id=1, source_target_pairs={{0,8},{1,9},{2,10},{3,11},{4,12},{5,13},{6,14},{7,15},{8,0},{9,1},... | collective-permute-start | bytes 1572872 | tf_op jit(solution)/shard_map/ppermute | solution.py:428
  191.8 45.8 %collective-permute-start.9 = (bf16[1,1,8,128,256]{4,3,2,1,0:T(8,128)(2,1)}, bf16[1,1,8,128,256]{4,3,2,1,0:T(8,128)(2,1)}, u32[]{:S(2)}, u32[]{:S(2)}) collective-permute-start(bf16[1,1,8,128,256]{4,3,2,1,0:T(8,128)(2,1)} %get-tuple-element.112), channel_id=1, source_target_pairs={{0,8},{1,9},{2,10},{3,11},{4,12},{5,13},{6,14},{7,15},{8,0},{9,1},... | collective-permute-start | bytes 1572872 | tf_op jit(solution)/shard_map/ppermute | solution.py:428
  226.4 26.2 %copy-start.9 = (bf16[2,1,8,128,256]{4,3,2,1,0:T(8,128)(2,1)}, bf16[2,1,8,128,256]{4,3,2,1,0:T(8,128)(2,1)S(1)}, u32[]{:S(2)}) copy-start(bf16[2,1,8,128,256]{4,3,2,1,0:T(8,128)(2,1)S(1)} %collective-permute-done.11.refs_2_) | copy-start | bytes 3145732
  226.4 12.6 %collective-permute-start.13 = (bf16[2,2,8,128,256]{4,3,2,1,0:T(8,128)(2,1)}, bf16[2,2,8,128,256]{4,3,2,1,0:T(8,128)(2,1)S(1)}, u32[]{:S(2)}, u32[]{:S(2)}) collective-permute-start(bf16[2,2,8,128,256]{4,3,2,1,0:T(8,128)(2,1)} %copy-done.2), channel_id=1, source_target_pairs={{0,1},{1,0},{2,3},{3,2},{4,5},{5,4},{6,7},{7,6},{8,9},{9,8},{10,11... | collective-permute-start | bytes 6291464 | tf_op jit(solution)/shard_map/ppermute | solution.py:428
  226.5 12.5 %collective-permute-start.14 = (bf16[2,2,8,128,256]{4,3,2,1,0:T(8,128)(2,1)S(1)}, bf16[2,2,8,128,256]{4,3,2,1,0:T(8,128)(2,1)S(1)}, u32[]{:S(2)}, u32[]{:S(2)}) collective-permute-start(bf16[2,2,8,128,256]{4,3,2,1,0:T(8,128)(2,1)S(1)} %collective-permute-done.1.refs_4_.refs_0_), channel_id=1, source_target_pairs={{0,1},{1,0},{2,3},{3,2},{4,5},{5,4},{6,7},{7,6},{8,9},{9,8},{10,11... | collective-permute-start | bytes 6291464 | tf_op jit(solution)/shard_map/ppermute | solution.py:428
  237.5 4.5 collective-permute-start.15
  237.5 48.4 %collective-permute-start.17 = (bf16[2,1,8,256,256]{4,3,2,1,0:T(8,128)(2,1)}, bf16[2,1,8,256,256]{4,3,2,1,0:T(8,128)(2,1)}, u32[]{:S(2)}, u32[]{:S(2)}) collective-permute-start(bf16[2,1,8,256,256]{4,3,2,1,0:T(8,128)(2,1)} %get-tuple-element.94.refs_4_), channel_id=1, source_target_pairs={{0,2},{1,3},{2,0},{3,1},{4,6},{5,7},{6,4},{7,5},{8,10},{9,11},{10,... | collective-permute-start | bytes 6291464 | tf_op jit(solution)/shard_map/ppermute | solution.py:428
  239.1 46.8 %collective-permute-start.16 = (bf16[2,1,8,128,256]{4,3,2,1,0:T(8,128)(2,1)}, bf16[2,1,8,128,256]{4,3,2,1,0:T(8,128)(2,1)}, u32[]{:S(2)}, u32[]{:S(2)}) collective-permute-start(bf16[2,1,8,128,256]{4,3,2,1,0:T(8,128)(2,1)} %get-tuple-element.117.refs_2_), channel_id=1, source_target_pairs={{0,4},{1,5},{2,6},{3,7},{4,0},{5,1},{6,2},{7,3},{8,12},{9,13},{10,... | collective-permute-start | bytes 3145736 | tf_op jit(solution)/shard_map/ppermute | solution.py:428
  239.1 1.3 copy-start.3
  240.4 1.4 copy-start.1
  285.9 6.0 %collective-permute-start.19 = (bf16[2,1,8,256,256]{4,3,2,1,0:T(8,128)(2,1)}, bf16[2,1,8,256,256]{4,3,2,1,0:T(8,128)(2,1)}, u32[]{:S(2)}, u32[]{:S(2)}) collective-permute-start(bf16[2,1,8,256,256]{4,3,2,1,0:T(8,128)(2,1)} %collective-permute-done.17.refs_4_), channel_id=1, source_target_pairs={{0,1},{1,0},{2,3},{3,2},{4,5},{5,4},{6,7},{7,6},{8,9},{9,8},{10,11... | collective-permute-start | bytes 6291464 | tf_op jit(solution)/shard_map/ppermute | solution.py:428
  285.9 48.3 %collective-permute-start.21 = (bf16[2,1,8,256,256]{4,3,2,1,0:T(8,128)(2,1)}, bf16[2,1,8,256,256]{4,3,2,1,0:T(8,128)(2,1)S(1)}, u32[]{:S(2)}, u32[]{:S(2)}) collective-permute-start(bf16[2,1,8,256,256]{4,3,2,1,0:T(8,128)(2,1)} %get-tuple-element.103.refs_4_), channel_id=1, source_target_pairs={{0,2},{1,3},{2,0},{3,1},{4,6},{5,7},{6,4},{7,5},{8,10},{9,11},{10,... | collective-permute-start | bytes 6291464 | tf_op jit(solution)/shard_map/ppermute | solution.py:428
  287.4 4.5 collective-permute-start.18
  287.7 46.5 %collective-permute-start.20 = (bf16[2,1,8,128,256]{4,3,2,1,0:T(8,128)(2,1)}, bf16[2,1,8,128,256]{4,3,2,1,0:T(8,128)(2,1)S(1)}, u32[]{:S(2)}, u32[]{:S(2)}) collective-permute-start(bf16[2,1,8,128,256]{4,3,2,1,0:T(8,128)(2,1)} %get-tuple-element.125.refs_2_), channel_id=1, source_target_pairs={{0,4},{1,5},{2,6},{3,7},{4,0},{5,1},{6,2},{7,3},{8,12},{9,13},{10,... | collective-permute-start | bytes 3145736 | tf_op jit(solution)/shard_map/ppermute | solution.py:428
  334.2 12.7 %copy-start.4 = (bf16[2,1,8,256,256]{4,3,2,1,0:T(8,128)(2,1)}, bf16[2,1,8,256,256]{4,3,2,1,0:T(8,128)(2,1)S(1)}, u32[]{:S(2)}) copy-start(bf16[2,1,8,256,256]{4,3,2,1,0:T(8,128)(2,1)S(1)} %collective-permute-done.21.refs_4_) | copy-start | bytes 6291460
  334.2 2.1 copy-start.7
  334.2 12.8 %collective-permute-start.25 = (bf16[2,1,8,256,256]{4,3,2,1,0:T(8,128)(2,1)S(1)}, bf16[2,1,8,256,256]{4,3,2,1,0:T(8,128)(2,1)}, u32[]{:S(2)}, u32[]{:S(2)}) collective-permute-start(bf16[2,1,8,256,256]{4,3,2,1,0:T(8,128)(2,1)S(1)} %collective-permute-done.21.refs_4_), channel_id=1, source_target_pairs={{0,1},{1,0},{2,3},{3,2},{4,5},{5,4},{6,7},{7,6},{8,9},{9,8},{10,11... | collective-permute-start | bytes 6291464 | tf_op jit(solution)/shard_map/ppermute | solution.py:428
  334.2 12.7 %collective-permute-start.24 = (bf16[2,1,8,128,256]{4,3,2,1,0:T(8,128)(2,1)}, bf16[2,1,8,128,256]{4,3,2,1,0:T(8,128)(2,1)}, u32[]{:S(2)}, u32[]{:S(2)}) collective-permute-start(bf16[2,1,8,128,256]{4,3,2,1,0:T(8,128)(2,1)} %collective-permute-done.12.refs_2_), channel_id=1, source_target_pairs={{0,1},{1,0},{2,3},{3,2},{4,5},{5,4},{6,7},{7,6},{8,9},{9,8},{10,11... | collective-permute-start | bytes 3145736 | tf_op jit(solution)/shard_map/ppermute | solution.py:428
  334.7 25.9 %collective-permute-start.26 = (bf16[2,1,8,128,256]{4,3,2,1,0:T(8,128)(2,1)}, bf16[2,1,8,128,256]{4,3,2,1,0:T(8,128)(2,1)}, u32[]{:S(2)}, u32[]{:S(2)}) collective-permute-start(bf16[2,1,8,128,256]{4,3,2,1,0:T(8,128)(2,1)} %collective-permute-done.16.refs_4_), channel_id=1, source_target_pairs={{0,2},{1,3},{2,0},{3,1},{4,6},{5,7},{6,4},{7,5},{8,10},{9,11},{10,... | collective-permute-start | bytes 3145736 | tf_op jit(solution)/shard_map/ppermute | solution.py:428
  336.3 28.1 %collective-permute-start.23 = (bf16[2,1,8,128,256]{4,3,2,1,0:T(8,128)(2,1)}, bf16[2,1,8,128,256]{4,3,2,1,0:T(8,128)(2,1)}, u32[]{:S(2)}, u32[]{:S(2)}) collective-permute-start(bf16[2,1,8,128,256]{4,3,2,1,0:T(8,128)(2,1)} %collective-permute-done.16.refs_4_), channel_id=1, source_target_pairs={{0,1},{1,0},{2,3},{3,2},{4,5},{5,4},{6,7},{7,6},{8,9},{9,8},{10,11... | collective-permute-start | bytes 3145736 | tf_op jit(solution)/shard_map/ppermute | solution.py:428
  346.9 14.9 %copy-start.5 = (f32[1,8,264,128]{3,2,1,0:T(8,128)S(1)}, f32[1,8,264,128]{3,2,1,0:T(8,128)}, u32[]{:S(2)}) copy-start(f32[1,8,264,128]{3,2,1,0:T(8,128)} %shard_map.57) | copy-start | bytes 3244036
  346.9 73.9 %collective-permute-start.28 = (f32[1,8,264,128]{3,2,1,0:T(8,128)}, f32[1,8,264,128]{3,2,1,0:T(8,128)}, u32[]{:S(2)}, u32[]{:S(2)}) collective-permute-start(f32[1,8,264,128]{3,2,1,0:T(8,128)} %shard_map.60), channel_id=1, source_target_pairs={{0,8},{1,9},{2,10},{3,11},{4,12},{5,13},{6,14},{7,15},{8,0},{9,1},... | collective-permute-start | bytes 3244040 | tf_op jit(solution)/shard_map/ppermute | solution.py:428
  347.0 14.3 %copy-start.8 = (bf16[2,1,8,128,256]{4,3,2,1,0:T(8,128)(2,1)S(1)}, bf16[2,1,8,128,256]{4,3,2,1,0:T(8,128)(2,1)}, u32[]{:S(2)}) copy-start(bf16[2,1,8,128,256]{4,3,2,1,0:T(8,128)(2,1)} %copy-done.7) | copy-start | bytes 3145732
  360.7 60.1 %collective-permute-start.27 = (bf16[2,1,8,128,256]{4,3,2,1,0:T(8,128)(2,1)}, bf16[2,1,8,128,256]{4,3,2,1,0:T(8,128)(2,1)}, u32[]{:S(2)}, u32[]{:S(2)}) collective-permute-start(bf16[2,1,8,128,256]{4,3,2,1,0:T(8,128)(2,1)} %collective-permute-done.26.refs_6_), channel_id=1, source_target_pairs={{0,1},{1,0},{2,3},{3,2},{4,5},{5,4},{6,7},{7,6},{8,9},{9,8},{10,11... | collective-permute-start | bytes 3145736 | tf_op jit(solution)/shard_map/ppermute | solution.py:428
  361.3 71.6 %collective-permute-start.29 = (bf16[2,1,8,128,256]{4,3,2,1,0:T(8,128)(2,1)S(1)}, bf16[2,1,8,128,256]{4,3,2,1,0:T(8,128)(2,1)}, u32[]{:S(2)}, u32[]{:S(2)}) collective-permute-start(bf16[2,1,8,128,256]{4,3,2,1,0:T(8,128)(2,1)S(1)} %copy-done.8), channel_id=1, source_target_pairs={{0,2},{1,3},{2,0},{3,1},{4,6},{5,7},{6,4},{7,5},{8,10},{9,11},{10,... | collective-permute-start | bytes 3145736 | tf_op jit(solution)/shard_map/ppermute | solution.py:428
  361.8 86.0 %collective-permute-start.31 = (f32[1,8,264,128]{3,2,1,0:T(8,128)S(1)}, f32[1,8,264,128]{3,2,1,0:T(8,128)S(1)}, u32[]{:S(2)}, u32[]{:S(2)}) collective-permute-start(f32[1,8,264,128]{3,2,1,0:T(8,128)S(1)} %copy-done.5), channel_id=1, source_target_pairs={{0,8},{1,9},{2,10},{3,11},{4,12},{5,13},{6,14},{7,15},{8,0},{9,1},... | collective-permute-start | bytes 3244040 | tf_op jit(solution)/shard_map/ppermute | solution.py:428
  364.3 83.4 %collective-permute-start.22 = (bf16[2,1,8,128,256]{4,3,2,1,0:T(8,128)(2,1)S(1)}, bf16[2,1,8,128,256]{4,3,2,1,0:T(8,128)(2,1)}, u32[]{:S(2)}, u32[]{:S(2)}) collective-permute-start(bf16[2,1,8,128,256]{4,3,2,1,0:T(8,128)(2,1)S(1)} %copy-done.8), channel_id=1, source_target_pairs={{0,1},{1,0},{2,3},{3,2},{4,5},{5,4},{6,7},{7,6},{8,9},{9,8},{10,11... | collective-permute-start | bytes 3145736 | tf_op jit(solution)/shard_map/ppermute | solution.py:428
  432.9 14.8 %collective-permute-start.30 = (bf16[2,1,8,128,256]{4,3,2,1,0:T(8,128)(2,1)}, bf16[2,1,8,128,256]{4,3,2,1,0:T(8,128)(2,1)}, u32[]{:S(2)}, u32[]{:S(2)}) collective-permute-start(bf16[2,1,8,128,256]{4,3,2,1,0:T(8,128)(2,1)} %collective-permute-done.29.refs_6_), channel_id=1, source_target_pairs={{0,1},{1,0},{2,3},{3,2},{4,5},{5,4},{6,7},{7,6},{8,9},{9,8},{10,11... | collective-permute-start | bytes 3145736 | tf_op jit(solution)/shard_map/ppermute | solution.py:428
  447.7 1.0 copy-start.6
